TPU v7x, 32 devices: a whole 2x2x4 slice. The times are simulated.
32 devices in a mesh: dp: 8 (over y, x, core), tensor: 4 (over z).
Axes of the slice: x: 2, y: 2, z: 4, core: 2. Of those that a mesh axis runs over, the one named last changes fastest.
Arguments:
- tokens: bfloat16 [4096, 1024], P(('dp', 'tensor')), may hold values from -5 to 5
- lengths: int32 [8, 2], P('dp'), may hold values from 0 to 512, as said below
- w_query: bfloat16 [1024, 1024], P('dp', 'tensor'), may hold values from -0.1875 to 0.1875
- b_query: float32 [1024], replicated, may hold values from -3 to 3
- w_key: bfloat16 [1024, 1024], P('dp', 'tensor'), may hold values from -0.1875 to 0.1875
- w_value: bfloat16 [1024, 1024], P('dp', 'tensor'), may hold values from -0.1875 to 0.1875
- b_value: float32 [1024], replicated, may hold values from -3 to 3
- w_out: bfloat16 [1024, 1024], P('tensor', 'dp'), may hold values from -3 to 3
- b_out: float32 [1024], replicated, may hold values from -3 to 3
- gain_attn: float32 [1024], replicated, may hold values from 0.1 to 1.9
- shift_attn: float32 [1024], replicated, may hold values from -3 to 3
- w_in: bfloat16 [1024, 4096], P('dp', 'tensor'), may hold values from -0.1875 to 0.1875
- b_in: float32 [4096], replicated, may hold values from -3 to 3
- w_back: bfloat16 [4096, 1024], P('tensor', 'dp'), may hold values from -0.09375 to 0.09375
- b_back: float32 [1024], replicated, may hold values from -3 to 3
- gain_ffn: float32 [1024], replicated, may hold values from 0.1 to 1.9
- shift_ffn: float32 [1024], replicated, may hold values from -3 to 3
- cotangent: bfloat16 [4096, 1024], P(('dp', 'tensor')), may hold values from -6 to 6
Outputs:
- output: bfloat16 [4096, 1024], P(('dp', 'tensor'))
- grad_tokens: float32 [4096, 1024], P(('dp', 'tensor'))
- grad_w_query: float32 [1024, 1024], P('dp', 'tensor')
- grad_b_query: float32 [1024], replicated
- grad_w_key: float32 [1024, 1024], P('dp', 'tensor')
- grad_w_value: float32 [1024, 1024], P('dp', 'tensor')
- grad_b_value: float32 [1024], replicated
- grad_w_out: float32 [1024, 1024], P('tensor', 'dp')
- grad_b_out: float32 [1024], replicated
- grad_gain_attn: float32 [1024], replicated
- grad_shift_attn: float32 [1024], replicated
- grad_w_in: float32 [1024, 4096], P('dp', 'tensor')
- grad_b_in: float32 [4096], replicated
- grad_w_back: float32 [4096, 1024], P('tensor', 'dp')
- grad_b_back: float32 [1024], replicated
- grad_gain_ffn: float32 [1024], replicated
- grad_shift_ffn: float32 [1024], replicated
Inputs may be any that keep to these rules, and one draw needn't show every extreme that they name: Each group's 2 lengths sum to at most 512; the first is 1 or more, the second may be 0; in every draw one group holds a single sequence of exactly 512 tokens.
All inputs are finite; a program needn't handle non-finite values.
Results may differ from a plain program's by a relative error of at most 0.02.
Values may be sent and summed in bfloat16 or wider, within the bound.
A program may use at most 128 MiB of HBM per device.

v0:
```python
import jax
import jax.numpy as jnp
from jax import lax
from jax.sharding import PartitionSpec as P

HD = 64


epsilon = 1e-06
masked_value = -1e30


def matmul_plain(left_side, right_side):
    return jnp.dot(left_side, right_side, preferred_element_type=jnp.float32)


def matmul_over_rows(left_side, right_side):
    return lax.dot_general(
        left_side, right_side, (((0,), (0,)), ((), ())), preferred_element_type=jnp.float32
    )


def matmul_over_cols(left_side, right_side):
    return lax.dot_general(
        left_side, right_side, (((1,), (1,)), ((), ())), preferred_element_type=jnp.float32
    )


def layer_norm(residual, gain_vec, shift_vec):
    mean_val = jnp.mean(residual, axis=-1, keepdims=True)
    centered = residual - mean_val
    inv_std = lax.rsqrt(jnp.mean(centered * centered, axis=-1, keepdims=True) + epsilon)
    normed = centered * inv_std
    return (normed * gain_vec + shift_vec, normed, inv_std)


def norm_back(grad_out, normed, inv_std, gain_vec):
    grad_norm = grad_out * gain_vec
    first_mean = jnp.mean(grad_norm, axis=-1, keepdims=True)
    second_mean = jnp.mean(grad_norm * normed, axis=-1, keepdims=True)
    return inv_std * (grad_norm - first_mean - normed * second_mean)


def gelu_parts(preact):
    cdf_val = 0.5 * (1.0 + lax.erf(preact * 0.7071067811865476))
    pdf_val = jnp.exp(-0.5 * preact * preact) * 0.3989422804014327
    return (preact * cdf_val, cdf_val + preact * pdf_val)


def attend_forward(query_rows, key_rows, value_rows, seg_ids, head_dim, block_rows):
    group_rows, head_cols = query_rows.shape
    pair_width = 2 * head_dim
    block_count = group_rows // block_rows
    pair_count = head_cols // pair_width
    score_scale = head_dim ** (-0.5)

    def attend_step(step_index, loop_carry):
        context, log_total = loop_carry
        pair_index = step_index // block_count
        row_start = step_index % block_count * block_rows
        first_col = pair_index * pair_width
        query_block = lax.dynamic_slice(
            query_rows, (row_start, first_col), (block_rows, pair_width)
        ).reshape(block_rows, 2, head_dim)
        key_pair = lax.dynamic_slice(key_rows, (0, first_col), (group_rows, pair_width)).reshape(
            group_rows, 2, head_dim
        )
        value_pair = lax.dynamic_slice(
            value_rows, (0, first_col), (group_rows, pair_width)
        ).reshape(group_rows, 2, head_dim)
        same_seg = seg_ids[:, None] == seg_ids[None, :]
        scores = (
            jnp.einsum("qhd,khd->hqk", query_block, key_pair, preferred_element_type=jnp.float32)
            * score_scale
        )
        scores = jnp.where(same_seg[None], scores, masked_value)
        row_max = jnp.max(scores, axis=-1, keepdims=True)
        block_total = row_max + jnp.log(jnp.sum(jnp.exp(scores - row_max), axis=-1, keepdims=True))
        prob_bf = jnp.exp(scores - block_total).astype(jnp.bfloat16)
        context_block = jnp.einsum(
            "hqk,khd->qhd", prob_bf, value_pair, preferred_element_type=jnp.float32
        ).astype(jnp.bfloat16)
        context = lax.dynamic_update_slice(
            context, context_block.reshape(block_rows, pair_width), (row_start, first_col)
        )
        log_total = lax.dynamic_update_slice(
            log_total, block_total[:, :, 0], (2 * pair_index, row_start)
        )
        return (context, log_total)

    start_carry = (
        jnp.zeros((group_rows, head_cols), jnp.bfloat16),
        jnp.zeros((head_cols // head_dim, group_rows), jnp.float32),
    )
    return lax.fori_loop(0, pair_count * block_count, attend_step, start_carry)


def attend_backward(
    query_rows,
    key_rows,
    value_rows,
    context,
    grad_context,
    log_total,
    seg_ids,
    head_dim,
    block_rows,
):
    group_rows, head_cols = query_rows.shape
    pair_width = 2 * head_dim
    block_count = group_rows // block_rows
    pair_count = head_cols // pair_width
    score_scale = head_dim ** (-0.5)

    def back_step(step_index, loop_carry):
        grad_query, grad_keys, grad_values = loop_carry
        pair_index = step_index // block_count
        row_start = step_index % block_count * block_rows
        first_col = pair_index * pair_width
        query_block = lax.dynamic_slice(
            query_rows, (row_start, first_col), (block_rows, pair_width)
        ).reshape(block_rows, 2, head_dim)
        key_pair = lax.dynamic_slice(key_rows, (0, first_col), (group_rows, pair_width)).reshape(
            group_rows, 2, head_dim
        )
        value_pair = lax.dynamic_slice(
            value_rows, (0, first_col), (group_rows, pair_width)
        ).reshape(group_rows, 2, head_dim)
        context_block = lax.dynamic_slice(
            context, (row_start, first_col), (block_rows, pair_width)
        ).reshape(block_rows, 2, head_dim)
        gctx_block = lax.dynamic_slice(
            grad_context, (row_start, first_col), (block_rows, pair_width)
        ).reshape(block_rows, 2, head_dim)
        total_block = lax.dynamic_slice(log_total, (2 * pair_index, row_start), (2, block_rows))
        same_seg = seg_ids[:, None] == seg_ids[None, :]
        scores = (
            jnp.einsum("qhd,khd->hqk", query_block, key_pair, preferred_element_type=jnp.float32)
            * score_scale
        )
        scores = jnp.where(same_seg[None], scores, masked_value)
        probs = jnp.exp(scores - total_block[:, :, None])
        prob_bf = probs.astype(jnp.bfloat16)
        grad_probs = jnp.einsum(
            "qhd,khd->hqk", gctx_block, value_pair, preferred_element_type=jnp.float32
        )
        delta_rows = jnp.sum(
            gctx_block.astype(jnp.float32) * context_block.astype(jnp.float32), axis=-1
        ).T[:, :, None]
        grad_scores = (probs * (grad_probs - delta_rows) * score_scale).astype(jnp.bfloat16)
        grad_q_block = jnp.einsum(
            "hqk,khd->qhd", grad_scores, key_pair, preferred_element_type=jnp.float32
        ).reshape(block_rows, pair_width)
        grad_k_pair = jnp.einsum(
            "hqk,qhd->khd", grad_scores, query_block, preferred_element_type=jnp.float32
        ).reshape(group_rows, pair_width)
        grad_v_pair = jnp.einsum(
            "hqk,qhd->khd", prob_bf, gctx_block, preferred_element_type=jnp.float32
        ).reshape(group_rows, pair_width)
        grad_query = lax.dynamic_update_slice(grad_query, grad_q_block, (row_start, first_col))
        old_keys = lax.dynamic_slice(grad_keys, (0, first_col), (group_rows, pair_width))
        grad_keys = lax.dynamic_update_slice(grad_keys, old_keys + grad_k_pair, (0, first_col))
        old_values = lax.dynamic_slice(grad_values, (0, first_col), (group_rows, pair_width))
        grad_values = lax.dynamic_update_slice(
            grad_values, old_values + grad_v_pair, (0, first_col)
        )
        return (grad_query, grad_keys, grad_values)

    zero_grad = jnp.zeros((group_rows, head_cols), jnp.float32)
    return lax.fori_loop(0, pair_count * block_count, back_step, (zero_grad, zero_grad, zero_grad))


def on_device(
    tokens,
    lengths,
    w_query,
    b_query,
    w_key,
    w_value,
    b_value,
    w_out,
    b_out,
    gain_attn,
    shift_attn,
    w_in,
    b_in,
    w_back,
    b_back,
    gain_ffn,
    shift_ffn,
    cotangent,
):
    tensor_size = lax.axis_size("tensor")
    tensor_index = lax.axis_index("tensor")
    local_rows = tokens.shape[0]
    group_rows = local_rows * tensor_size
    head_cols = w_query.shape[1]
    hidden_cols = w_in.shape[1]
    block_rows = min(512, group_rows)
    seq_lens = lengths[0]
    live_end = seq_lens[0] + seq_lens[1]
    positions = jnp.arange(group_rows, dtype=jnp.int32)
    seg_ids = (positions >= seq_lens[0]).astype(jnp.int32) + (positions >= live_end).astype(
        jnp.int32
    )
    local_pos = tensor_index * local_rows + jnp.arange(local_rows, dtype=jnp.int32)
    live_rows = (local_pos < live_end).astype(jnp.float32)[:, None]
    rows_full = lax.all_gather(tokens, "tensor", axis=0, tiled=True)
    attn_mats = (
        lax.all_gather(w_query, "dp", axis=0, tiled=True),
        lax.all_gather(w_key, "dp", axis=0, tiled=True),
        lax.all_gather(w_value, "dp", axis=0, tiled=True),
        lax.all_gather(w_out, "dp", axis=1, tiled=True),
    )
    mat_query, mat_key, mat_value, mat_out = attn_mats
    bias_query = lax.dynamic_slice_in_dim(b_query, tensor_index * head_cols, head_cols)
    bias_value = lax.dynamic_slice_in_dim(b_value, tensor_index * head_cols, head_cols)
    bias_in = lax.dynamic_slice_in_dim(b_in, tensor_index * hidden_cols, hidden_cols)
    query_rows = (matmul_plain(rows_full, mat_query) + bias_query).astype(jnp.bfloat16)
    key_rows = matmul_plain(rows_full, mat_key).astype(jnp.bfloat16)
    value_rows = (matmul_plain(rows_full, mat_value) + bias_value).astype(jnp.bfloat16)
    context, log_total = attend_forward(query_rows, key_rows, value_rows, seg_ids, HD, block_rows)
    attn_sum = lax.psum_scatter(
        matmul_plain(context, mat_out).astype(jnp.bfloat16),
        "tensor",
        scatter_dimension=0,
        tiled=True,
    ).astype(jnp.float32)
    resid_one = tokens.astype(jnp.float32) + attn_sum + b_out
    hidden_one, normed_one, inv_one = layer_norm(resid_one, gain_attn, shift_attn)
    hidden_bf = hidden_one.astype(jnp.bfloat16)
    hidden_full = lax.all_gather(hidden_bf, "tensor", axis=0, tiled=True)
    ffn_mats = (
        lax.all_gather(w_in, "dp", axis=0, tiled=True),
        lax.all_gather(w_back, "dp", axis=1, tiled=True),
    )
    mat_in, mat_back = ffn_mats
    preact = matmul_plain(hidden_full, mat_in) + bias_in
    activ_val, gelu_slope = gelu_parts(preact)
    activation = activ_val.astype(jnp.bfloat16)
    ffn_sum = lax.psum_scatter(
        matmul_plain(activation, mat_back).astype(jnp.bfloat16),
        "tensor",
        scatter_dimension=0,
        tiled=True,
    ).astype(jnp.float32)
    resid_two = hidden_one + ffn_sum + b_back
    normed_out, normed_two, inv_two = layer_norm(resid_two, gain_ffn, shift_ffn)
    output = (normed_out * live_rows).astype(jnp.bfloat16)
    grad_final = cotangent.astype(jnp.float32) * live_rows
    grad_gain_ffn = jnp.sum(grad_final * normed_two, axis=0)
    grad_shift_ffn = jnp.sum(grad_final, axis=0)
    grad_two = norm_back(grad_final, normed_two, inv_two, gain_ffn)
    grad_b_back = jnp.sum(grad_two, axis=0)
    mat_query, mat_key, mat_value, mat_out, mat_in, mat_back = (
        lax.all_gather(w_query, "dp", axis=0, tiled=True),
        lax.all_gather(w_key, "dp", axis=0, tiled=True),
        lax.all_gather(w_value, "dp", axis=0, tiled=True),
        lax.all_gather(w_out, "dp", axis=1, tiled=True),
        lax.all_gather(w_in, "dp", axis=0, tiled=True),
        lax.all_gather(w_back, "dp", axis=1, tiled=True),
    )
    grad_two_full = lax.all_gather(grad_two.astype(jnp.bfloat16), "tensor", axis=0, tiled=True)
    grad_w_back = matmul_over_rows(activation, grad_two_full)
    grad_pre = matmul_over_cols(grad_two_full, mat_back) * gelu_slope
    grad_b_in_part = jnp.sum(grad_pre, axis=0)
    grad_pre_bf = grad_pre.astype(jnp.bfloat16)
    grad_w_in = matmul_over_rows(hidden_full, grad_pre_bf)
    grad_one_out = grad_two + lax.psum_scatter(
        matmul_over_cols(grad_pre_bf, mat_in).astype(jnp.bfloat16),
        "tensor",
        scatter_dimension=0,
        tiled=True,
    ).astype(jnp.float32)
    grad_w_in, grad_w_back = (
        lax.psum_scatter(grad_w_in, "dp", scatter_dimension=0, tiled=True),
        lax.psum_scatter(grad_w_back, "dp", scatter_dimension=1, tiled=True),
    )
    grad_gain_attn = jnp.sum(grad_one_out * normed_one, axis=0)
    grad_shift_attn = jnp.sum(grad_one_out, axis=0)
    grad_one = norm_back(grad_one_out, normed_one, inv_one, gain_attn)
    grad_b_out = jnp.sum(grad_one, axis=0)
    grad_one_full = lax.all_gather(grad_one.astype(jnp.bfloat16), "tensor", axis=0, tiled=True)
    grad_w_out = matmul_over_rows(context, grad_one_full)
    grad_context = matmul_over_cols(grad_one_full, mat_out).astype(jnp.bfloat16)
    grad_query, grad_keys, grad_values = attend_backward(
        query_rows, key_rows, value_rows, context, grad_context, log_total, seg_ids, HD, block_rows
    )
    grad_b_query_part = jnp.sum(grad_query, axis=0)
    grad_b_value_part = jnp.sum(grad_values, axis=0)
    grad_query_bf = grad_query.astype(jnp.bfloat16)
    grad_keys_bf = grad_keys.astype(jnp.bfloat16)
    grad_values_bf = grad_values.astype(jnp.bfloat16)
    grad_w_query = matmul_over_rows(rows_full, grad_query_bf)
    grad_w_key = matmul_over_rows(rows_full, grad_keys_bf)
    grad_w_value = matmul_over_rows(rows_full, grad_values_bf)
    query_part = matmul_over_cols(grad_query_bf, mat_query)
    key_part = matmul_over_cols(grad_keys_bf, mat_key)
    value_part = matmul_over_cols(grad_values_bf, mat_value)
    grad_in = grad_one + lax.psum_scatter(
        (query_part + key_part + value_part).astype(jnp.bfloat16),
        "tensor",
        scatter_dimension=0,
        tiled=True,
    ).astype(jnp.float32)
    grad_w_query, grad_w_key, grad_w_value, grad_w_out = (
        lax.psum_scatter(grad_w_query, "dp", scatter_dimension=0, tiled=True),
        lax.psum_scatter(grad_w_key, "dp", scatter_dimension=0, tiled=True),
        lax.psum_scatter(grad_w_value, "dp", scatter_dimension=0, tiled=True),
        lax.psum_scatter(grad_w_out, "dp", scatter_dimension=1, tiled=True),
    )

    def widen(part_vec, full_width):
        return lax.dynamic_update_slice_in_dim(
            jnp.zeros((full_width,), jnp.float32), part_vec, tensor_index * part_vec.shape[0], 0
        )

    small_sums = lax.psum(
        (
            widen(grad_b_query_part, b_query.shape[0]),
            widen(grad_b_value_part, b_value.shape[0]),
            grad_b_out,
            grad_gain_attn,
            grad_shift_attn,
            widen(grad_b_in_part, b_in.shape[0]),
            grad_b_back,
            grad_gain_ffn,
            grad_shift_ffn,
        ),
        ("dp", "tensor"),
    )
    return (
        output,
        grad_in,
        grad_w_query,
        small_sums[0],
        grad_w_key,
        grad_w_value,
        small_sums[1],
        grad_w_out,
        small_sums[2],
        small_sums[3],
        small_sums[4],
        grad_w_in,
        small_sums[5],
        grad_w_back,
        small_sums[6],
        small_sums[7],
        small_sums[8],
    )


def solution(mesh):
    placed = (
        P(("dp", "tensor"), None),
        P("dp", None),
        P("dp", "tensor"),
        P(),
        P("dp", "tensor"),
        P("dp", "tensor"),
        P(),
        P("tensor", "dp"),
        P(),
        P(),
        P(),
        P("dp", "tensor"),
        P(),
        P("tensor", "dp"),
        P(),
        P(),
        P(),
        P(("dp", "tensor"), None),
    )
    return jax.shard_map(
        on_device,
        mesh=mesh,
        in_specs=placed,
        out_specs=(
            P(("dp", "tensor"), None),
            P(("dp", "tensor"), None),
            P("dp", "tensor"),
            P(),
            P("dp", "tensor"),
            P("dp", "tensor"),
            P(),
            P("tensor", "dp"),
            P(),
            P(),
            P(),
            P("dp", "tensor"),
            P(),
            P("tensor", "dp"),
            P(),
            P(),
            P(),
        ),
        check_vma=False,
    )
```

profile of v0, /device:TPU:1, one launch (start us, length us, event | category | flops | bytes accessed | tf_op | source)
XLA Modules:
  0.0 597.7 jit_solution(13437722508312491656)
XLA Ops:
  13.0 11.5 %all_gather.37 = bf16[1024,256]{1,0:T(8,128)(2,1)S(1)} all-gather(bf16[128,256]{1,0:T(8,128)(2,1)} %param.27), channel_id=1, replica_groups=mesh['dp'=8,'tensor'=4] {'dp'}, dimensions={0}, use_global_device_ids=true | all-gather | bytes 589824 | tf_op jit(solution)/shard_map/all_gather | solution.py:212
  24.4 9.5 %all_gather.38 = bf16[1024,256]{1,0:T(8,128)(2,1)S(1)} all-gather(bf16[128,256]{1,0:T(8,128)(2,1)} %param.24), channel_id=1, replica_groups=mesh['dp'=8,'tensor'=4] {'dp'}, dimensions={0}, use_global_device_ids=true | all-gather | bytes 589824 | tf_op jit(solution)/shard_map/all_gather | solution.py:210
  34.0 9.2 %all_gather.39 = bf16[1024,256]{1,0:T(8,128)(2,1)S(1)} all-gather(bf16[128,256]{1,0:T(8,128)(2,1)} %param.26), channel_id=1, replica_groups=mesh['dp'=8,'tensor'=4] {'dp'}, dimensions={0}, use_global_device_ids=true | all-gather | bytes 589824 | tf_op jit(solution)/shard_map/all_gather | solution.py:211
  43.1 10.6 %all_gather.40 = bf16[256,1024]{1,0:T(8,128)(2,1)} all-gather(bf16[256,128]{1,0:T(8,128)(2,1)S(1)} %copy-done.33), channel_id=1, replica_groups=mesh['dp'=8,'tensor'=4] {'dp'}, dimensions={1}, use_global_device_ids=true | all-gather | bytes 589824 | tf_op jit(solution)/shard_map/all_gather | solution.py:213
  56.9 4.8 while.38
  64.9 26.2 %reduce-scatter.11.cloned.1.call-done = bf16[128,1024]{1,0:T(8,128)(2,1)} async-done(((bf16[512,1024]{1,0:T(8,128)(2,1)}), bf16[128,1024]{1,0:T(8,128)(2,1)}) %reduce-scatter.11.cloned.1.call-update) | async-done | bytes 262160 | tf_op jit(solution)/shard_map/reduce_scatter | solution.py:223
  96.6 26.7 %all-gather.9.cloned.1.call-done = bf16[512,1024]{1,0:T(8,128)(2,1)} async-done(((bf16[128,1024]{1,0:T(8,128)(2,1)}), bf16[512,1024]{1,0:T(8,128)(2,1)}) %all-gather.9.cloned.1.call-update) | async-done | bytes 1048592 | tf_op jit(solution)/shard_map/all_gather | solution.py:232
  123.3 4.6 multiply_convert_fusion.1
  127.9 25.6 %all-gather.13.cloned.1.call-done = bf16[1024,1024]{1,0:T(8,128)(2,1)} async-done(((bf16[1024,128]{1,0:T(8,128)(2,1)}), bf16[1024,1024]{1,0:T(8,128)(2,1)}) %all-gather.13.cloned.1.call-update) | async-done | bytes 2097168 | tf_op jit(solution)/shard_map/all_gather | solution.py:235
  153.5 3.9 convolution_convert_fusion.2
  157.5 26.6 %reduce-scatter.13.cloned.1.call-done = bf16[128,1024]{1,0:T(8,128)(2,1)} async-done(((bf16[512,1024]{1,0:T(8,128)(2,1)}), bf16[128,1024]{1,0:T(8,128)(2,1)}) %reduce-scatter.13.cloned.1.call-update) | async-done | bytes 262160 | tf_op jit(solution)/shard_map/reduce_scatter | solution.py:241
  187.3 26.3 %all-gather.15.cloned.1.call-done = bf16[512,1024]{1,0:T(8,128)(2,1)} async-done(((bf16[128,1024]{1,0:T(8,128)(2,1)}), bf16[512,1024]{1,0:T(8,128)(2,1)}) %all-gather.15.cloned.1.call-update) | async-done | bytes 1048592 | tf_op jit(solution)/shard_map/all_gather | solution.py:263
  213.6 5.2 fusion.37
  222.1 26.9 %reduce-scatter.15.cloned.1.call-done = bf16[128,1024]{1,0:T(8,128)(2,1)} async-done(((bf16[512,1024]{1,0:T(8,128)(2,1)}), bf16[128,1024]{1,0:T(8,128)(2,1)}) %reduce-scatter.15.cloned.1.call-update) | async-done | bytes 262160 | tf_op jit(solution)/shard_map/reduce_scatter | solution.py:269
  253.7 26.2 %all-gather.17.cloned.1.call-done = bf16[512,1024]{1,0:T(8,128)(2,1)} async-done(((bf16[128,1024]{1,0:T(8,128)(2,1)}), bf16[512,1024]{1,0:T(8,128)(2,1)}) %all-gather.17.cloned.1.call-update) | async-done | bytes 1048592 | tf_op jit(solution)/shard_map/all_gather | solution.py:283
  283.3 13.1 %while.39 = (s32[]{:T(128)}, f32[512,256]{0,1:T(8,128)}, f32[512,256]{0,1:T(8,128)S(1)}, f32[512,256]{0,1:T(8,128)S(1)}, bf16[512,256]{0,1:T(8,128)(2,1)S(1)}, /...) while((s32[]{:T(128)}, f32[512,256]{0,1:T(8,128)}, ...), condition=%wide.region_17.18_spmd.clone, body=%wide.region_15.17_spmd.clone.sunk | while | flops 340395520 | bytes 25846364 | solution.py:170
  308.1 4.5 fusion.41
  320.0 41.3 %all-reduce = (f32[1024]{0:T(1024)}, f32[1024]{0:T(1024)}, f32[1024]{0:T(1024)}, f32[1024]{0:T(1024)}, f32[1024]{0:T(1024)}, /*index=5*/f32[4096]{0:T(1024)}, f32[1024]{0:T(1024)}, f32[1024]{0:T(1024)}, f32[1024]{0:T(1024)}) all-reduce(f32[1024]{0:T(1024)S(1)} %dynamic_update_slice.62, ...), channel_id=1, replica_groups=mesh['dp'=8,'tensor'=4] {'dp','tensor'}, use_global_device_ids=true, to_apply=%region_21.22 | all-reduce | flops 12288 | bytes 98304 | tf_op jit(solution)/shard_map/psum | solution.py:318
  362.9 11.1 %reduce-scatter.21.cloned.1.call-done = f32[128,256]{0,1:T(8,128)} async-done(((f32[1024,256]{0,1:T(8,128)}), f32[128,256]{0,1:T(8,128)}) %reduce-scatter.21.cloned.1.call-update) | async-done | bytes 131088 | tf_op jit(solution)/shard_map/reduce_scatter | solution.py:308
  375.7 37.3 %reduce-scatter.23.cloned.1.call-done = f32[128,256]{0,1:T(8,128)} async-done(((f32[1024,256]{0,1:T(8,128)}), f32[128,256]{0,1:T(8,128)}) %reduce-scatter.23.cloned.1.call-update) | async-done | bytes 131088 | tf_op jit(solution)/shard_map/reduce_scatter | solution.py:309
  414.7 27.5 %reduce-scatter.17.cloned.1.call-done = bf16[128,1024]{1,0:T(8,128)(2,1)} async-done(((bf16[512,1024]{1,0:T(8,128)(2,1)}), bf16[128,1024]{1,0:T(8,128)(2,1)}) %reduce-scatter.17.cloned.1.call-update) | async-done | bytes 262160 | tf_op jit(solution)/shard_map/reduce_scatter | solution.py:300
  443.9 36.5 %reduce-scatter.25.cloned.1.call-done = f32[256,128]{1,0:T(8,128)} async-done(((f32[256,1024]{1,0:T(8,128)}), f32[256,128]{1,0:T(8,128)}) %reduce-scatter.25.cloned.1.call-update) | async-done | bytes 131088 | tf_op jit(solution)/shard_map/reduce_scatter | solution.py:310
  480.5 55.1 %reduce-scatter.29.cloned.1.call-done = f32[1024,128]{1,0:T(8,128)} async-done(((f32[1024,1024]{1,0:T(8,128)}), f32[1024,128]{1,0:T(8,128)}) %reduce-scatter.29.cloned.1.call-update) | async-done | bytes 524304 | tf_op jit(solution)/shard_map/reduce_scatter | solution.py:277
  535.6 54.8 %reduce-scatter.27.cloned.1.call-done = f32[128,1024]{1,0:T(8,128)} async-done(((f32[1024,1024]{1,0:T(8,128)}), f32[128,1024]{1,0:T(8,128)}) %reduce-scatter.27.cloned.1.call-update) | async-done | bytes 524304 | tf_op jit(solution)/shard_map/reduce_scatter | solution.py:276
  (251 shorter events, 72.8 us)
Async XLA Ops:
  8.0 35.1 %copy-start.33 = (bf16[256,128]{1,0:T(8,128)(2,1)S(1)}, bf16[256,128]{1,0:T(8,128)(2,1)}, u32[]{:S(2)}) copy-start(bf16[256,128]{1,0:T(8,128)(2,1)} %param.29) | copy-start | bytes 196612
  8.0 45.7 %all-gather.7.cloned.1.call-start = ((), (), s32[]{:S(2)}) async-start(), calls=%async_computation.10 | async-start | bytes 1310720 | tf_op jit(solution)/shard_map/all_gather | solution.py:208
  8.8 82.3 %reduce-scatter.11.cloned.1.call-start = ((), (), s32[]{:S(2)}) async-start(), calls=%async_computation.11 | async-start | bytes 1310720 | tf_op jit(solution)/shard_map/reduce_scatter | solution.py:223
  24.4 31.2 %copy-start.16 = (bf16[1024,256]{1,0:T(8,128)(2,1)}, bf16[1024,256]{1,0:T(8,128)(2,1)S(1)}, u32[]{:S(2)}) copy-start(bf16[1024,256]{1,0:T(8,128)(2,1)S(1)} %all_gather.37) | copy-start | bytes 1572868
  61.7 31.6 %copy-start.32 = (f32[1024]{0:T(1024)S(1)}, f32[1024]{0:T(1024)}, u32[]{:S(2)}) copy-start(f32[1024]{0:T(1024)} %param.31) | copy-start | bytes 12292
  61.8 31.6 %copy-start.34 = (f32[1024]{0:T(1024)S(1)}, f32[1024]{0:T(1024)}, u32[]{:S(2)}) copy-start(f32[1024]{0:T(1024)} %param.32) | copy-start | bytes 12292
  64.3 32.3 %all-gather.11.cloned.1.call-start = ((), (), s32[]{:S(2)}) async-start(), calls=%async_computation.13 | async-start | bytes 2359296 | tf_op jit(solution)/shard_map/all_gather | solution.py:234
  64.9 58.4 %all-gather.9.cloned.1.call-start = ((), (), s32[]{:S(2)}) async-start(), calls=%async_computation.12 | async-start | bytes 1310720 | tf_op jit(solution)/shard_map/all_gather | solution.py:232
  95.2 58.3 %all-gather.13.cloned.1.call-start = ((), (), s32[]{:S(2)}) async-start(), calls=%async_computation.14 | async-start | bytes 2359296 | tf_op jit(solution)/shard_map/all_gather | solution.py:235
  95.8 88.2 %reduce-scatter.13.cloned.1.call-start = ((), (), s32[]{:S(2)}) async-start(), calls=%async_computation.15 | async-start | bytes 1310720 | tf_op jit(solution)/shard_map/reduce_scatter | solution.py:241
  153.5 30.5 %copy-start.11 = (bf16[128,1024]{1,0:T(8,128)(2,1)S(1)}, bf16[128,1024]{1,0:T(8,128)(2,1)}, u32[]{:S(2)}) copy-start(bf16[128,1024]{1,0:T(8,128)(2,1)} %reduce-scatter.11.cloned.1.call-done) | copy-start | bytes 786436
  153.5 30.5 %copy-start.40 = (f32[1024]{0:T(1024)S(1)}, f32[1024]{0:T(1024)}, u32[]{:S(2)}) copy-start(f32[1024]{0:T(1024)} %param.36) | copy-start | bytes 12292
  157.4 56.2 %all-gather.15.cloned.1.call-start = ((), (), s32[]{:S(2)}) async-start(), calls=%async_computation.16 | async-start | bytes 1310720 | tf_op jit(solution)/shard_map/all_gather | solution.py:263
  187.0 61.9 %reduce-scatter.15.cloned.1.call-start = ((), (), s32[]{:S(2)}) async-start(), calls=%async_computation.17 | async-start | bytes 1310720 | tf_op jit(solution)/shard_map/reduce_scatter | solution.py:269
  222.1 57.8 %all-gather.17.cloned.1.call-start = ((), (), s32[]{:S(2)}) async-start(), calls=%async_computation.18 | async-start | bytes 1310720 | tf_op jit(solution)/shard_map/all_gather | solution.py:283
  249.0 30.9 %copy-start.18 = (bf16[256,1024]{1,0:T(8,128)(2,1)S(1)}, bf16[256,1024]{1,0:T(8,128)(2,1)}, u32[]{:S(2)}) copy-start(bf16[256,1024]{1,0:T(8,128)(2,1)} %all_gather.40) | copy-start | bytes 1572868
  253.6 107.7 %reduce-scatter.19.cloned.1.call-start = ((), (), s32[]{:S(2)}) async-start(), calls=%async_computation.20 | async-start | bytes 1179648 | tf_op jit(solution)/shard_map/reduce_scatter | solution.py:307
  299.3 74.8 %reduce-scatter.21.cloned.1.call-start = ((), (), s32[]{:S(2)}) async-start(), calls=%async_computation.21 | async-start | bytes 1179648 | tf_op jit(solution)/shard_map/reduce_scatter | solution.py:308
  300.8 112.2 %reduce-scatter.23.cloned.1.call-start = ((), (), s32[]{:S(2)}) async-start(), calls=%async_computation.22 | async-start | bytes 1179648 | tf_op jit(solution)/shard_map/reduce_scatter | solution.py:309
  302.4 139.7 %reduce-scatter.17.cloned.1.call-start = ((), (), s32[]{:S(2)}) async-start(), calls=%async_computation.19 | async-start | bytes 1310720 | tf_op jit(solution)/shard_map/reduce_scatter | solution.py:300
  306.5 174.0 %reduce-scatter.25.cloned.1.call-start = ((), (), s32[]{:S(2)}) async-start(), calls=%async_computation.23 | async-start | bytes 1179648 | tf_op jit(solution)/shard_map/reduce_scatter | solution.py:310
  308.0 227.6 %reduce-scatter.29.cloned.1.call-start = ((), (), s32[]{:S(2)}) async-start(), calls=%async_computation.25 | async-start | bytes 4718592 | tf_op jit(solution)/shard_map/reduce_scatter | solution.py:277
  312.6 277.8 %reduce-scatter.27.cloned.1.call-start = ((), (), s32[]{:S(2)}) async-start(), calls=%async_computation.24 | async-start | bytes 4718592 | tf_op jit(solution)/shard_map/reduce_scatter | solution.py:276
  317.4 124.7 %copy-start.15 = (f32[128,1024]{1,0:T(8,128)S(1)}, f32[128,1024]{1,0:T(8,128)}, u32[]{:S(2)}) copy-start(f32[128,1024]{1,0:T(8,128)} %copy-done.14) | copy-start | bytes 1572868
  (47 other events, 302.0 us)
Sparse Core Ops, SparseCore 0:
  10.4 29.5 all-gather.6
  64.4 26.6 reduce-scatter.10
  157.5 26.4 reduce-scatter.12
  187.2 26.3 all-gather.14
  222.2 26.7 reduce-scatter.14
Sparse Core Ops, SparseCore 1:
  66.7 27.8 all-gather.10
  96.5 26.8 all-gather.8
  125.1 28.4 all-gather.12
  253.7 26.1 all-gather.16
  299.4 35.5 reduce-scatter.18
  338.1 35.9 reduce-scatter.20
  377.1 35.9 reduce-scatter.22
  415.2 26.9 reduce-scatter.16
  445.8 34.7 reduce-scatter.24
  484.4 51.1 reduce-scatter.28
  539.4 50.9 reduce-scatter.26
where the time goes:
time: 600 us; the launch traced here: 598 us
  waiting for transfers between devices  409 us (68%)
  blocking collectives  82 us (14%)
  matrix products  48.7 us (8%)
  other arithmetic  21.4 us (4%)
  local copies, waits for them, and re-layouts  17.9 us (3%)
  between operations  17.3 us (3%)
    reduce_scatter x1, waiting for transfers between devices, on_device(): lax.psum_scatter(grad_w_back, 'dp', scatter_dimension=1, tiled=True)  55.1 us
    reduce_scatter x1, waiting for transfers between devices, on_device(): lax.psum_scatter(grad_w_in, 'dp', scatter_dimension=0, tiled=True)  54.8 us
    psum x1, blocking collectives, on_device(): lax.psum((widen(grad_b_query_part, b_query.shape[0]), widen(grad_b_value_...  41.3 us
    reduce_scatter x1, waiting for transfers between devices, on_device(): lax.psum_scatter(grad_w_value, 'dp', scatter_dimension=0, tiled=True)  37.3 us
    reduce_scatter x1, waiting for transfers between devices, on_device(): lax.psum_scatter(grad_w_out, 'dp', scatter_dimension=1, tiled=True)  36.5 us
    reduce_scatter x1, waiting for transfers between devices, on_device(): lax.psum_scatter((query_part + key_part + value_part).astype(jnp.bfloat16...  27.5 us
    reduce_scatter x1, waiting for transfers between devices, on_device(): lax.psum_scatter(matmul_over_cols(grad_pre_bf, mat_in).astype(jnp.bfloat1...  26.9 us
    all_gather x1, waiting for transfers between devices, on_device(): hidden_full = lax.all_gather(hidden_bf, 'tensor', axis=0, tiled=True)  26.7 us
  transfers between devices with their start and end apart: 16, of which 13 were waited for; matrix products, arithmetic and copies ran while one was open for 6% of the time, Pallas kernels for 0%

commit v1 on v0

--- a/solution.py
+++ b/solution.py
@@ -1,6 +1,10 @@
+from types import SimpleNamespace
+
 import jax
 import jax.numpy as jnp
 from jax import lax
+from jax.experimental import pallas as pl
+from jax.experimental.pallas import tpu as pltpu
 from jax.sharding import PartitionSpec as P
 
 HD = 64
@@ -170,7 +174,7 @@
     return lax.fori_loop(0, pair_count * block_count, back_step, (zero_grad, zero_grad, zero_grad))
 
 
-def on_device(
+def on_device_plain(
     tokens,
     lengths,
     w_query,
@@ -350,6 +354,832 @@
     )
 
 
+MESH_ID = pl.DeviceIdType.MESH
+F32 = jnp.float32
+BF16 = jnp.bfloat16
+
+SLOTS = 4
+BLOCK = 128
+GROUP = 512
+WIDTH = 1024
+HEAD_COLS = 256
+HIDDEN = 1024
+N_SEM = 176
+HALVES = dict(q=(128, 256), k=(128, 256), v=(128, 256), o=(256, 128), i=(128, 1024), b=(1024, 128))
+STAGES = ("xa", "ya", "s2", "r2", "zs", "zr")
+
+
+def flip(bit):
+    return 1 - bit
+
+
+def slot_step(t, j):
+    return (t % 2 + j % 2) % 2 + 2 * ((t // 2 + j // 2) % 2)
+
+
+def rows_of(r, count=BLOCK):
+    return pl.ds(pl.multiple_of(r * BLOCK, BLOCK), count)
+
+
+def cols_of(n, count=256):
+    return pl.ds(pl.multiple_of(n * count, count), count)
+
+
+def dot_nn(a, b):
+    return jnp.dot(a, b, preferred_element_type=F32)
+
+
+def dot_nt(a, b):
+    return lax.dot_general(a, b, (((1,), (1,)), ((), ())), preferred_element_type=F32)
+
+
+def dot_tn(a, b):
+    return lax.dot_general(a, b, (((0,), (0,)), ((), ())), preferred_element_type=F32)
+
+
+def scratch_table():
+    act = lambda n: pltpu.VMEM((GROUP, n), BF16)
+    table = dict(
+        w3=pltpu.VMEM((3 * WIDTH, HEAD_COLS), BF16),
+        wo=pltpu.VMEM((4, HEAD_COLS, 256), BF16),
+        wi=pltpu.VMEM((WIDTH, HIDDEN), BF16),
+        wb=pltpu.VMEM((4, HIDDEN, 256), BF16),
+        lens_own=pltpu.VMEM((2, 8, 128), F32),
+        lens_got=pltpu.VMEM((2, 8, 128), F32),
+        lens_use=pltpu.VMEM((2, 8, 128), F32),
+        tk=act(WIDTH),
+        tkt=pltpu.VMEM((WIDTH, GROUP), BF16),
+        cot_own=pltpu.VMEM((BLOCK, WIDTH), BF16),
+        bias=pltpu.VMEM((GROUP, GROUP), F32),
+        q=act(HEAD_COLS),
+        qt=pltpu.VMEM((HEAD_COLS, GROUP), BF16),
+        k=act(HEAD_COLS),
+        ks=act(HEAD_COLS),
+        v=act(HEAD_COLS),
+        ps=pltpu.VMEM((4, GROUP, GROUP), BF16),
+        ctx=act(HEAD_COLS),
+        ctxt=pltpu.VMEM((HEAD_COLS, GROUP), BF16),
+        hid=act(WIDTH),
+        hidt=pltpu.VMEM((WIDTH, GROUP), BF16),
+        act=act(HIDDEN),
+        actt=pltpu.VMEM((HIDDEN, GROUP), BF16),
+        slope=pltpu.VMEM((GROUP, HIDDEN), F32),
+        g2=act(WIDTH),
+        gpre=act(HIDDEN),
+        g1=act(WIDTH),
+        gctxt=pltpu.VMEM((HEAD_COLS, GROUP), BF16),
+        dq=act(HEAD_COLS),
+        dkt=pltpu.VMEM((HEAD_COLS, GROUP), F32),
+        dvt=pltpu.VMEM((HEAD_COLS, GROUP), F32),
+        dk=act(HEAD_COLS),
+        dv=act(HEAD_COLS),
+        hid1=pltpu.VMEM((BLOCK, WIDTH), F32),
+        normed1=pltpu.VMEM((BLOCK, WIDTH), F32),
+        inv1=pltpu.VMEM((BLOCK, 128), F32),
+        g2f=pltpu.VMEM((BLOCK, WIDTH), F32),
+        g1f=pltpu.VMEM((BLOCK, WIDTH), F32),
+        out_own=pltpu.VMEM((BLOCK, WIDTH), BF16),
+        gtok_own=pltpu.VMEM((BLOCK, WIDTH), BF16),
+        gtok_got=pltpu.VMEM((BLOCK, WIDTH), BF16),
+        rs_own=pltpu.VMEM((4, BLOCK, WIDTH), BF16),
+        rs_out=pltpu.VMEM((4, 3, BLOCK, WIDTH), BF16),
+        rs_got=pltpu.VMEM((4, 3, BLOCK, WIDTH), BF16),
+        sums=pltpu.VMEM((6, 16, WIDTH), F32),
+        sums_got=pltpu.VMEM((5, 16, WIDTH), F32),
+        gb_in=pltpu.VMEM((1, HIDDEN), F32),
+        g3=pltpu.VMEM((3 * WIDTH, HEAD_COLS), BF16),
+        go=pltpu.VMEM((4, HEAD_COLS, 256), BF16),
+        gi=pltpu.VMEM((WIDTH, HIDDEN), BF16),
+        gb=pltpu.VMEM((4, HIDDEN, 256), BF16),
+        stage={},
+        ssem=pltpu.SemaphoreType.DMA((N_SEM,)),
+        rsem=pltpu.SemaphoreType.DMA((N_SEM,)),
+    )
+    for name, dims in HALVES.items():
+        table["stage"][name] = {part: pltpu.VMEM((2,) + dims, BF16) for part in STAGES}
+    return table
+
+
+def layer_kernel(tok, lens, wq, bq, wk, wv, bv, wo, bo, ga, sa, wi, bi, wb, bb, gf, sf, cot, out, gtok, gq, gk, gv, go, gi,
+                 gb, sums, *scratch):
+    a = SimpleNamespace(tok=tok, lens=lens, wq=wq, bq=bq, wk=wk, wv=wv, bv=bv, wo=wo, bo=bo, ga=ga, sa=sa, wi=wi, bi=bi,
+                        wb=wb, bb=bb, gf=gf, sf=sf, cot=cot)
+    o = SimpleNamespace(out=out, gtok=gtok, gq=gq, gk=gk, gv=gv, go=go, gi=gi, gb=gb, sums=sums)
+    s = SimpleNamespace(**jax.tree.unflatten(jax.tree.structure(scratch_table()), scratch))
+    ssem, rsem = s.ssem, s.rsem
+
+    dp = lax.axis_index("dp")
+    z = lax.axis_index("tensor")
+    b, c = dp // 2, dp % 2
+    zl, zh = z % 2, z // 2
+    t = zl * 2 + c
+    bx = b + 1 - 2 * (b % 2)
+    by = (b + 2) % 4
+    bd = 3 - b
+    t1, t2, t3 = slot_step(t, 1), slot_step(t, 2), slot_step(t, 3)
+
+    def dev(pos, core, zz):
+        return (pos * 2 + core, zz)
+
+    partner = dev(b, flip(c), z)
+    z_near = z + 1 - 2 * (z % 2)
+    z_far = (z + 2) % 4
+    pair = dev(b, c, z_near)
+    across = dev(b, c, z_far)
+    x_near = dev(bx, c, z)
+    y_near = dev(by, c, z)
+
+    taken = {"s": 0, "r": 0}
+
+    def take(kind, count=1):
+        first = taken[kind]
+        taken[kind] = first + count
+        assert taken[kind] <= N_SEM
+        return first
+
+    to_drain = []
+
+    def send(src, dst, device, sk, rk, cond=None):
+        copy = pltpu.make_async_remote_copy(
+            src_ref=src, dst_ref=dst, send_sem=ssem.at[sk], recv_sem=rsem.at[rk], device_id=device,
+            device_id_type=MESH_ID)
+        copy.start()
+        if cond is None:
+            to_drain.append((copy, None))
+
+    def got(dst, rk):
+        pltpu.make_async_copy(dst, dst, rsem.at[rk]).wait()
+
+    def send_or_keep(src, dst, device, is_self, sk, rk):
+        copy = pltpu.make_async_remote_copy(
+            src_ref=src, dst_ref=dst, send_sem=ssem.at[sk], recv_sem=rsem.at[rk], device_id=device,
+            device_id_type=MESH_ID)
+
+        @pl.when(is_self)
+        def _():
+            pltpu.make_async_copy(src, dst, rsem.at[rk]).start()
+
+        @pl.when(jnp.logical_not(is_self))
+        def _():
+            copy.start()
+
+        to_drain.append((copy, is_self))
+
+    barrier = pltpu.get_barrier_semaphore()
+    peers = [x_near, y_near]
+    for dz in range(4):
+        for dc in range(2):
+            if dz or dc:
+                peers.append(dev(b, (c + dc) % 2, (z + dz) % 4))
+    for peer in peers:
+        pl.semaphore_signal(barrier, inc=1, device_id=peer, device_id_type=MESH_ID)
+    pl.semaphore_wait(barrier, len(peers))
+
+    def piece_qkv(m, home):
+        base = m * WIDTH
+        return SimpleNamespace(
+            home=home,
+            own=lambda bb, cc: s.w3.at[pl.ds(pl.multiple_of(base + bb * 256 + cc * 128, 128), 128), :],
+            block=lambda bb: s.w3.at[pl.ds(pl.multiple_of(base + bb * 256, 256), 256), :],
+            half=lambda bb, h: s.w3.at[pl.ds(pl.multiple_of(base + bb * 256 + h * 128, 128), 128), :])
+
+    piece_o = SimpleNamespace(
+        home=a.wo,
+        own=lambda bb, cc: s.wo.at[bb, :, pl.ds(pl.multiple_of(cc * 128, 128), 128)],
+        block=lambda bb: s.wo.at[bb],
+        half=lambda bb, h: s.wo.at[bb, pl.ds(h * 128, 128), :])
+
+    def piece_in(j):
+        cols = pl.ds(j * 512, 512)
+        return SimpleNamespace(
+            home=a.wi.at[:, cols],
+            own=lambda bb, cc: s.wi.at[pl.ds(pl.multiple_of(bb * 256 + cc * 128, 128), 128), cols],
+            block=lambda bb: s.wi.at[pl.ds(pl.multiple_of(bb * 256, 256), 256), cols],
+            half=lambda bb, h: s.wi.at[pl.ds(pl.multiple_of(bb * 256 + h * 128, 128), 128), cols])
+
+    def piece_back(j):
+        part = pl.ds(j * 512, 512)
+        return SimpleNamespace(
+            home=a.wb.at[part, :],
+            own=lambda bb, cc: s.wb.at[bb, part, pl.ds(pl.multiple_of(cc * 128, 128), 128)],
+            block=lambda bb: s.wb.at[bb, part, :],
+            half=lambda bb, h: s.wb.at[bb, pl.ds(j * 512 + h * 256, 256), :])
+
+    pieces = dict(q=piece_qkv(0, a.wq), k=piece_qkv(1, a.wk), v=piece_qkv(2, a.wv), o=piece_o,
+                  i0=piece_in(0), i1=piece_in(1), b0=piece_back(0), b1=piece_back(1))
+    for piece in pieces.values():
+        piece.s1 = take("s", 2)
+        piece.r1 = take("r", 2)
+        piece.s2 = take("s", 4)
+        piece.r2 = take("r", 4)
+
+    def from_home(name):
+        piece = pieces[name]
+        for far in range(2):
+            zt, ct = z // 2 + 2 * far, z % 2
+            is_self = jnp.logical_and(zt == z, ct == c)
+            send_or_keep(piece.home, piece.own(b, c), dev(b, ct, zt), is_self, piece.s1 + far,
+                         piece.r1 + c)
+
+    def over_plane(name):
+        piece = pieces[name]
+        for cc in range(2):
+            got(piece.own(b, cc), piece.r1 + cc)
+        send(piece.block(b), piece.block(b), x_near, piece.s2, piece.r2)
+        send(piece.block(b), piece.block(b), y_near, piece.s2 + 1, piece.r2 + 1)
+
+    def relay(name):
+        piece = pieces[name]
+        got(piece.block(bx), piece.r2)
+        send(piece.half(bx, 0), piece.half(bx, 0), y_near, piece.s2 + 2, piece.r2 + 2)
+        got(piece.block(by), piece.r2 + 1)
+        send(piece.half(by, 1), piece.half(by, 1), x_near, piece.s2 + 3, piece.r2 + 3)
+
+    def arrived(name):
+        piece = pieces[name]
+        got(piece.half(bd, 0), piece.r2 + 2)
+        got(piece.half(bd, 1), piece.r2 + 3)
+
+    tok_s, tok_r = take("s", 2), take("r", 4)
+    fwd_s = take("s", 4)
+    lens_s, lens_r = take("s"), take("r")
+    cot_s, cot_r = take("s"), take("r")
+
+    def send_lens():
+        first = a.lens[0, 0].astype(F32)
+        s.lens_own[0] = jnp.full((8, 128), first, F32)
+        s.lens_own[1] = jnp.full((8, 128), first + a.lens[0, 1].astype(F32), F32)
+        send(s.lens_own, s.lens_got, partner, lens_s, lens_r)
+
+    def take_lens():
+        got(s.lens_got, lens_r)
+
+        @pl.when(c == zh)
+        def _():
+            s.lens_use[...] = s.lens_own[...]
+
+        @pl.when(c != zh)
+        def _():
+            s.lens_use[...] = s.lens_got[...]
+
+    def tok_block(r):
+        return s.tk.at[rows_of(r), :]
+
+    def send_tokens():
+        for j in range(2):
+            zt = 2 * c + j
+            send_or_keep(a.tok, tok_block(z), dev(b, c, zt), zt == z, tok_s + j, tok_r + z)
+
+    def share_tokens():
+        for r in range(SLOTS):
+            got(tok_block(r), tok_r + r)
+            copy = pltpu.make_async_remote_copy(
+                src_ref=tok_block(r), dst_ref=tok_block(r), send_sem=ssem.at[fwd_s + r], recv_sem=rsem.at[tok_r + r],
+                device_id=partner, device_id_type=MESH_ID)
+
+            @pl.when(c == zh)
+            def _():
+                copy.start()
+
+            to_drain.append((copy, c != zh))
+
+    def send_cotangent():
+        zt, ct = 2 * c + z // 2, z % 2
+        is_self = jnp.logical_and(zt == z, ct == c)
+        send_or_keep(a.cot, s.cot_own, dev(b, ct, zt), is_self, cot_s, cot_r)
+
+    gather_s = [take("s", 3) for _ in range(3)]
+    gather_r = [take("r", 3) for _ in range(3)]
+    scatter_s = [take("s", 3) for _ in range(4)]
+    scatter_r = [take("r", 3) for _ in range(4)]
+
+    def block_at(full, r):
+        return full.at[rows_of(r), :]
+
+    def gather_start(which, full):
+        send(block_at(full, t), block_at(full, t), pair, gather_s[which], gather_r[which] + 1)
+        send(block_at(full, t), block_at(full, t), partner, gather_s[which] + 1, gather_r[which])
+
+    def gather_steps(which, full):
+        forward = pltpu.make_async_remote_copy(
+            src_ref=block_at(full, t2), dst_ref=block_at(full, t2), send_sem=ssem.at[gather_s[which] + 2],
+            recv_sem=rsem.at[gather_r[which] + 2], device_id=partner, device_id_type=MESH_ID)
+        to_drain.append((forward, None))
+
+        def step(j):
+            @pl.when(j == 1)
+            def _():
+                got(block_at(full, t1), gather_r[which])
+
+            @pl.when(j == 2)
+            def _():
+                got(block_at(full, t2), gather_r[which] + 1)
+                forward.start()
+
+            @pl.when(j == 3)
+            def _():
+                got(block_at(full, t3), gather_r[which] + 2)
+
+        return step
+
+    def scatter(which, part):
+        out, back = s.rs_out, s.rs_got
+        ss, rr = scatter_s[which], scatter_r[which]
+        part(t3, out.at[which, 0], None)
+        send(out.at[which, 0], back.at[which, 0], partner, ss, rr)
+        part(t1, out.at[which, 2], None)
+        send(out.at[which, 2], back.at[which, 2], partner, ss + 2, rr + 2)
+        got(back.at[which, 0], rr)
+        part(t2, out.at[which, 1], back.at[which, 0])
+        send(out.at[which, 1], back.at[which, 1], pair, ss + 1, rr + 1)
+        part(t, s.rs_own.at[which], None)
+
+    def scatter_wait(which):
+        got(s.rs_got.at[which, 2], scatter_r[which] + 2)
+        got(s.rs_got.at[which, 1], scatter_r[which] + 1)
+
+    def scatter_rows(which, chunk):
+        total = s.rs_own[which, chunk, :].astype(F32) + s.rs_got[which, 2, chunk, :].astype(F32)
+        return total + s.rs_got[which, 1, chunk, :].astype(F32)
+
+    def put_part(dst, add, n, value):
+        value = value.astype(BF16)
+        if add is not None:
+            value = (value.astype(F32) + add[:, cols_of(n)].astype(F32)).astype(BF16)
+        dst[:, cols_of(n)] = value
+
+    def loop(count, body):
+        lax.fori_loop(0, count, lambda i, _: (body(i), 0)[1], 0)
+
+    def grad_qkv(m):
+        base = m * WIDTH
+        return lambda bb, h: s.g3.at[pl.ds(pl.multiple_of(base + bb * 256 + h * 128, 128), 128), :]
+
+    grad_half = dict(
+        q=grad_qkv(0), k=grad_qkv(1), v=grad_qkv(2),
+        o=lambda bb, h: s.go.at[bb, :, pl.ds(h * 128, 128)],
+        i=lambda bb, h: s.gi.at[pl.ds(pl.multiple_of(bb * 256 + h * 128, 128), 128), :],
+        b=lambda bb, h: s.gb.at[bb, :, pl.ds(h * 128, 128)])
+    grad_out = dict(q=o.gq, k=o.gk, v=o.gv, o=o.go, i=o.gi, b=o.gb)
+    grad_chunk = dict(q=128, k=128, v=128, o=128, i=32, b=256)
+    grad_s = {name: take("s", 8) for name in grad_half}
+    grad_r = {name: take("r", 8) for name in grad_half}
+
+    def stage(name, *which):
+        return tuple(s.stage[name][STAGES[i]] for i in which)
+
+    def chunks(name, body):
+        size = grad_chunk[name]
+        count = HALVES[name][0] // size
+        loop(count, lambda i: body(pl.ds(pl.multiple_of(i * size, size), size)))
+
+    def grad_first(name):
+        half, ss, rr = grad_half[name], grad_s[name], grad_r[name]
+        xa, ya = stage(name, 0, 1)
+        send(half(bd, 0), xa.at[1], x_near, ss + 1, rr + 1)
+        send(half(bd, 1), ya.at[1], y_near, ss + 3, rr + 3)
+        send(half(bx, 0), xa.at[0], x_near, ss, rr)
+        send(half(by, 1), ya.at[0], y_near, ss + 2, rr + 2)
+
+    def grad_second(name):
+        half, ss, rr = grad_half[name], grad_s[name], grad_r[name]
+        xa, ya, s2, r2 = stage(name, 0, 1, 2, 3)
+        got(xa.at[1], rr + 1)
+        mine = half(by, 0)
+
+        def add_x(ch):
+            s2[0, ch, :] = (mine[ch, :].astype(F32) + xa[1, ch, :].astype(F32)).astype(BF16)
+        chunks(name, add_x)
+        send(s2.at[0], r2.at[0], y_near, ss + 4, rr + 4)
+        got(ya.at[1], rr + 3)
+        other = half(bx, 1)
+
+        def add_y(ch):
+            s2[1, ch, :] = (other[ch, :].astype(F32) + ya[1, ch, :].astype(F32)).astype(BF16)
+        chunks(name, add_y)
+        send(s2.at[1], r2.at[1], x_near, ss + 5, rr + 5)
+
+    def grad_third(name):
+        half, ss, rr = grad_half[name], grad_s[name], grad_r[name]
+        xa, ya, r2 = stage(name, 0, 1, 3)
+        zs, zr = stage(name, 4, 5)
+        for h, first in ((0, xa), (1, ya)):
+            got(first.at[0], rr + 2 * h)
+            got(r2.at[h], rr + 4 + h)
+            mine = half(b, h)
+
+            def add_all(ch):
+                total = mine[ch, :].astype(F32) + first[0, ch, :].astype(F32) + r2[h, ch, :].astype(F32)
+                zs[h, ch, :] = total.astype(BF16)
+            chunks(name, add_all)
+            is_self = jnp.logical_and(c == h, z == t)
+            send_or_keep(zs.at[h], zr.at[zh], dev(b, h, t), is_self, ss + 6 + h, rr + 6 + zh)
+
+    def grad_final(name):
+        rr, (zr,) = grad_r[name], stage(name, 5)
+        got(zr.at[0], rr + 6)
+        got(zr.at[1], rr + 7)
+
+        def add_both(ch):
+            grad_out[name][ch, :] = zr[0, ch, :].astype(F32) + zr[1, ch, :].astype(F32)
+        chunks(name, add_both)
+
+    from_home("q")
+    from_home("k")
+    from_home("v")
+    send_lens()
+    send_tokens()
+    from_home("o")
+    from_home("i0")
+    from_home("i1")
+    from_home("b0")
+    from_home("b1")
+    send_cotangent()
+    s.sums[0] = jnp.zeros((16, WIDTH), F32)
+    s.gb_in[...] = jnp.zeros((1, HIDDEN), F32)
+    over_plane("q")
+    over_plane("k")
+    over_plane("v")
+    relay("q")
+    relay("k")
+    relay("v")
+    share_tokens()
+    over_plane("o")
+    take_lens()
+
+    def make_bias(r):
+        first, end = s.lens_use[0][0:1, 0:1], s.lens_use[1][0:1, 0:1]
+        row = (lax.broadcasted_iota(jnp.int32, (BLOCK, GROUP), 0) + r * BLOCK).astype(F32)
+        col = lax.broadcasted_iota(jnp.int32, (BLOCK, GROUP), 1).astype(F32)
+        seg = lambda p: jnp.where(p >= end, 2.0, jnp.where(p >= first, 1.0, 0.0))
+        s.bias[rows_of(r), :] = jnp.where(seg(row) == seg(col), 0.0, masked_value)
+    loop(SLOTS, make_bias)
+
+    def turn_tokens(r):
+        s.tkt[:, rows_of(r)] = s.tk[rows_of(r), :].T
+    loop(SLOTS, turn_tokens)
+
+    head_cols = pl.ds(pl.multiple_of(t * HEAD_COLS, HEAD_COLS), HEAD_COLS)
+
+    def project(m):
+        def body(r):
+            rows = rows_of(r)
+            acc = dot_nn(s.tk[rows, :], s.w3[pl.ds(m * WIDTH, WIDTH), :])
+            if m == 0:
+                acc = acc + a.bq[:, head_cols]
+                scaled = acc.astype(BF16).astype(F32) * 0.125
+                s.q[rows, :] = scaled.astype(BF16)
+                s.qt[:, rows] = scaled.astype(BF16).T
+            elif m == 1:
+                s.k[rows, :] = acc.astype(BF16)
+                s.ks[rows, :] = (acc.astype(BF16).astype(F32) * 0.125).astype(BF16)
+            else:
+                acc = acc + a.bv[:, head_cols]
+                s.v[rows, :] = acc.astype(BF16)
+        loop(SLOTS, body)
+
+    for m, name in enumerate("qkv"):
+        arrived(name)
+        project(m)
+    relay("o")
+
+    def attend(r):
+        rows = rows_of(r)
+        parts = []
+        for h in range(4):
+            cols = slice(64 * h, 64 * h + 64)
+            scores = dot_nt(s.q[rows, cols], s.k[:, cols]) + s.bias[rows, :]
+            top = jnp.max(scores, axis=-1, keepdims=True)
+            weight = jnp.exp(scores - top)
+            total = jnp.sum(weight, axis=-1, keepdims=True)
+            prob = (weight * (1.0 / total)).astype(BF16)
+            s.ps[h, rows, :] = prob
+            parts.append(dot_nn(prob, s.v[:, cols]))
+        context = jnp.concatenate(parts, axis=1).astype(BF16)
+        s.ctx[rows, :] = context
+        s.ctxt[:, rows] = context.T
+    loop(SLOTS, attend)
+
+    over_plane("i0")
+    over_plane("i1")
+    arrived("o")
+
+    def attn_part(r, dst, add):
+        rows = s.ctx[rows_of(r), :]
+        loop(4, lambda n: put_part(dst, add, n, dot_nn(rows, s.wo[n])))
+    scatter(0, attn_part)
+    relay("i0")
+    relay("i1")
+    over_plane("b0")
+    over_plane("b1")
+    scatter_wait(0)
+
+    CH = 32
+
+    def own_chunk(i):
+        return pl.ds(pl.multiple_of(i * CH, CH), CH)
+
+    def group_chunk(i):
+        return pl.ds(pl.multiple_of(t * BLOCK + i * CH, CH), CH)
+
+    def norm_one(i):
+        ch = own_chunk(i)
+        resid = s.tk[group_chunk(i), :].astype(F32) + scatter_rows(0, ch) + a.bo[...]
+        centered = resid - jnp.mean(resid, axis=-1, keepdims=True)
+        inv = lax.rsqrt(jnp.mean(centered * centered, axis=-1, keepdims=True) + epsilon)
+        normed = centered * inv
+        hidden = normed * a.ga[...] + a.sa[...]
+        s.normed1[ch, :] = normed
+        s.inv1[ch, :] = jnp.broadcast_to(inv, (CH, 128))
+        s.hid1[ch, :] = hidden
+        s.hid[group_chunk(i), :] = hidden.astype(BF16)
+    loop(BLOCK // CH, norm_one)
+    gather_start(0, s.hid)
+    arrived("i0")
+    arrived("i1")
+
+    next_hid = gather_steps(0, s.hid)
+
+    def ffn_in(j):
+        next_hid(j)
+        r = slot_step(t, j)
+        rows = rows_of(r)
+
+        def body(n):
+            cols = cols_of(n)
+            bias = a.bi[:, pl.ds(pl.multiple_of(t * HIDDEN + n * 256, 256), 256)]
+            pre = dot_nn(s.hid[rows, :], s.wi[:, cols]) + bias
+            cdf = 0.5 * (1.0 + lax.erf(pre * 0.7071067811865476))
+            pdf = jnp.exp(-0.5 * pre * pre) * 0.3989422804014327
+            s.act[rows, cols] = (pre * cdf).astype(BF16)
+            s.slope[rows, cols] = cdf + pre * pdf
+        loop(4, body)
+        s.actt[:, rows] = s.act[rows, :].T
+        s.hidt[:, rows] = s.hid[rows, :].T
+    loop(SLOTS, ffn_in)
+    relay("b0")
+    relay("b1")
+    arrived("b0")
+    arrived("b1")
+
+    def ffn_part(r, dst, add):
+        loop(4, lambda n: put_part(dst, add, n, dot_nn(s.act[rows_of(r), :], s.wb[n])))
+    scatter(1, ffn_part)
+    got(s.cot_own, cot_r)
+    scatter_wait(1)
+
+    def add_rows(row, value):
+        s.sums[0, row:row + 1, :] += jnp.sum(value, axis=0, keepdims=True)
+
+    def norm_two(i):
+        ch = own_chunk(i)
+        resid = s.hid1[ch, :] + scatter_rows(1, ch) + a.bb[...]
+        centered = resid - jnp.mean(resid, axis=-1, keepdims=True)
+        inv = lax.rsqrt(jnp.mean(centered * centered, axis=-1, keepdims=True) + epsilon)
+        normed = centered * inv
+        position = lax.broadcasted_iota(jnp.int32, (CH, 128), 0) + (t * BLOCK + i * CH)
+        live = jnp.where(position.astype(F32) < s.lens_use[1][0:1, :], 1.0, 0.0)[:, 0:1]
+        s.out_own[ch, :] = ((normed * a.gf[...] + a.sf[...]) * live).astype(BF16)
+        grad = s.cot_own[ch, :].astype(F32) * live
+        add_rows(4, grad * normed)
+        add_rows(5, grad)
+        u = grad * a.gf[...]
+        first = jnp.mean(u, axis=-1, keepdims=True)
+        second = jnp.mean(u * normed, axis=-1, keepdims=True)
+        grad_two = inv * (u - first - normed * second)
+        add_rows(3, grad_two)
+        s.g2f[ch, :] = grad_two
+        s.g2[group_chunk(i), :] = grad_two.astype(BF16)
+    loop(BLOCK // CH, norm_two)
+    gather_start(1, s.g2)
+    out_s, out_r = take("s"), take("r")
+    home_self = jnp.logical_and(zh == c, t == z)
+    send_or_keep(s.out_own, o.out, dev(b, zh, t), home_self, out_s, out_r)
+
+    next_g2 = gather_steps(1, s.g2)
+
+    def ffn_back(j):
+        next_g2(j)
+        r = slot_step(t, j)
+        rows = rows_of(r)
+
+        def body(n):
+            cols = cols_of(n)
+            acc = dot_nt(s.g2[rows, 0:256], s.wb[0, cols, :])
+            for k in range(1, 4):
+                acc = acc + dot_nt(s.g2[rows, 256 * k:256 * k + 256], s.wb[k, cols, :])
+            grad = acc * s.slope[rows, cols]
+            s.gb_in[:, cols] += jnp.sum(grad, axis=0, keepdims=True)
+            s.gpre[rows, cols] = grad.astype(BF16)
+        loop(4, body)
+    loop(SLOTS, ffn_back)
+
+    def grad_back(n):
+        def body(m):
+            part = cols_of(m)
+            s.gb[n, part, :] = dot_nn(s.actt[part, :], s.g2[:, cols_of(n)]).astype(BF16)
+        loop(4, body)
+    loop(4, grad_back)
+    grad_first("b")
+
+    def in_part(r, dst, add):
+        loop(4, lambda n: put_part(dst, add, n, dot_nt(s.gpre[rows_of(r), :], s.wi[cols_of(n), :])))
+    scatter(2, in_part)
+
+    def grad_in(n):
+        def body(m):
+            part = cols_of(m)
+            s.gi[part, cols_of(n)] = dot_nn(s.hidt[part, :], s.gpre[:, cols_of(n)]).astype(BF16)
+        loop(4, body)
+    loop(4, grad_in)
+    grad_first("i")
+    scatter_wait(2)
+
+    def norm_one_back(i):
+        ch = own_chunk(i)
+        grad = s.g2f[ch, :] + scatter_rows(2, ch)
+        normed = s.normed1[ch, :]
+        add_rows(1, grad * normed)
+        add_rows(2, grad)
+        u = grad * a.ga[...]
+        first = jnp.mean(u, axis=-1, keepdims=True)
+        second = jnp.mean(u * normed, axis=-1, keepdims=True)
+        grad_one = s.inv1[ch, 0:1] * (u - first - normed * second)
+        add_rows(0, grad_one)
+        s.g1f[ch, :] = grad_one
+        s.g1[group_chunk(i), :] = grad_one.astype(BF16)
+    loop(BLOCK // CH, norm_one_back)
+    gather_start(2, s.g1)
+    grad_second("b")
+    s.dkt[...] = jnp.zeros((HEAD_COLS, GROUP), F32)
+    s.dvt[...] = jnp.zeros((HEAD_COLS, GROUP), F32)
+
+    next_g1 = gather_steps(2, s.g1)
+
+    def attend_back(j):
+        next_g1(j)
+        r = slot_step(t, j)
+        rows = rows_of(r)
+        acc = dot_nt(s.g1[rows, 0:256], s.wo[0])
+        for k in range(1, 4):
+            acc = acc + dot_nt(s.g1[rows, 256 * k:256 * k + 256], s.wo[k])
+        grad_ctx = acc.astype(BF16)
+        s.gctxt[:, rows] = grad_ctx.T
+        product = grad_ctx.astype(F32) * s.ctx[rows, :].astype(F32)
+        parts = []
+        for h in range(4):
+            cols = slice(64 * h, 64 * h + 64)
+            prob = s.ps[h, rows, :]
+            delta = jnp.sum(product[:, cols], axis=-1, keepdims=True)
+            grad_prob = dot_nt(grad_ctx[:, cols], s.v[:, cols])
+            grad_score = (prob.astype(F32) * (grad_prob - delta)).astype(BF16)
+            parts.append(dot_nn(grad_score, s.ks[:, cols]))
+            s.dkt[cols, :] += dot_nn(s.qt[cols, rows], grad_score)
+            s.dvt[cols, :] += dot_nn(s.gctxt[cols, rows], prob)
+        grad_query = jnp.concatenate(parts, axis=1)
+        for k in range(4):
+            @pl.when(t == k)
+            def _():
+                s.sums[0, 6:7, 256 * k:256 * k + 256] += jnp.sum(grad_query, axis=0, keepdims=True)
+        s.dq[rows, :] = grad_query.astype(BF16)
+    loop(SLOTS, attend_back)
+
+    grad_second("i")
+
+    def turn_back(r):
+        rows = rows_of(r)
+        s.dk[rows, :] = s.dkt[:, rows].T.astype(BF16)
+        grad_value = s.dvt[:, rows].T
+        for k in range(4):
+            @pl.when(t == k)
+            def _():
+                s.sums[0, 7:8, 256 * k:256 * k + 256] += jnp.sum(grad_value, axis=0, keepdims=True)
+        s.dv[rows, :] = grad_value.astype(BF16)
+    loop(SLOTS, turn_back)
+    for k in range(4):
+        @pl.when(t == k)
+        def _():
+            s.sums[0, 8 + k:9 + k, :] = s.gb_in[...]
+
+    sums_s, sums_r = take("s", 5), take("r", 5)
+    sums_to = [partner, x_near, y_near, pair, across]
+
+    def sums_start(k):
+        send(s.sums.at[k], s.sums_got.at[k], sums_to[k], sums_s + k, sums_r + k)
+
+    def sums_finish(k):
+        got(s.sums_got.at[k], sums_r + k)
+        total = s.sums[k] + s.sums_got[k]
+        if k == 4:
+            o.sums[...] = total
+        else:
+            s.sums[k + 1] = total
+
+    sums_start(0)
+
+    def tok_part(r, dst, add):
+        rows = rows_of(r)
+
+        def body(n):
+            acc = dot_nt(s.dq[rows, :], s.w3[cols_of(n), :])
+            acc = acc + dot_nt(s.dk[rows, :], s.w3[pl.ds(pl.multiple_of(WIDTH + n * 256, 256), 256), :])
+            acc = acc + dot_nt(s.dv[rows, :], s.w3[pl.ds(pl.multiple_of(2 * WIDTH + n * 256, 256), 256), :])
+            put_part(dst, add, n, acc)
+        loop(4, body)
+    scatter(3, tok_part)
+    sums_finish(0)
+    sums_start(1)
+
+    def grad_head(m, src):
+        def body(n):
+            part = cols_of(n)
+            dst = pl.ds(pl.multiple_of(m * WIDTH + n * 256, 256), 256)
+            s.g3[dst, :] = dot_nn(s.tkt[part, :], src[...]).astype(BF16)
+        loop(4, body)
+
+    def grad_o(n):
+        s.go[n] = dot_nn(s.ctxt[...], s.g1[:, cols_of(n)]).astype(BF16)
+    loop(4, grad_o)
+    grad_first("o")
+    sums_finish(1)
+    sums_start(2)
+    grad_head(0, s.dq)
+    grad_first("q")
+    grad_head(1, s.dk)
+    grad_first("k")
+    grad_head(2, s.dv)
+    grad_first("v")
+    sums_finish(2)
+    sums_start(3)
+    grad_third("b")
+    grad_third("i")
+    scatter_wait(3)
+
+    def last_rows(i):
+        ch = own_chunk(i)
+        s.gtok_own[ch, :] = (s.g1f[ch, :] + scatter_rows(3, ch)).astype(BF16)
+    loop(BLOCK // CH, last_rows)
+    gtok_s, gtok_r = take("s"), take("r")
+    send_or_keep(s.gtok_own, s.gtok_got, dev(b, zh, t), home_self, gtok_s, gtok_r)
+    sums_finish(3)
+    sums_start(4)
+    for name in "oqkv":
+        grad_second(name)
+    grad_final("b")
+    grad_final("i")
+    got(s.gtok_got, gtok_r)
+
+    def widen_rows(i):
+        ch = own_chunk(i)
+        o.gtok[ch, :] = s.gtok_got[ch, :].astype(F32)
+    loop(BLOCK // CH, widen_rows)
+    sums_finish(4)
+    for name in "oqkv":
+        grad_third(name)
+    for name in "oqkv":
+        grad_final(name)
+    got(o.out, out_r)
+
+    for copy, skipped in to_drain:
+        if skipped is None:
+            copy.wait_send()
+        else:
+            @pl.when(jnp.logical_not(skipped))
+            def _():
+                copy.wait_send()
+
+
+def on_device_fused(tokens, lengths, w_query, b_query, w_key, w_value, b_value, w_out, b_out, gain_attn, shift_attn,
+                    w_in, b_in, w_back, b_back, gain_ffn, shift_ffn, cotangent):
+    row = lambda vec: vec.reshape(1, -1)
+    operands = (tokens, lengths, w_query, row(b_query), w_key, w_value, row(b_value), w_out, row(b_out),
+                row(gain_attn), row(shift_attn), w_in, row(b_in), w_back, row(b_back), row(gain_ffn),
+                row(shift_ffn), cotangent)
+    vmem = pl.BlockSpec(memory_space=pltpu.VMEM)
+    in_specs = [vmem] * len(operands)
+    in_specs[1] = pl.BlockSpec(memory_space=pltpu.SMEM)
+    shape = lambda dims, dtype: jax.ShapeDtypeStruct(dims, dtype)
+    out_shape = (
+        shape(tokens.shape, BF16), shape(tokens.shape, F32), shape(w_query.shape, F32), shape(w_key.shape, F32),
+        shape(w_value.shape, F32), shape(w_out.shape, F32), shape(w_in.shape, F32), shape(w_back.shape, F32),
+        shape((16, WIDTH), F32))
+    out, gtok, gq, gk, gv, go, gi, gb, sums = pl.pallas_call(
+        layer_kernel,
+        out_shape=out_shape,
+        in_specs=in_specs,
+        out_specs=(vmem,) * len(out_shape),
+        scratch_shapes=jax.tree.leaves(scratch_table()),
+        compiler_params=pltpu.CompilerParams(collective_id=0, has_side_effects=True, vmem_limit_bytes=64 * 1024 * 1000),
+        name="layer",
+    )(*operands)
+    return (out, gtok, gq, sums[6], gk, gv, sums[7], go, sums[0], sums[1], sums[2], gi, sums[8:12].reshape(-1), gb,
+            sums[3], sums[4], sums[5])
+
+
+def fits_fused(mesh):
+    return dict(mesh.shape) == {"dp": 8, "tensor": 4}
+
+
 def solution(mesh):
     placed = (
         P(("dp", "tensor"), None),
@@ -371,6 +1201,7 @@
         P(),
         P(("dp", "tensor"), None),
     )
+    on_device = on_device_fused if fits_fused(mesh) else on_device_plain
     return jax.shard_map(
         on_device,
         mesh=mesh,

time: 600 us -> 224 us (0.37)
  waiting for transfers between devices: 409 us -> 0 us
  Pallas kernels: 0 us -> 212 us
  blocking collectives: 82 us -> 0 us
  matrix products: 48.7 us -> 0 us
  other arithmetic: 21.4 us -> 0 us
  between operations: 17.3 us -> 0.69 us
  local copies, waits for them, and re-layouts: 17.9 us -> 10.9 us
    reduce_scatter x10 -> x0, waiting for transfers between devices: 302 us -> none  [the longest x1 55.1 us: on_device(): lax.psum_scatter(grad_w_back, 'dp', scatter_dimension=1, tiled=True)]
    pallas_call x0 -> x1, Pallas kernels: none -> 212 us  [on_device_fused(): pl.pallas_call(layer_kernel, out_shape=out_shape, in_specs=in_specs, out_...]
    all_gather x6 -> x0, waiting for transfers between devices: 105 us -> none  [the longest x1 26.7 us: on_device(): hidden_full = lax.all_gather(hidden_bf, 'tensor', axis=0, tiled=True)]
    dot_general x32 -> x0, matrix products: 48.7 us -> none  [the longest x6 15 us: matmul_over_rows(): lax.dot_general(left_side, right_side, (((0,), (0,)), ((), ())), preferre...]
    psum x1 -> x0, blocking collectives: 41.3 us -> none  [on_device(): lax.psum((widen(grad_b_query_part, b_query.shape[0]), widen(grad_b_value_...]
    all_gather x4 -> x0, blocking collectives: 40.8 us -> none  [the longest x1 11.5 us: on_device(): lax.all_gather(w_value, 'dp', axis=0, tiled=True)]
    reduce_sum x13 -> x0, other arithmetic: 11.7 us -> none  [the longest x2 2.39 us: layer_norm(): mean_val = jnp.mean(residual, axis=-1, keepdims=True)]
  transfers between devices with their start and end apart: 16 -> 0, of which waited for: 13 -> 0; matrix products, arithmetic and copies ran while one was open for 6% -> 0% of each run, Pallas kernels for 0% -> 0%
where the time goes in v1:
time: 224 us
  Pallas kernels  212 us (95%)
  local copies, waits for them, and re-layouts  10.9 us (5%)
    pallas_call x1, Pallas kernels, on_device_fused(): pl.pallas_call(layer_kernel, out_shape=out_shape, in_specs=in_specs, out_...  212 us
    unnamed x24, local copies, waits for them, and re-layouts  9.04 us

profile of v1, /device:TPU:1, one launch (start us, length us, event | category | flops | bytes accessed | tf_op | source)
XLA Modules:
  0.0 224.0 jit_solution(11238471991423527015)
XLA Ops:
  0.7 212.4 %layer.1 = (bf16[128,1024]{1,0:T(8,128)(2,1)}, f32[128,1024]{1,0:T(8,128)}, f32[128,256]{1,0:T(8,128)}, f32[128,256]{1,0:T(8,128)}, f32[128,256]{1,0:T(8,128)}, ...) custom-call(bf16[128,1024]{1,0:T(8,128)(2,1)} %tok.1, s32[1,2]{1,0:T(1,128)} %lens.1, ...), custom_call_target="tpu_custom_call" | custom-call | tf_op jit(solution)/shard_map/layer/pallas_call | solution.py:1166
  213.1 0.0 copy-start.2
  213.1 0.8 slice_bitcast_fusion
  213.9 1.9 fusion
  215.8 0.6 copy.37
  216.4 1.7 copy.46
  218.0 0.0 copy-done.2
  218.0 0.0 copy-start.6
  218.1 0.0 copy-start.5
  218.1 0.0 copy-start.4
  218.1 0.8 copy.47
  218.9 0.2 copy-done.6
  219.0 0.0 copy-start.1
  219.1 0.7 copy.48
  219.7 0.0 copy-done.5
  219.7 0.7 copy.49
  220.4 0.0 copy-done.4
  220.4 0.7 copy.50
  221.0 0.3 copy-done.3
  221.3 0.7 copy.51
  222.0 0.0 copy-done.1
  222.0 0.8 copy.52
  222.8 0.4 copy-done
  223.2 0.8 copy.53
  (2 shorter events, 0.0 us)
Async XLA Ops:
  213.1 5.0 %copy-start.2 = (f32[128,1024]{1,0:T(8,128)S(1)}, f32[128,1024]{1,0:T(8,128)}, u32[]{:S(2)}) copy-start(f32[128,1024]{1,0:T(8,128)} %get-tuple-element.61) | copy-start | bytes 1572868
  218.0 1.0 copy-start.6
  218.1 1.7 copy-start.5
  218.1 2.3 %copy-start.4 = (f32[128,256]{1,0:T(8,128)S(1)}, f32[128,256]{1,0:T(8,128)}, u32[]{:S(2)}) copy-start(f32[128,256]{1,0:T(8,128)} %get-tuple-element.65) | copy-start | bytes 393220
  219.0 2.9 %copy-start.1 = (f32[128,1024]{1,0:T(8,128)S(1)}, f32[128,1024]{1,0:T(8,128)}, u32[]{:S(2)}) copy-start(f32[128,1024]{1,0:T(8,128)} %get-tuple-element.71) | copy-start | bytes 1572868
  220.4 1.0 copy-start.3
  222.0 1.2 copy-start

commit v2 on v1

--- a/solution.py
+++ b/solution.py
@@ -364,9 +364,12 @@
 WIDTH = 1024
 HEAD_COLS = 256
 HIDDEN = 1024
-N_SEM = 176
-HALVES = dict(q=(128, 256), k=(128, 256), v=(128, 256), o=(256, 128), i=(128, 1024), b=(1024, 128))
-STAGES = ("xa", "ya", "s2", "r2", "zs", "zr")
+N_SEND = 58
+N_GOT = 110
+HALF = BLOCK // 2
+HALVES = dict(q=(128, 256), k=(128, 256), v=(128, 256), o=(256, 128), i0=(128, 512), i1=(128, 512), b0=(512, 128),
+              b1=(512, 128))
+VECTORS = dict(bq=1024, bv=1024, bo=1024, ga=1024, sa=1024, bi=4096, bb=1024, gf=1024, sf=1024)
 
 
 def flip(bit):
@@ -404,6 +407,10 @@
         wo=pltpu.VMEM((4, HEAD_COLS, 256), BF16),
         wi=pltpu.VMEM((WIDTH, HIDDEN), BF16),
         wb=pltpu.VMEM((4, HIDDEN, 256), BF16),
+        w3t=pltpu.VMEM((3, HEAD_COLS, WIDTH), BF16),
+        wot=pltpu.VMEM((WIDTH, HEAD_COLS), BF16),
+        wit=pltpu.VMEM((HIDDEN, WIDTH), BF16),
+        wbt=pltpu.VMEM((WIDTH, HIDDEN), BF16),
         lens_own=pltpu.VMEM((2, 8, 128), F32),
         lens_got=pltpu.VMEM((2, 8, 128), F32),
         lens_use=pltpu.VMEM((2, 8, 128), F32),
@@ -440,33 +447,35 @@
         g1f=pltpu.VMEM((BLOCK, WIDTH), F32),
         out_own=pltpu.VMEM((BLOCK, WIDTH), BF16),
         gtok_own=pltpu.VMEM((BLOCK, WIDTH), BF16),
-        gtok_got=pltpu.VMEM((BLOCK, WIDTH), BF16),
         rs_own=pltpu.VMEM((4, BLOCK, WIDTH), BF16),
         rs_out=pltpu.VMEM((4, 3, BLOCK, WIDTH), BF16),
         rs_got=pltpu.VMEM((4, 3, BLOCK, WIDTH), BF16),
         sums=pltpu.VMEM((6, 16, WIDTH), F32),
         sums_got=pltpu.VMEM((5, 16, WIDTH), F32),
         gb_in=pltpu.VMEM((1, HIDDEN), F32),
+        vectors={name: pltpu.VMEM((1, width), F32) for name, width in VECTORS.items()},
+        vsem=pltpu.SemaphoreType.DMA((len(VECTORS),)),
         g3=pltpu.VMEM((3 * WIDTH, HEAD_COLS), BF16),
         go=pltpu.VMEM((4, HEAD_COLS, 256), BF16),
         gi=pltpu.VMEM((WIDTH, HIDDEN), BF16),
         gb=pltpu.VMEM((4, HIDDEN, 256), BF16),
         stage={},
-        ssem=pltpu.SemaphoreType.DMA((N_SEM,)),
-        rsem=pltpu.SemaphoreType.DMA((N_SEM,)),
+        ssem=pltpu.SemaphoreType.DMA((N_SEND,)),
+        rsem=pltpu.SemaphoreType.DMA((N_GOT,)),
     )
     for name, dims in HALVES.items():
-        table["stage"][name] = {part: pltpu.VMEM((2,) + dims, BF16) for part in STAGES}
+        table["stage"][name] = pltpu.VMEM((10,) + dims, BF16)
     return table
 
 
-def layer_kernel(tok, lens, wq, bq, wk, wv, bv, wo, bo, ga, sa, wi, bi, wb, bb, gf, sf, cot, out, gtok, gq, gk, gv, go, gi,
-                 gb, sums, *scratch):
+def layer_kernel(tok, lens, wq, bq, wk, wv, bv, wo, bo, ga, sa, wi, bi, wb, bb, gf, sf, cot, out, gtok, sums, zq, zk, zv,
+                 zo, zi0, zi1, zb0, zb1, *scratch):
     a = SimpleNamespace(tok=tok, lens=lens, wq=wq, bq=bq, wk=wk, wv=wv, bv=bv, wo=wo, bo=bo, ga=ga, sa=sa, wi=wi, bi=bi,
                         wb=wb, bb=bb, gf=gf, sf=sf, cot=cot)
-    o = SimpleNamespace(out=out, gtok=gtok, gq=gq, gk=gk, gv=gv, go=go, gi=gi, gb=gb, sums=sums)
+    o = SimpleNamespace(out=out, gtok=gtok, sums=sums)
+    landed = dict(q=zq, k=zk, v=zv, o=zo, i0=zi0, i1=zi1, b0=zb0, b1=zb1)
     s = SimpleNamespace(**jax.tree.unflatten(jax.tree.structure(scratch_table()), scratch))
-    ssem, rsem = s.ssem, s.rsem
+    ssem, rsem, vsem, vectors = s.ssem, s.rsem, s.vsem, s.vectors
 
     dp = lax.axis_index("dp")
     z = lax.axis_index("tensor")
@@ -494,26 +503,30 @@
     def take(kind, count=1):
         first = taken[kind]
         taken[kind] = first + count
-        assert taken[kind] <= N_SEM
+        assert taken[kind] <= (N_SEND if kind == "s" else N_GOT)
         return first
 
     to_drain = []
 
-    def send(src, dst, device, sk, rk, cond=None):
-        copy = pltpu.make_async_remote_copy(
+    def make_copy(src, dst, device, sk, rk):
+        return pltpu.make_async_remote_copy(
             src_ref=src, dst_ref=dst, send_sem=ssem.at[sk], recv_sem=rsem.at[rk], device_id=device,
             device_id_type=MESH_ID)
-        copy.start()
-        if cond is None:
-            to_drain.append((copy, None))
+
+    def send(src, dst, device, sk, rk):
+        make_copy(src, dst, device, sk, rk).start()
 
     def got(dst, rk):
         pltpu.make_async_copy(dst, dst, rsem.at[rk]).wait()
 
+    def left(size_of, sk):
+        pltpu.make_async_copy(size_of, size_of, ssem.at[sk]).wait()
+
+    def at_end(size_of, sk, skipped=None, instead=None):
+        to_drain.append((size_of, sk, skipped, instead))
+
     def send_or_keep(src, dst, device, is_self, sk, rk):
-        copy = pltpu.make_async_remote_copy(
-            src_ref=src, dst_ref=dst, send_sem=ssem.at[sk], recv_sem=rsem.at[rk], device_id=device,
-            device_id_type=MESH_ID)
+        copy = make_copy(src, dst, device, sk, rk)
 
         @pl.when(is_self)
         def _():
@@ -522,8 +535,6 @@
         @pl.when(jnp.logical_not(is_self))
         def _():
             copy.start()
-
-        to_drain.append((copy, is_self))
 
     barrier = pltpu.get_barrier_semaphore()
     peers = [x_near, y_near]
@@ -567,41 +578,42 @@
 
     pieces = dict(q=piece_qkv(0, a.wq), k=piece_qkv(1, a.wk), v=piece_qkv(2, a.wv), o=piece_o,
                   i0=piece_in(0), i1=piece_in(1), b0=piece_back(0), b1=piece_back(1))
-    for piece in pieces.values():
-        piece.s1 = take("s", 2)
-        piece.r1 = take("r", 2)
-        piece.s2 = take("s", 4)
-        piece.r2 = take("r", 4)
+    first_size = dict(
+        q=s.w3.at[0:768, :], k=s.w3.at[0:768, :], v=s.w3.at[0:768, :], o=s.wo.at[0:3], i0=s.wi.at[0:768, 0:512],
+        i1=s.wi.at[0:768, 0:512], b0=s.wb.at[0:3, 0:512, :], b1=s.wb.at[0:3, 0:512, :])
+    for name, piece in pieces.items():
+        piece.s1, piece.r1 = take("s"), take("r")
+        piece.s2, piece.r2 = take("s"), take("r", 3)
+        keeps_one = jnp.logical_or(jnp.logical_and(z == 0, c == 0), jnp.logical_and(z == 3, c == 1))
+        at_end(piece.block(b), piece.s1, keeps_one, piece.own(b, 0))
+        at_end(first_size[name], piece.s2)
 
     def from_home(name):
         piece = pieces[name]
         for far in range(2):
             zt, ct = z // 2 + 2 * far, z % 2
             is_self = jnp.logical_and(zt == z, ct == c)
-            send_or_keep(piece.home, piece.own(b, c), dev(b, ct, zt), is_self, piece.s1 + far,
-                         piece.r1 + c)
+            send_or_keep(piece.home, piece.own(b, c), dev(b, ct, zt), is_self, piece.s1, piece.r1)
 
     def over_plane(name):
         piece = pieces[name]
-        for cc in range(2):
-            got(piece.own(b, cc), piece.r1 + cc)
+        got(piece.block(b), piece.r1)
         send(piece.block(b), piece.block(b), x_near, piece.s2, piece.r2)
-        send(piece.block(b), piece.block(b), y_near, piece.s2 + 1, piece.r2 + 1)
+        send(piece.block(b), piece.block(b), y_near, piece.s2, piece.r2 + 1)
 
     def relay(name):
         piece = pieces[name]
         got(piece.block(bx), piece.r2)
-        send(piece.half(bx, 0), piece.half(bx, 0), y_near, piece.s2 + 2, piece.r2 + 2)
+        send(piece.half(bx, 0), piece.half(bx, 0), y_near, piece.s2, piece.r2 + 2)
         got(piece.block(by), piece.r2 + 1)
-        send(piece.half(by, 1), piece.half(by, 1), x_near, piece.s2 + 3, piece.r2 + 3)
+        send(piece.half(by, 1), piece.half(by, 1), x_near, piece.s2, piece.r2 + 2)
 
     def arrived(name):
         piece = pieces[name]
-        got(piece.half(bd, 0), piece.r2 + 2)
-        got(piece.half(bd, 1), piece.r2 + 3)
+        got(piece.block(bd), piece.r2 + 2)
 
     tok_s, tok_r = take("s", 2), take("r", 4)
-    fwd_s = take("s", 4)
+    fwd_s = take("s", 6)
     lens_s, lens_r = take("s"), take("r")
     cot_s, cot_r = take("s"), take("r")
 
@@ -610,6 +622,7 @@
         s.lens_own[0] = jnp.full((8, 128), first, F32)
         s.lens_own[1] = jnp.full((8, 128), first + a.lens[0, 1].astype(F32), F32)
         send(s.lens_own, s.lens_got, partner, lens_s, lens_r)
+        at_end(s.lens_own, lens_s)
 
     def take_lens():
         got(s.lens_got, lens_r)
@@ -625,88 +638,131 @@
     def tok_block(r):
         return s.tk.at[rows_of(r), :]
 
+    inner, outer = 1 + c, 3 * c
+    is_relay = jnp.logical_and(c == zh, z == inner)
+    is_inner = jnp.logical_and(z >= 1, z <= 2)
+
     def send_tokens():
-        for j in range(2):
-            zt = 2 * c + j
-            send_or_keep(a.tok, tok_block(z), dev(b, c, zt), zt == z, tok_s + j, tok_r + z)
-
-    def share_tokens():
-        for r in range(SLOTS):
-            got(tok_block(r), tok_r + r)
-            copy = pltpu.make_async_remote_copy(
-                src_ref=tok_block(r), dst_ref=tok_block(r), send_sem=ssem.at[fwd_s + r], recv_sem=rsem.at[tok_r + r],
-                device_id=partner, device_id_type=MESH_ID)
+        near = z // 2 == c
+        first = jnp.where(near, 2 * c, inner)
+        send_or_keep(a.tok, tok_block(z), dev(b, c, first), first == z, tok_s, tok_r + z)
+        at_end(tok_block(z), tok_s, first == z)
+        second = make_copy(a.tok, tok_block(z), dev(b, c, 2 * c + 1), tok_s + 1, tok_r + z)
+        keep = jnp.logical_and(near, z == 2 * c + 1)
+        go = jnp.logical_and(near, z != 2 * c + 1)
+
+        @pl.when(keep)
+        def _():
+            pltpu.make_async_copy(a.tok, tok_block(z), rsem.at[tok_r + z]).start()
+
+        @pl.when(go)
+        def _():
+            second.start()
+
+        at_end(tok_block(z), tok_s + 1, jnp.logical_not(go))
+
+    def pass_on(half, far):
+        for k in range(2):
+            r = half * 2 + k
+            block = tok_block(r)
+            got(block, tok_r + r)
+            if far:
+                on = make_copy(block, block, dev(b, c, outer), fwd_s + k, tok_r + r)
+
+                @pl.when(is_relay)
+                def _():
+                    on.start()
+            copy = make_copy(block, block, partner, fwd_s + 2 + 2 * far + k, tok_r + r)
 
             @pl.when(c == zh)
             def _():
                 copy.start()
 
-            to_drain.append((copy, c != zh))
+    for k in range(6):
+        at_end(s.tk.at[0:BLOCK, :], fwd_s + k, jnp.logical_not(is_relay) if k < 2 else c != zh)
 
     def send_cotangent():
         zt, ct = 2 * c + z // 2, z % 2
         is_self = jnp.logical_and(zt == z, ct == c)
         send_or_keep(a.cot, s.cot_own, dev(b, ct, zt), is_self, cot_s, cot_r)
-
-    gather_s = [take("s", 3) for _ in range(3)]
-    gather_r = [take("r", 3) for _ in range(3)]
-    scatter_s = [take("s", 3) for _ in range(4)]
-    scatter_r = [take("r", 3) for _ in range(4)]
+        at_end(s.cot_own, cot_s, is_self)
+
+    gather_s, gather_r = take("s", 3), take("r", 12)
+    scatter_s, scatter_r = take("s", 4), take("r", 20)
+    for k in range(3):
+        at_end(s.tk.at[0:3 * BLOCK, :], gather_s + k)
+    for k in range(4):
+        at_end(s.tk.at[0:3 * BLOCK, :], scatter_s + k)
 
     def block_at(full, r):
         return full.at[rows_of(r), :]
 
-    def gather_start(which, full):
-        send(block_at(full, t), block_at(full, t), pair, gather_s[which], gather_r[which] + 1)
-        send(block_at(full, t), block_at(full, t), partner, gather_s[which] + 1, gather_r[which])
-
-    def gather_steps(which, full):
-        forward = pltpu.make_async_remote_copy(
-            src_ref=block_at(full, t2), dst_ref=block_at(full, t2), send_sem=ssem.at[gather_s[which] + 2],
-            recv_sem=rsem.at[gather_r[which] + 2], device_id=partner, device_id_type=MESH_ID)
-        to_drain.append((forward, None))
-
-        def step(j):
-            @pl.when(j == 1)
-            def _():
-                got(block_at(full, t1), gather_r[which])
-
-            @pl.when(j == 2)
-            def _():
-                got(block_at(full, t2), gather_r[which] + 1)
-                forward.start()
-
-            @pl.when(j == 3)
-            def _():
-                got(block_at(full, t3), gather_r[which] + 2)
-
-        return step
+    def half_at(full, r, k):
+        return full.at[pl.ds(pl.multiple_of(r * BLOCK + k * HALF, HALF), HALF), :]
+
+    def gather_start(which, full, k):
+        mine = half_at(full, t, k)
+        send(mine, mine, pair, gather_s + which, gather_r + 4 * which + 1 + k)
+        send(mine, mine, partner, gather_s + which, gather_r + 4 * which)
+
+    def gather_step(which, full, j):
+        base = gather_r + 4 * which
+
+        @pl.when(j == 1)
+        def _():
+            got(block_at(full, t1), base)
+
+        @pl.when(j == 2)
+        def _():
+            for k in range(2):
+                near = half_at(full, t2, k)
+                got(near, base + 1 + k)
+                send(near, near, partner, gather_s + which, base + 3)
+
+        @pl.when(j == 3)
+        def _():
+            got(block_at(full, t3), base + 3)
+
+    halves = [pl.ds(k * HALF, HALF) for k in range(2)]
 
     def scatter(which, part):
         out, back = s.rs_out, s.rs_got
-        ss, rr = scatter_s[which], scatter_r[which]
-        part(t3, out.at[which, 0], None)
-        send(out.at[which, 0], back.at[which, 0], partner, ss, rr)
-        part(t1, out.at[which, 2], None)
-        send(out.at[which, 2], back.at[which, 2], partner, ss + 2, rr + 2)
-        got(back.at[which, 0], rr)
-        part(t2, out.at[which, 1], back.at[which, 0])
-        send(out.at[which, 1], back.at[which, 1], pair, ss + 1, rr + 1)
-        part(t, s.rs_own.at[which], None)
-
-    def scatter_wait(which):
-        got(s.rs_got.at[which, 2], scatter_r[which] + 2)
-        got(s.rs_got.at[which, 1], scatter_r[which] + 1)
+        ss, rr = scatter_s + which, scatter_r + 5 * which
+        for k in range(2):
+            mine = out.at[which, 0, halves[k], :]
+            part(t3 * BLOCK + k * HALF, HALF, mine, None)
+            send(mine, back.at[which, 0, halves[k], :], partner, ss, rr + k)
+        for k in range(2):
+            mine, theirs = out.at[which, 1, halves[k], :], back.at[which, 0, halves[k], :]
+            got(theirs, rr + k)
+            part(t2 * BLOCK + k * HALF, HALF, mine, theirs)
+            send(mine, back.at[which, 1, halves[k], :], pair, ss, rr + 2 + k)
+        part(t1 * BLOCK, BLOCK, out.at[which, 2], None)
+        send(out.at[which, 2], back.at[which, 2], partner, ss, rr + 4)
+        part(t * BLOCK, BLOCK, s.rs_own.at[which], None)
+
+    def scatter_wait(which, k):
+        rr = scatter_r + 5 * which
+        if k == 0:
+            got(s.rs_got.at[which, 2], rr + 4)
+        got(s.rs_got.at[which, 1, halves[k], :], rr + 2 + k)
 
     def scatter_rows(which, chunk):
         total = s.rs_own[which, chunk, :].astype(F32) + s.rs_got[which, 2, chunk, :].astype(F32)
         return total + s.rs_got[which, 1, chunk, :].astype(F32)
 
+    def by_halves(which, body, after):
+        for k in range(2):
+            scatter_wait(which, k)
+            loop(2, lambda i: body(2 * k + i))
+            after(k)
+
     def put_part(dst, add, n, value):
+        cols = slice(256 * n, 256 * n + 256)
         value = value.astype(BF16)
         if add is not None:
-            value = (value.astype(F32) + add[:, cols_of(n)].astype(F32)).astype(BF16)
-        dst[:, cols_of(n)] = value
+            value = (value.astype(F32) + add[:, cols].astype(F32)).astype(BF16)
+        dst[:, cols] = value
 
     def loop(count, body):
         lax.fori_loop(0, count, lambda i, _: (body(i), 0)[1], 0)
@@ -715,97 +771,96 @@
         base = m * WIDTH
         return lambda bb, h: s.g3.at[pl.ds(pl.multiple_of(base + bb * 256 + h * 128, 128), 128), :]
 
+    def grad_in_part(k):
+        cols = pl.ds(k * 512, 512)
+        return lambda bb, h: s.gi.at[pl.ds(pl.multiple_of(bb * 256 + h * 128, 128), 128), cols]
+
+    def grad_back_part(k):
+        part = pl.ds(k * 512, 512)
+        return lambda bb, h: s.gb.at[bb, part, pl.ds(h * 128, 128)]
+
     grad_half = dict(
-        q=grad_qkv(0), k=grad_qkv(1), v=grad_qkv(2),
-        o=lambda bb, h: s.go.at[bb, :, pl.ds(h * 128, 128)],
-        i=lambda bb, h: s.gi.at[pl.ds(pl.multiple_of(bb * 256 + h * 128, 128), 128), :],
-        b=lambda bb, h: s.gb.at[bb, :, pl.ds(h * 128, 128)])
-    grad_out = dict(q=o.gq, k=o.gk, v=o.gv, o=o.go, i=o.gi, b=o.gb)
-    grad_chunk = dict(q=128, k=128, v=128, o=128, i=32, b=256)
-    grad_s = {name: take("s", 8) for name in grad_half}
-    grad_r = {name: take("r", 8) for name in grad_half}
-
-    def stage(name, *which):
-        return tuple(s.stage[name][STAGES[i]] for i in which)
+        q=grad_qkv(0), k=grad_qkv(1), v=grad_qkv(2), o=lambda bb, h: s.go.at[bb, :, pl.ds(h * 128, 128)],
+        i0=grad_in_part(0), i1=grad_in_part(1), b0=grad_back_part(0), b1=grad_back_part(1))
+    grad_s = {name: take("s", 2) for name in grad_half}
+    grad_r = {name: take("r", 4) for name in grad_half}
+    keeps_part = jnp.logical_or(jnp.logical_and(z == 0, c == 0), jnp.logical_and(z == 3, c == 1))
+    for name in grad_half:
+        at_end(s.stage[name].at[0:6], grad_s[name])
+        at_end(s.stage[name].at[0:2], grad_s[name] + 1, keeps_part, s.stage[name].at[0])
 
     def chunks(name, body):
-        size = grad_chunk[name]
+        size = 64 if name in ("i0", "i1") else 128
         count = HALVES[name][0] // size
         loop(count, lambda i: body(pl.ds(pl.multiple_of(i * size, size), size)))
 
     def grad_first(name):
-        half, ss, rr = grad_half[name], grad_s[name], grad_r[name]
-        xa, ya = stage(name, 0, 1)
-        send(half(bd, 0), xa.at[1], x_near, ss + 1, rr + 1)
-        send(half(bd, 1), ya.at[1], y_near, ss + 3, rr + 3)
-        send(half(bx, 0), xa.at[0], x_near, ss, rr)
-        send(half(by, 1), ya.at[0], y_near, ss + 2, rr + 2)
+        half, ss, rr, st = grad_half[name], grad_s[name], grad_r[name], s.stage[name]
+        send(half(bd, 0), st.at[1], x_near, ss, rr)
+        send(half(bd, 1), st.at[3], y_near, ss, rr + 1)
+        send(half(bx, 0), st.at[0], x_near, ss, rr + 2)
+        send(half(by, 1), st.at[2], y_near, ss, rr + 2)
 
     def grad_second(name):
-        half, ss, rr = grad_half[name], grad_s[name], grad_r[name]
-        xa, ya, s2, r2 = stage(name, 0, 1, 2, 3)
-        got(xa.at[1], rr + 1)
-        mine = half(by, 0)
-
-        def add_x(ch):
-            s2[0, ch, :] = (mine[ch, :].astype(F32) + xa[1, ch, :].astype(F32)).astype(BF16)
-        chunks(name, add_x)
-        send(s2.at[0], r2.at[0], y_near, ss + 4, rr + 4)
-        got(ya.at[1], rr + 3)
-        other = half(bx, 1)
-
-        def add_y(ch):
-            s2[1, ch, :] = (other[ch, :].astype(F32) + ya[1, ch, :].astype(F32)).astype(BF16)
-        chunks(name, add_y)
-        send(s2.at[1], r2.at[1], x_near, ss + 5, rr + 5)
+        half, ss, rr, st = grad_half[name], grad_s[name], grad_r[name], s.stage[name]
+        for h, block, to in ((0, by, y_near), (1, bx, x_near)):
+            got(st.at[1 + 2 * h], rr + h)
+            mine = half(block, h)
+
+            def add(ch):
+                st[4 + h, ch, :] = (mine[ch, :].astype(F32) + st[1 + 2 * h, ch, :].astype(F32)).astype(BF16)
+            chunks(name, add)
+            send(st.at[4 + h], st.at[6 + h], to, ss, rr + 2)
 
     def grad_third(name):
-        half, ss, rr = grad_half[name], grad_s[name], grad_r[name]
-        xa, ya, r2 = stage(name, 0, 1, 3)
-        zs, zr = stage(name, 4, 5)
-        for h, first in ((0, xa), (1, ya)):
-            got(first.at[0], rr + 2 * h)
-            got(r2.at[h], rr + 4 + h)
+        half, ss, rr, st = grad_half[name], grad_s[name], grad_r[name], s.stage[name]
+        zr = landed[name]
+        got(st.at[0:4], rr + 2)
+        for h in range(2):
             mine = half(b, h)
 
             def add_all(ch):
-                total = mine[ch, :].astype(F32) + first[0, ch, :].astype(F32) + r2[h, ch, :].astype(F32)
-                zs[h, ch, :] = total.astype(BF16)
+                total = mine[ch, :].astype(F32) + st[2 * h, ch, :].astype(F32) + st[6 + h, ch, :].astype(F32)
+                st[8 + h, ch, :] = total.astype(BF16)
             chunks(name, add_all)
             is_self = jnp.logical_and(c == h, z == t)
-            send_or_keep(zs.at[h], zr.at[zh], dev(b, h, t), is_self, ss + 6 + h, rr + 6 + zh)
+            send_or_keep(st.at[8 + h], zr.at[zh], dev(b, h, t), is_self, ss + 1, rr + 3)
 
     def grad_final(name):
-        rr, (zr,) = grad_r[name], stage(name, 5)
-        got(zr.at[0], rr + 6)
-        got(zr.at[1], rr + 7)
-
-        def add_both(ch):
-            grad_out[name][ch, :] = zr[0, ch, :].astype(F32) + zr[1, ch, :].astype(F32)
-        chunks(name, add_both)
-
+        got(landed[name], grad_r[name] + 3)
+
+    send_tokens()
+    send_lens()
+    for name, ref in vectors.items():
+        pltpu.make_async_copy(getattr(a, name), ref, vsem.at[list(vectors).index(name)]).start()
+    s.sums[0] = jnp.zeros((16, WIDTH), F32)
+    s.gb_in[...] = jnp.zeros((1, HIDDEN), F32)
+    s.dkt[...] = jnp.zeros((HEAD_COLS, GROUP), F32)
+    s.dvt[...] = jnp.zeros((HEAD_COLS, GROUP), F32)
+    pass_on(zh, 0)
     from_home("q")
     from_home("k")
     from_home("v")
-    send_lens()
-    send_tokens()
+
+    @pl.when(is_inner)
+    def _():
+        pass_on(flip(zh), 1)
+
+    over_plane("q")
     from_home("o")
     from_home("i0")
-    from_home("i1")
-    from_home("b0")
-    from_home("b1")
-    send_cotangent()
-    s.sums[0] = jnp.zeros((16, WIDTH), F32)
-    s.gb_in[...] = jnp.zeros((1, HIDDEN), F32)
-    over_plane("q")
     over_plane("k")
     over_plane("v")
-    relay("q")
-    relay("k")
-    relay("v")
-    share_tokens()
-    over_plane("o")
+    from_home("i1")
+
+    @pl.when(jnp.logical_not(is_inner))
+    def _():
+        pass_on(flip(zh), 1)
+
     take_lens()
+    for name, ref in vectors.items():
+        pltpu.make_async_copy(getattr(a, name), ref, vsem.at[list(vectors).index(name)]).wait()
+        setattr(a, name, ref)
 
     def make_bias(r):
         first, end = s.lens_use[0][0:1, 0:1], s.lens_use[1][0:1, 0:1]
@@ -814,6 +869,9 @@
         seg = lambda p: jnp.where(p >= end, 2.0, jnp.where(p >= first, 1.0, 0.0))
         s.bias[rows_of(r), :] = jnp.where(seg(row) == seg(col), 0.0, masked_value)
     loop(SLOTS, make_bias)
+    relay("q")
+    relay("k")
+    relay("v")
 
     def turn_tokens(r):
         s.tkt[:, rows_of(r)] = s.tk[rows_of(r), :].T
@@ -822,25 +880,26 @@
     head_cols = pl.ds(pl.multiple_of(t * HEAD_COLS, HEAD_COLS), HEAD_COLS)
 
     def project(m):
-        def body(r):
-            rows = rows_of(r)
-            acc = dot_nn(s.tk[rows, :], s.w3[pl.ds(m * WIDTH, WIDTH), :])
-            if m == 0:
-                acc = acc + a.bq[:, head_cols]
-                scaled = acc.astype(BF16).astype(F32) * 0.125
-                s.q[rows, :] = scaled.astype(BF16)
-                s.qt[:, rows] = scaled.astype(BF16).T
-            elif m == 1:
-                s.k[rows, :] = acc.astype(BF16)
-                s.ks[rows, :] = (acc.astype(BF16).astype(F32) * 0.125).astype(BF16)
-            else:
-                acc = acc + a.bv[:, head_cols]
-                s.v[rows, :] = acc.astype(BF16)
-        loop(SLOTS, body)
-
+        acc = dot_nn(s.tk[...], s.w3[m * WIDTH:(m + 1) * WIDTH, :])
+        if m == 0:
+            value = (acc + a.bq[:, head_cols]).astype(BF16)
+            scaled = (value.astype(F32) * 0.125).astype(BF16)
+            s.q[...] = scaled
+            s.qt[...] = scaled.T
+        elif m == 1:
+            value = acc.astype(BF16)
+            s.k[...] = value
+            s.ks[...] = (value.astype(F32) * 0.125).astype(BF16)
+        else:
+            s.v[...] = (acc + a.bv[:, head_cols]).astype(BF16)
+
+    from_home("b0")
+    over_plane("o")
+    over_plane("i0")
     for m, name in enumerate("qkv"):
         arrived(name)
         project(m)
+    from_home("b1")
     relay("o")
 
     def attend(r):
@@ -858,21 +917,25 @@
         context = jnp.concatenate(parts, axis=1).astype(BF16)
         s.ctx[rows, :] = context
         s.ctxt[:, rows] = context.T
-    loop(SLOTS, attend)
-
-    over_plane("i0")
+    loop(2, attend)
     over_plane("i1")
+    loop(2, lambda r: attend(r + 2))
+    relay("i0")
+    over_plane("b0")
     arrived("o")
 
-    def attn_part(r, dst, add):
-        rows = s.ctx[rows_of(r), :]
-        loop(4, lambda n: put_part(dst, add, n, dot_nn(rows, s.wo[n])))
+    def attn_part(first, count, dst, add):
+        rows = s.ctx[pl.ds(pl.multiple_of(first, HALF), count), :]
+        for n in range(4):
+            put_part(dst, add, n, dot_nn(rows, s.wo[n]))
     scatter(0, attn_part)
-    relay("i0")
     relay("i1")
-    over_plane("b0")
     over_plane("b1")
-    scatter_wait(0)
+    for m in range(3):
+        for n in range(4):
+            s.w3t[m, :, 256 * n:256 * n + 256] = s.w3[m * WIDTH + 256 * n:m * WIDTH + 256 * n + 256, :].T
+    for n in range(4):
+        s.wot[256 * n:256 * n + 256, :] = s.wo[n].T
 
     CH = 32
 
@@ -893,40 +956,52 @@
         s.inv1[ch, :] = jnp.broadcast_to(inv, (CH, 128))
         s.hid1[ch, :] = hidden
         s.hid[group_chunk(i), :] = hidden.astype(BF16)
-    loop(BLOCK // CH, norm_one)
-    gather_start(0, s.hid)
+    by_halves(0, norm_one, lambda k: gather_start(0, s.hid, k))
+    send_cotangent()
     arrived("i0")
     arrived("i1")
 
-    next_hid = gather_steps(0, s.hid)
-
     def ffn_in(j):
-        next_hid(j)
+        gather_step(0, s.hid, j)
         r = slot_step(t, j)
         rows = rows_of(r)
-
-        def body(n):
-            cols = cols_of(n)
+        for n in range(4):
+            cols = slice(256 * n, 256 * n + 256)
             bias = a.bi[:, pl.ds(pl.multiple_of(t * HIDDEN + n * 256, 256), 256)]
             pre = dot_nn(s.hid[rows, :], s.wi[:, cols]) + bias
             cdf = 0.5 * (1.0 + lax.erf(pre * 0.7071067811865476))
             pdf = jnp.exp(-0.5 * pre * pre) * 0.3989422804014327
             s.act[rows, cols] = (pre * cdf).astype(BF16)
             s.slope[rows, cols] = cdf + pre * pdf
-        loop(4, body)
+    loop(SLOTS, ffn_in)
+
+    def turn_ffn(r):
+        rows = rows_of(r)
         s.actt[:, rows] = s.act[rows, :].T
         s.hidt[:, rows] = s.hid[rows, :].T
-    loop(SLOTS, ffn_in)
     relay("b0")
+    loop(SLOTS, turn_ffn)
+
+    def turn_wi(r):
+        rows = rows_of(r)
+        s.wit[:, rows] = s.wi[rows, :].T
+    loop(8, turn_wi)
     relay("b1")
     arrived("b0")
     arrived("b1")
 
-    def ffn_part(r, dst, add):
-        loop(4, lambda n: put_part(dst, add, n, dot_nn(s.act[rows_of(r), :], s.wb[n])))
+    def ffn_part(first, count, dst, add):
+        rows = pl.ds(pl.multiple_of(first, HALF), count)
+        for n in range(4):
+            put_part(dst, add, n, dot_nn(s.act[rows, :], s.wb[n]))
     scatter(1, ffn_part)
+
+    def turn_wb(r):
+        rows = rows_of(r)
+        for n in range(4):
+            s.wbt[256 * n:256 * n + 256, rows] = s.wb[n, rows, :].T
+    loop(8, turn_wb)
     got(s.cot_own, cot_r)
-    scatter_wait(1)
 
     def add_rows(row, value):
         s.sums[0, row:row + 1, :] += jnp.sum(value, axis=0, keepdims=True)
@@ -950,50 +1025,54 @@
         add_rows(3, grad_two)
         s.g2f[ch, :] = grad_two
         s.g2[group_chunk(i), :] = grad_two.astype(BF16)
-    loop(BLOCK // CH, norm_two)
-    gather_start(1, s.g2)
+    by_halves(1, norm_two, lambda k: gather_start(1, s.g2, k))
     out_s, out_r = take("s"), take("r")
     home_self = jnp.logical_and(zh == c, t == z)
-    send_or_keep(s.out_own, o.out, dev(b, zh, t), home_self, out_s, out_r)
-
-    next_g2 = gather_steps(1, s.g2)
 
     def ffn_back(j):
-        next_g2(j)
+        gather_step(1, s.g2, j)
         r = slot_step(t, j)
         rows = rows_of(r)
-
-        def body(n):
-            cols = cols_of(n)
-            acc = dot_nt(s.g2[rows, 0:256], s.wb[0, cols, :])
-            for k in range(1, 4):
-                acc = acc + dot_nt(s.g2[rows, 256 * k:256 * k + 256], s.wb[k, cols, :])
-            grad = acc * s.slope[rows, cols]
+        for n in range(4):
+            cols = slice(256 * n, 256 * n + 256)
+            grad = dot_nn(s.g2[rows, :], s.wbt[:, cols]) * s.slope[rows, cols]
             s.gb_in[:, cols] += jnp.sum(grad, axis=0, keepdims=True)
             s.gpre[rows, cols] = grad.astype(BF16)
-        loop(4, body)
     loop(SLOTS, ffn_back)
-
-    def grad_back(n):
+    send_or_keep(s.out_own, o.out, dev(b, zh, t), home_self, out_s, out_r)
+    at_end(s.out_own, out_s, home_self)
+
+    def grad_back(k):
+        part = slice(512 * k, 512 * k + 512)
+
+        def body(n):
+            for e in range(2):
+                block = n * 2 + e
+                s.gb[block, part, :] = dot_nn(s.actt[part, :], s.g2[:, cols_of(block)]).astype(BF16)
+        loop(2, body)
+
+    def grad_in(k):
+        cols = slice(512 * k, 512 * k + 512)
+
         def body(m):
-            part = cols_of(m)
-            s.gb[n, part, :] = dot_nn(s.actt[part, :], s.g2[:, cols_of(n)]).astype(BF16)
-        loop(4, body)
-    loop(4, grad_back)
-    grad_first("b")
-
-    def in_part(r, dst, add):
-        loop(4, lambda n: put_part(dst, add, n, dot_nt(s.gpre[rows_of(r), :], s.wi[cols_of(n), :])))
+            part = rows_of(m * 4, 512)
+            s.gi[part, cols] = dot_nn(s.hidt[part, :], s.gpre[:, cols]).astype(BF16)
+        loop(2, body)
+
+    grad_back(0)
+    grad_first("b0")
+    grad_back(1)
+    grad_first("b1")
+
+    def in_part(first, count, dst, add):
+        rows = pl.ds(pl.multiple_of(first, HALF), count)
+        for n in range(4):
+            put_part(dst, add, n, dot_nn(s.gpre[rows, :], s.wit[:, 256 * n:256 * n + 256]))
     scatter(2, in_part)
-
-    def grad_in(n):
-        def body(m):
-            part = cols_of(m)
-            s.gi[part, cols_of(n)] = dot_nn(s.hidt[part, :], s.gpre[:, cols_of(n)]).astype(BF16)
-        loop(4, body)
-    loop(4, grad_in)
-    grad_first("i")
-    scatter_wait(2)
+    grad_in(0)
+    grad_in(1)
+    grad_second("b0")
+    grad_first("i0")
 
     def norm_one_back(i):
         ch = own_chunk(i)
@@ -1008,22 +1087,15 @@
         add_rows(0, grad_one)
         s.g1f[ch, :] = grad_one
         s.g1[group_chunk(i), :] = grad_one.astype(BF16)
-    loop(BLOCK // CH, norm_one_back)
-    gather_start(2, s.g1)
-    grad_second("b")
-    s.dkt[...] = jnp.zeros((HEAD_COLS, GROUP), F32)
-    s.dvt[...] = jnp.zeros((HEAD_COLS, GROUP), F32)
-
-    next_g1 = gather_steps(2, s.g1)
+    by_halves(2, norm_one_back, lambda k: gather_start(2, s.g1, k))
+    grad_second("b1")
+    grad_first("i1")
 
     def attend_back(j):
-        next_g1(j)
+        gather_step(2, s.g1, j)
         r = slot_step(t, j)
         rows = rows_of(r)
-        acc = dot_nt(s.g1[rows, 0:256], s.wo[0])
-        for k in range(1, 4):
-            acc = acc + dot_nt(s.g1[rows, 256 * k:256 * k + 256], s.wo[k])
-        grad_ctx = acc.astype(BF16)
+        grad_ctx = dot_nn(s.g1[rows, :], s.wot[...]).astype(BF16)
         s.gctxt[:, rows] = grad_ctx.T
         product = grad_ctx.astype(F32) * s.ctx[rows, :].astype(F32)
         parts = []
@@ -1042,9 +1114,11 @@
             def _():
                 s.sums[0, 6:7, 256 * k:256 * k + 256] += jnp.sum(grad_query, axis=0, keepdims=True)
         s.dq[rows, :] = grad_query.astype(BF16)
-    loop(SLOTS, attend_back)
-
-    grad_second("i")
+    loop(2, attend_back)
+    grad_third("b0")
+    loop(2, lambda j: attend_back(j + 2))
+    grad_second("i0")
+    grad_third("b1")
 
     def turn_back(r):
         rows = rows_of(r)
@@ -1062,10 +1136,11 @@
             s.sums[0, 8 + k:9 + k, :] = s.gb_in[...]
 
     sums_s, sums_r = take("s", 5), take("r", 5)
-    sums_to = [partner, x_near, y_near, pair, across]
+    sums_to = [partner, across, pair, x_near, y_near]
 
     def sums_start(k):
         send(s.sums.at[k], s.sums_got.at[k], sums_to[k], sums_s + k, sums_r + k)
+        at_end(s.sums.at[k], sums_s + k)
 
     def sums_finish(k):
         got(s.sums_got.at[k], sums_r + k)
@@ -1077,76 +1152,92 @@
 
     sums_start(0)
 
-    def tok_part(r, dst, add):
-        rows = rows_of(r)
-
-        def body(n):
-            acc = dot_nt(s.dq[rows, :], s.w3[cols_of(n), :])
-            acc = acc + dot_nt(s.dk[rows, :], s.w3[pl.ds(pl.multiple_of(WIDTH + n * 256, 256), 256), :])
-            acc = acc + dot_nt(s.dv[rows, :], s.w3[pl.ds(pl.multiple_of(2 * WIDTH + n * 256, 256), 256), :])
+    def tok_part(first, count, dst, add):
+        rows = pl.ds(pl.multiple_of(first, HALF), count)
+        for n in range(4):
+            cols = slice(256 * n, 256 * n + 256)
+            acc = dot_nn(s.dq[rows, :], s.w3t[0, :, cols])
+            acc = acc + dot_nn(s.dk[rows, :], s.w3t[1, :, cols])
+            acc = acc + dot_nn(s.dv[rows, :], s.w3t[2, :, cols])
             put_part(dst, add, n, acc)
-        loop(4, body)
     scatter(3, tok_part)
     sums_finish(0)
     sums_start(1)
 
     def grad_head(m, src):
-        def body(n):
-            part = cols_of(n)
-            dst = pl.ds(pl.multiple_of(m * WIDTH + n * 256, 256), 256)
-            s.g3[dst, :] = dot_nn(s.tkt[part, :], src[...]).astype(BF16)
-        loop(4, body)
-
-    def grad_o(n):
-        s.go[n] = dot_nn(s.ctxt[...], s.g1[:, cols_of(n)]).astype(BF16)
-    loop(4, grad_o)
+        s.g3[m * WIDTH:(m + 1) * WIDTH, :] = dot_nn(s.tkt[...], src[...]).astype(BF16)
+
+    for n in range(4):
+        s.go[n] = dot_nn(s.ctxt[...], s.g1[:, 256 * n:256 * n + 256]).astype(BF16)
+    grad_head(0, s.dq)
+    grad_head(1, s.dk)
+    grad_head(2, s.dv)
+    grad_second("i1")
     grad_first("o")
-    sums_finish(1)
-    sums_start(2)
-    grad_head(0, s.dq)
     grad_first("q")
-    grad_head(1, s.dk)
+    grad_third("i0")
+    grad_third("i1")
+    grad_second("o")
     grad_first("k")
-    grad_head(2, s.dv)
-    grad_first("v")
-    sums_finish(2)
-    sums_start(3)
-    grad_third("b")
-    grad_third("i")
-    scatter_wait(3)
 
     def last_rows(i):
         ch = own_chunk(i)
         s.gtok_own[ch, :] = (s.g1f[ch, :] + scatter_rows(3, ch)).astype(BF16)
-    loop(BLOCK // CH, last_rows)
+    by_halves(3, last_rows, lambda k: None)
     gtok_s, gtok_r = take("s"), take("r")
-    send_or_keep(s.gtok_own, s.gtok_got, dev(b, zh, t), home_self, gtok_s, gtok_r)
+    send_or_keep(s.gtok_own, o.gtok, dev(b, zh, t), home_self, gtok_s, gtok_r)
+    at_end(s.gtok_own, gtok_s, home_self)
+    grad_second("q")
+    grad_first("v")
+    grad_third("o")
+    sums_finish(1)
+    sums_start(2)
+    grad_second("k")
+    grad_third("q")
+    sums_finish(2)
+    sums_start(3)
+    grad_second("v")
+    grad_third("k")
+    grad_third("v")
     sums_finish(3)
     sums_start(4)
-    for name in "oqkv":
-        grad_second(name)
-    grad_final("b")
-    grad_final("i")
-    got(s.gtok_got, gtok_r)
-
-    def widen_rows(i):
-        ch = own_chunk(i)
-        o.gtok[ch, :] = s.gtok_got[ch, :].astype(F32)
-    loop(BLOCK // CH, widen_rows)
+    grad_final("b0")
+    grad_final("b1")
+    grad_final("i0")
+    grad_final("i1")
+    got(o.gtok, gtok_r)
+    got(o.out, out_r)
+    grad_final("o")
+    grad_final("q")
     sums_finish(4)
-    for name in "oqkv":
-        grad_third(name)
-    for name in "oqkv":
-        grad_final(name)
-    got(o.out, out_r)
-
-    for copy, skipped in to_drain:
+    grad_final("k")
+    grad_final("v")
+
+    for size_of, sk, skipped, instead in to_drain:
         if skipped is None:
-            copy.wait_send()
+            left(size_of, sk)
         else:
             @pl.when(jnp.logical_not(skipped))
             def _():
-                copy.wait_send()
+                left(size_of, sk)
+            if instead is not None:
+                @pl.when(skipped)
+                def _():
+                    left(instead, sk)
+
+
+def result_kernel(out, gtok, sums, zq, zk, zv, zo, zi0, zi1, zb0, zb1, o_out, o_gtok, o_gq, o_gbq, o_gk, o_gv, o_gbv, o_go,
+                  o_gbo, o_gga, o_gsa, o_gi, o_gbi, o_gb, o_gbb, o_ggf, o_gsf):
+    both = lambda ref: ref[0].astype(F32) + ref[1].astype(F32)
+    o_out[...] = out[...]
+    o_gtok[...] = gtok[...].astype(F32)
+    o_gq[...], o_gk[...], o_gv[...], o_go[...] = both(zq), both(zk), both(zv), both(zo)
+    o_gi[:, :512], o_gi[:, 512:] = both(zi0), both(zi1)
+    o_gb[:512, :], o_gb[512:, :] = both(zb0), both(zb1)
+    for row, ref in ((6, o_gbq), (7, o_gbv), (0, o_gbo), (1, o_gga), (2, o_gsa), (3, o_gbb), (4, o_ggf), (5, o_gsf)):
+        ref[...] = sums[row:row + 1, :]
+    for k in range(4):
+        o_gbi[:, WIDTH * k:WIDTH * k + WIDTH] = sums[8 + k:9 + k, :]
 
 
 def on_device_fused(tokens, lengths, w_query, b_query, w_key, w_value, b_value, w_out, b_out, gain_attn, shift_attn,
@@ -1156,24 +1247,34 @@
                 row(gain_attn), row(shift_attn), w_in, row(b_in), w_back, row(b_back), row(gain_ffn),
                 row(shift_ffn), cotangent)
     vmem = pl.BlockSpec(memory_space=pltpu.VMEM)
-    in_specs = [vmem] * len(operands)
+    stay = pl.BlockSpec(memory_space=pl.ANY)
+    in_specs = [stay] * len(operands)
     in_specs[1] = pl.BlockSpec(memory_space=pltpu.SMEM)
     shape = lambda dims, dtype: jax.ShapeDtypeStruct(dims, dtype)
-    out_shape = (
-        shape(tokens.shape, BF16), shape(tokens.shape, F32), shape(w_query.shape, F32), shape(w_key.shape, F32),
-        shape(w_value.shape, F32), shape(w_out.shape, F32), shape(w_in.shape, F32), shape(w_back.shape, F32),
-        shape((16, WIDTH), F32))
-    out, gtok, gq, gk, gv, go, gi, gb, sums = pl.pallas_call(
+    between = [shape(tokens.shape, BF16), shape(tokens.shape, BF16), shape((16, WIDTH), F32)]
+    between += [shape((2,) + HALVES[name], BF16) for name in ("q", "k", "v", "o", "i0", "i1", "b0", "b1")]
+    parts = pl.pallas_call(
         layer_kernel,
-        out_shape=out_shape,
+        out_shape=between,
         in_specs=in_specs,
-        out_specs=(vmem,) * len(out_shape),
+        out_specs=[stay, stay, vmem] + [stay] * 8,
         scratch_shapes=jax.tree.leaves(scratch_table()),
         compiler_params=pltpu.CompilerParams(collective_id=0, has_side_effects=True, vmem_limit_bytes=64 * 1024 * 1000),
         name="layer",
     )(*operands)
-    return (out, gtok, gq, sums[6], gk, gv, sums[7], go, sums[0], sums[1], sums[2], gi, sums[8:12].reshape(-1), gb,
-            sums[3], sums[4], sums[5])
+    line = shape((1, WIDTH), F32)
+    results = (
+        shape(tokens.shape, BF16), shape(tokens.shape, F32), shape(w_query.shape, F32), line, shape(w_key.shape, F32),
+        shape(w_value.shape, F32), line, shape(w_out.shape, F32), line, line, line, shape(w_in.shape, F32),
+        shape((1, b_in.shape[0]), F32), shape(w_back.shape, F32), line, line, line)
+    outs = pl.pallas_call(
+        result_kernel,
+        out_shape=results,
+        in_specs=[vmem] * len(between),
+        out_specs=[vmem] * len(results),
+        name="results",
+    )(*parts)
+    return tuple(v.reshape(-1) if v.shape[0] == 1 else v for v in outs)
 
 
 def fits_fused(mesh):

time: 224 us -> 169 us (0.75); the launches traced: 224 us -> 166 us
  Pallas kernels: 212 us -> 165 us
  local copies, waits for them, and re-layouts: 10.9 us -> 0 us
    pallas_call x1 -> x2, Pallas kernels: 212 us -> 165 us  [the longest x1 162 us: on_device_fused(): pl.pallas_call(layer_kernel, out_shape=between, in_specs=in_specs, out_sp...]
    unnamed x24 -> x0, local copies, waits for them, and re-layouts: 9.04 us -> none
where the time goes in v2:
time: 169 us; the launch traced here: 166 us
  Pallas kernels  165 us (98%)
    pallas_call x1, Pallas kernels, on_device_fused(): pl.pallas_call(layer_kernel, out_shape=between, in_specs=in_specs, out_sp...  162 us

profile of v2, /device:TPU:1, one launch (start us, length us, event | category | flops | bytes accessed | tf_op | source)
XLA Modules:
  0.0 166.0 jit_solution(7053170116932543141)
XLA Ops:
  0.7 162.1 %layer.1 = (bf16[128,1024]{1,0:T(8,128)(2,1)}, bf16[128,1024]{1,0:T(8,128)(2,1)}, f32[16,1024]{1,0:T(8,128)}, bf16[2,128,256]{2,1,0:T(8,128)(2,1)}, bf16[2,128,2...) custom-call(bf16[128,1024]{1,0:T(8,128)(2,1)} %tok.1, ...), custom_call_target="tpu_custom_call" | custom-call | tf_op jit(solution)/shard_map/layer/pallas_call | solution.py:1256
  162.8 3.0 %results.1 = (bf16[128,1024]{1,0:T(8,128)(2,1)}, f32[128,1024]{1,0:T(8,128)}, f32[128,256]{1,0:T(8,128)}, f32[1,1024]{1,0:T(1,128)}, f32[128,256]{1,0:T(8,128)},...) custom-call(bf16[128,1024]{1,0:T(8,128)(2,1)} %get-tuple-element.45., ...), custom_call_target="tpu_custom_call" | custom-call | tf_op jit(solution)/shard_map/results/pallas_call | solution.py:1270

commit v3 on v2

--- a/solution.py
+++ b/solution.py
@@ -455,6 +455,7 @@
         gb_in=pltpu.VMEM((1, HIDDEN), F32),
         vectors={name: pltpu.VMEM((1, width), F32) for name, width in VECTORS.items()},
         vsem=pltpu.SemaphoreType.DMA((len(VECTORS),)),
+        turn=pltpu.SemaphoreType.REGULAR((4,)),
         g3=pltpu.VMEM((3 * WIDTH, HEAD_COLS), BF16),
         go=pltpu.VMEM((4, HEAD_COLS, 256), BF16),
         gi=pltpu.VMEM((WIDTH, HIDDEN), BF16),
@@ -588,12 +589,18 @@
         at_end(piece.block(b), piece.s1, keeps_one, piece.own(b, 0))
         at_end(first_size[name], piece.s2)
 
+    def to_outer(name):
+        piece = pieces[name]
+        is_self = jnp.logical_and(z == 3 * zh, z % 2 == c)
+        send_or_keep(piece.home, piece.own(b, c), dev(b, z % 2, 3 * zh), is_self, piece.s1, piece.r1)
+
+    def to_inner(name):
+        piece = pieces[name]
+        send(piece.home, piece.own(b, c), dev(b, z % 2, 2 - zh), piece.s1, piece.r1)
+
     def from_home(name):
-        piece = pieces[name]
-        for far in range(2):
-            zt, ct = z // 2 + 2 * far, z % 2
-            is_self = jnp.logical_and(zt == z, ct == c)
-            send_or_keep(piece.home, piece.own(b, c), dev(b, ct, zt), is_self, piece.s1, piece.r1)
+        to_inner(name)
+        to_outer(name)
 
     def over_plane(name):
         piece = pieces[name]
@@ -741,6 +748,39 @@
         send(out.at[which, 2], back.at[which, 2], partner, ss, rr + 4)
         part(t * BLOCK, BLOCK, s.rs_own.at[which], None)
 
+    def scatter_cols(which, blocks, k):
+        out, back = s.rs_out, s.rs_got
+        ss, rr = scatter_s + which, scatter_r + 5 * which
+        slots = [pl.ds(pl.multiple_of(block * 256, 256), 256) for block in blocks]
+        size = s.rs_got.at[which, 0, :, 0:256 * len(blocks)]
+
+        def product(row, block):
+            rows = pl.ds(pl.multiple_of(row * BLOCK, BLOCK), BLOCK)
+            return dot_nn(s.act[rows, :], s.wb[block])
+
+        def cast(row, slot):
+            for block, cols in zip(blocks, slots):
+                out[which, slot, :, cols] = product(row, block).astype(BF16)
+
+        cast(t3, 0)
+        for cols in slots:
+            send(out.at[which, 0, :, cols], back.at[which, 0, :, cols], partner, ss, rr + k)
+        cast(t1, 2)
+        for cols in slots:
+            send(out.at[which, 2, :, cols], back.at[which, 2, :, cols], partner, ss, rr + 4)
+        got(size, rr + k)
+        for block, cols in zip(blocks, slots):
+            total = product(t2, block).astype(BF16).astype(F32) + back[which, 0, :, cols].astype(F32)
+            out[which, 1, :, cols] = total.astype(BF16)
+            send(out.at[which, 1, :, cols], back.at[which, 1, :, cols], pair, ss, rr + 2)
+        for block, cols in zip(blocks, slots):
+            s.rs_own[which, :, cols] = product(t, block).astype(BF16)
+
+    def scatter_cols_wait(which):
+        rr = scatter_r + 5 * which
+        got(s.rs_got.at[which, 2], rr + 4)
+        got(s.rs_got.at[which, 1], rr + 2)
+
     def scatter_wait(which, k):
         rr = scatter_r + 5 * which
         if k == 0:
@@ -752,8 +792,11 @@
         return total + s.rs_got[which, 1, chunk, :].astype(F32)
 
     def by_halves(which, body, after):
+        if which == 1:
+            scatter_cols_wait(which)
         for k in range(2):
-            scatter_wait(which, k)
+            if which != 1:
+                scatter_wait(which, k)
             loop(2, lambda i: body(2 * k + i))
             after(k)
 
@@ -794,10 +837,13 @@
         count = HALVES[name][0] // size
         loop(count, lambda i: body(pl.ds(pl.multiple_of(i * size, size), size)))
 
-    def grad_first(name):
+    def grad_first(name, part=2):
         half, ss, rr, st = grad_half[name], grad_s[name], grad_r[name], s.stage[name]
-        send(half(bd, 0), st.at[1], x_near, ss, rr)
-        send(half(bd, 1), st.at[3], y_near, ss, rr + 1)
+        if part in (0, 2):
+            send(half(bd, 0), st.at[1], x_near, ss, rr)
+            send(half(bd, 1), st.at[3], y_near, ss, rr + 1)
+        if part == 0:
+            return
         send(half(bx, 0), st.at[0], x_near, ss, rr + 2)
         send(half(by, 1), st.at[2], y_near, ss, rr + 2)
 
@@ -829,7 +875,12 @@
     def grad_final(name):
         got(landed[name], grad_r[name] + 3)
 
+    to_inner("q")
+    to_inner("k")
     send_tokens()
+    to_inner("v")
+    for name in "qkv":
+        to_outer(name)
     send_lens()
     for name, ref in vectors.items():
         pltpu.make_async_copy(getattr(a, name), ref, vsem.at[list(vectors).index(name)]).start()
@@ -837,30 +888,28 @@
     s.gb_in[...] = jnp.zeros((1, HIDDEN), F32)
     s.dkt[...] = jnp.zeros((HEAD_COLS, GROUP), F32)
     s.dvt[...] = jnp.zeros((HEAD_COLS, GROUP), F32)
+    def in_turn(k):
+        @pl.when(is_inner)
+        def _():
+            pl.semaphore_signal(s.turn.at[k], inc=1, device_id=pair, device_id_type=MESH_ID)
+
+        @pl.when(jnp.logical_not(is_inner))
+        def _():
+            pl.semaphore_wait(s.turn.at[k], 1)
+
+    over_plane("q")
+    over_plane("k")
+    relay("q")
     pass_on(zh, 0)
-    from_home("q")
-    from_home("k")
-    from_home("v")
+    to_inner("o")
 
     @pl.when(is_inner)
     def _():
         pass_on(flip(zh), 1)
 
-    over_plane("q")
-    from_home("o")
-    from_home("i0")
-    over_plane("k")
-    over_plane("v")
-    from_home("i1")
-
-    @pl.when(jnp.logical_not(is_inner))
-    def _():
-        pass_on(flip(zh), 1)
-
+    in_turn(0)
+    to_inner("i0")
     take_lens()
-    for name, ref in vectors.items():
-        pltpu.make_async_copy(getattr(a, name), ref, vsem.at[list(vectors).index(name)]).wait()
-        setattr(a, name, ref)
 
     def make_bias(r):
         first, end = s.lens_use[0][0:1, 0:1], s.lens_use[1][0:1, 0:1]
@@ -869,9 +918,30 @@
         seg = lambda p: jnp.where(p >= end, 2.0, jnp.where(p >= first, 1.0, 0.0))
         s.bias[rows_of(r), :] = jnp.where(seg(row) == seg(col), 0.0, masked_value)
     loop(SLOTS, make_bias)
-    relay("q")
+    for name, ref in vectors.items():
+        pltpu.make_async_copy(getattr(a, name), ref, vsem.at[list(vectors).index(name)]).wait()
+        setattr(a, name, ref)
     relay("k")
+    over_plane("v")
     relay("v")
+
+    @pl.when(is_inner)
+    def _():
+        over_plane("o")
+
+    @pl.when(jnp.logical_not(is_inner))
+    def _():
+        pass_on(flip(zh), 1)
+
+    in_turn(1)
+    to_outer("o")
+    to_outer("i0")
+    to_inner("i1")
+
+    @pl.when(jnp.logical_not(is_inner))
+    def _():
+        over_plane("o")
+
 
     def turn_tokens(r):
         s.tkt[:, rows_of(r)] = s.tk[rows_of(r), :].T
@@ -893,14 +963,16 @@
         else:
             s.v[...] = (acc + a.bv[:, head_cols]).astype(BF16)
 
-    from_home("b0")
-    over_plane("o")
+    arrived("q")
+    project(0)
+    arrived("k")
+    project(1)
     over_plane("i0")
-    for m, name in enumerate("qkv"):
-        arrived(name)
-        project(m)
-    from_home("b1")
-    relay("o")
+    in_turn(2)
+    to_outer("i1")
+    to_inner("b0")
+    arrived("v")
+    project(2)
 
     def attend(r):
         rows = rows_of(r)
@@ -918,7 +990,11 @@
         s.ctx[rows, :] = context
         s.ctxt[:, rows] = context.T
     loop(2, attend)
+    relay("o")
     over_plane("i1")
+    in_turn(3)
+    to_outer("b0")
+    from_home("b1")
     loop(2, lambda r: attend(r + 2))
     relay("i0")
     over_plane("b0")
@@ -930,7 +1006,6 @@
             put_part(dst, add, n, dot_nn(rows, s.wo[n]))
     scatter(0, attn_part)
     relay("i1")
-    over_plane("b1")
     for m in range(3):
         for n in range(4):
             s.w3t[m, :, 256 * n:256 * n + 256] = s.w3[m * WIDTH + 256 * n:m * WIDTH + 256 * n + 256, :].T
@@ -956,8 +1031,10 @@
         s.inv1[ch, :] = jnp.broadcast_to(inv, (CH, 128))
         s.hid1[ch, :] = hidden
         s.hid[group_chunk(i), :] = hidden.astype(BF16)
+    over_plane("b1")
     by_halves(0, norm_one, lambda k: gather_start(0, s.hid, k))
     send_cotangent()
+    relay("b0")
     arrived("i0")
     arrived("i1")
 
@@ -979,22 +1056,17 @@
         rows = rows_of(r)
         s.actt[:, rows] = s.act[rows, :].T
         s.hidt[:, rows] = s.hid[rows, :].T
-    relay("b0")
+    relay("b1")
+    scatter_cols(1, (b, bx, by), 0)
     loop(SLOTS, turn_ffn)
 
     def turn_wi(r):
         rows = rows_of(r)
         s.wit[:, rows] = s.wi[rows, :].T
     loop(8, turn_wi)
-    relay("b1")
     arrived("b0")
     arrived("b1")
-
-    def ffn_part(first, count, dst, add):
-        rows = pl.ds(pl.multiple_of(first, HALF), count)
-        for n in range(4):
-            put_part(dst, add, n, dot_nn(s.act[rows, :], s.wb[n]))
-    scatter(1, ffn_part)
+    scatter_cols(1, (bd,), 1)
 
     def turn_wb(r):
         rows = rows_of(r)
@@ -1030,7 +1102,9 @@
     home_self = jnp.logical_and(zh == c, t == z)
 
     def ffn_back(j):
-        gather_step(1, s.g2, j)
+        @pl.when(j < 3)
+        def _():
+            gather_step(1, s.g2, j)
         r = slot_step(t, j)
         rows = rows_of(r)
         for n in range(4):
@@ -1038,7 +1112,7 @@
             grad = dot_nn(s.g2[rows, :], s.wbt[:, cols]) * s.slope[rows, cols]
             s.gb_in[:, cols] += jnp.sum(grad, axis=0, keepdims=True)
             s.gpre[rows, cols] = grad.astype(BF16)
-    loop(SLOTS, ffn_back)
+    loop(SLOTS - 1, ffn_back)
     send_or_keep(s.out_own, o.out, dev(b, zh, t), home_self, out_s, out_r)
     at_end(s.out_own, out_s, home_self)
 
@@ -1059,8 +1133,10 @@
             s.gi[part, cols] = dot_nn(s.hidt[part, :], s.gpre[:, cols]).astype(BF16)
         loop(2, body)
 
+    gather_step(1, s.g2, 3)
     grad_back(0)
     grad_first("b0")
+    ffn_back(3)
     grad_back(1)
     grad_first("b1")
 
@@ -1072,7 +1148,6 @@
     grad_in(0)
     grad_in(1)
     grad_second("b0")
-    grad_first("i0")
 
     def norm_one_back(i):
         ch = own_chunk(i)
@@ -1089,7 +1164,8 @@
         s.g1[group_chunk(i), :] = grad_one.astype(BF16)
     by_halves(2, norm_one_back, lambda k: gather_start(2, s.g1, k))
     grad_second("b1")
-    grad_first("i1")
+    grad_first("i0")
+    grad_first("i1", 0)
 
     def attend_back(j):
         gather_step(2, s.g1, j)
@@ -1117,7 +1193,6 @@
     loop(2, attend_back)
     grad_third("b0")
     loop(2, lambda j: attend_back(j + 2))
-    grad_second("i0")
     grad_third("b1")
 
     def turn_back(r):
@@ -1160,6 +1235,8 @@
             acc = acc + dot_nn(s.dk[rows, :], s.w3t[1, :, cols])
             acc = acc + dot_nn(s.dv[rows, :], s.w3t[2, :, cols])
             put_part(dst, add, n, acc)
+    grad_second("i0")
+    grad_first("i1", 1)
     scatter(3, tok_part)
     sums_finish(0)
     sums_start(1)
@@ -1190,14 +1267,14 @@
     grad_second("q")
     grad_first("v")
     grad_third("o")
+    grad_second("k")
+    grad_third("q")
     sums_finish(1)
     sums_start(2)
-    grad_second("k")
-    grad_third("q")
+    grad_second("v")
+    grad_third("k")
     sums_finish(2)
     sums_start(3)
-    grad_second("v")
-    grad_third("k")
     grad_third("v")
     sums_finish(3)
     sums_start(4)

time: 169 us -> 154 us (0.911); the launches traced: 166 us -> 154 us
  Pallas kernels: 165 us -> 153 us
    pallas_call x1, Pallas kernels: 162 us -> 150 us  [on_device_fused(): pl.pallas_call(layer_kernel, out_shape=between, in_specs=in_specs, out_sp...]
where the time goes in v3:
time: 154 us
  Pallas kernels  153 us (99%)
    pallas_call x1, Pallas kernels, on_device_fused(): pl.pallas_call(layer_kernel, out_shape=between, in_specs=in_specs, out_sp...  150 us

profile of v3, /device:TPU:1, one launch (start us, length us, event | category | flops | bytes accessed | tf_op | source)
XLA Modules:
  0.0 154.3 jit_solution(11882039143038902471)
XLA Ops:
  0.7 150.4 %layer.1 = (bf16[128,1024]{1,0:T(8,128)(2,1)}, bf16[128,1024]{1,0:T(8,128)(2,1)}, f32[16,1024]{1,0:T(8,128)}, bf16[2,128,256]{2,1,0:T(8,128)(2,1)}, bf16[2,128,2...) custom-call(bf16[128,1024]{1,0:T(8,128)(2,1)} %tok.1, ...), custom_call_target="tpu_custom_call" | custom-call | tf_op jit(solution)/shard_map/layer/pallas_call | solution.py:1333
  151.0 3.0 %results.1 = (bf16[128,1024]{1,0:T(8,128)(2,1)}, f32[128,1024]{1,0:T(8,128)}, f32[128,256]{1,0:T(8,128)}, f32[1,1024]{1,0:T(1,128)}, f32[128,256]{1,0:T(8,128)},...) custom-call(bf16[128,1024]{1,0:T(8,128)(2,1)} %get-tuple-element.45., ...), custom_call_target="tpu_custom_call" | custom-call | tf_op jit(solution)/shard_map/results/pallas_call | solution.py:1347

commit v4 on v3

--- a/solution.py
+++ b/solution.py
@@ -496,6 +496,7 @@
     z_far = (z + 2) % 4
     pair = dev(b, c, z_near)
     across = dev(b, c, z_far)
+    is_inner = jnp.logical_and(z >= 1, z <= 2)
     x_near = dev(bx, c, z)
     y_near = dev(by, c, z)
 
@@ -598,9 +599,10 @@
         piece = pieces[name]
         send(piece.home, piece.own(b, c), dev(b, z % 2, 2 - zh), piece.s1, piece.r1)
 
-    def from_home(name):
-        to_inner(name)
-        to_outer(name)
+    def to_outer_in_turn(name):
+        @pl.when(is_inner)
+        def _():
+            to_outer(name)
 
     def over_plane(name):
         piece = pieces[name]
@@ -615,6 +617,18 @@
         got(piece.block(by), piece.r2 + 1)
         send(piece.half(by, 1), piece.half(by, 1), x_near, piece.s2, piece.r2 + 2)
 
+    def over_plane_now(names, chosen, relays=()):
+        @pl.when(chosen)
+        def _():
+            for name in relays:
+                relay(name)
+            for name in names:
+                over_plane(name)
+
+    lives_here = jnp.logical_or(jnp.logical_and(z == 0, c == 0), jnp.logical_and(z == 3, c == 1))
+
+    lives_away = jnp.logical_not(lives_here)
+
     def arrived(name):
         piece = pieces[name]
         got(piece.block(bd), piece.r2 + 2)
@@ -647,7 +661,6 @@
 
     inner, outer = 1 + c, 3 * c
     is_relay = jnp.logical_and(c == zh, z == inner)
-    is_inner = jnp.logical_and(z >= 1, z <= 2)
 
     def send_tokens():
         near = z // 2 == c
@@ -881,6 +894,12 @@
     to_inner("v")
     for name in "qkv":
         to_outer(name)
+
+    @pl.when(jnp.logical_not(is_inner))
+    def _():
+        for name in ("o", "i0", "i1", "b0", "b1"):
+            to_outer(name)
+
     send_lens()
     for name, ref in vectors.items():
         pltpu.make_async_copy(getattr(a, name), ref, vsem.at[list(vectors).index(name)]).start()
@@ -923,24 +942,20 @@
         setattr(a, name, ref)
     relay("k")
     over_plane("v")
+    over_plane_now(("o", "i0"), lives_here)
+    over_plane_now(("o",), is_inner)
     relay("v")
-
-    @pl.when(is_inner)
-    def _():
-        over_plane("o")
+    over_plane_now(("i1",), lives_here, relays=("o",))
 
     @pl.when(jnp.logical_not(is_inner))
     def _():
         pass_on(flip(zh), 1)
 
     in_turn(1)
-    to_outer("o")
-    to_outer("i0")
+    to_outer_in_turn("o")
+    to_outer_in_turn("i0")
     to_inner("i1")
-
-    @pl.when(jnp.logical_not(is_inner))
-    def _():
-        over_plane("o")
+    over_plane_now(("o",), jnp.logical_not(jnp.logical_or(is_inner, lives_here)))
 
 
     def turn_tokens(r):
@@ -967,9 +982,10 @@
     project(0)
     arrived("k")
     project(1)
-    over_plane("i0")
+    over_plane_now(("i0",), lives_away)
+    over_plane_now(("b0",), lives_here, relays=("i0",))
     in_turn(2)
-    to_outer("i1")
+    to_outer_in_turn("i1")
     to_inner("b0")
     arrived("v")
     project(2)
@@ -990,14 +1006,16 @@
         s.ctx[rows, :] = context
         s.ctxt[:, rows] = context.T
     loop(2, attend)
-    relay("o")
-    over_plane("i1")
+    over_plane_now((), lives_away, relays=("o",))
+    over_plane_now(("i1",), lives_away)
+    over_plane_now(("b1",), lives_here)
     in_turn(3)
-    to_outer("b0")
-    from_home("b1")
+    to_outer_in_turn("b0")
+    to_outer_in_turn("b1")
+    to_inner("b1")
     loop(2, lambda r: attend(r + 2))
-    relay("i0")
-    over_plane("b0")
+    over_plane_now((), lives_away, relays=("i0",))
+    over_plane_now(("b0",), lives_away)
     arrived("o")
 
     def attn_part(first, count, dst, add):
@@ -1031,7 +1049,7 @@
         s.inv1[ch, :] = jnp.broadcast_to(inv, (CH, 128))
         s.hid1[ch, :] = hidden
         s.hid[group_chunk(i), :] = hidden.astype(BF16)
-    over_plane("b1")
+    over_plane_now(("b1",), lives_away)
     by_halves(0, norm_one, lambda k: gather_start(0, s.hid, k))
     send_cotangent()
     relay("b0")
@@ -1113,8 +1131,6 @@
             s.gb_in[:, cols] += jnp.sum(grad, axis=0, keepdims=True)
             s.gpre[rows, cols] = grad.astype(BF16)
     loop(SLOTS - 1, ffn_back)
-    send_or_keep(s.out_own, o.out, dev(b, zh, t), home_self, out_s, out_r)
-    at_end(s.out_own, out_s, home_self)
 
     def grad_back(k):
         part = slice(512 * k, 512 * k + 512)
@@ -1138,7 +1154,9 @@
     grad_first("b0")
     ffn_back(3)
     grad_back(1)
-    grad_first("b1")
+    grad_first("b1", 0)
+    send_or_keep(s.out_own, o.out, dev(b, zh, t), home_self, out_s, out_r)
+    at_end(s.out_own, out_s, home_self)
 
     def in_part(first, count, dst, add):
         rows = pl.ds(pl.multiple_of(first, HALF), count)
@@ -1148,6 +1166,9 @@
     grad_in(0)
     grad_in(1)
     grad_second("b0")
+    grad_first("b1", 1)
+    grad_second("b1")
+    grad_first("i0", 0)
 
     def norm_one_back(i):
         ch = own_chunk(i)
@@ -1163,9 +1184,8 @@
         s.g1f[ch, :] = grad_one
         s.g1[group_chunk(i), :] = grad_one.astype(BF16)
     by_halves(2, norm_one_back, lambda k: gather_start(2, s.g1, k))
-    grad_second("b1")
-    grad_first("i0")
-    grad_first("i1", 0)
+    grad_first("i0", 1)
+    grad_third("b0")
 
     def attend_back(j):
         gather_step(2, s.g1, j)
@@ -1191,9 +1211,11 @@
                 s.sums[0, 6:7, 256 * k:256 * k + 256] += jnp.sum(grad_query, axis=0, keepdims=True)
         s.dq[rows, :] = grad_query.astype(BF16)
     loop(2, attend_back)
-    grad_third("b0")
-    loop(2, lambda j: attend_back(j + 2))
     grad_third("b1")
+    loop(1, lambda j: attend_back(j + 2))
+    grad_second("i0")
+    grad_first("i1")
+    loop(1, lambda j: attend_back(j + 3))
 
     def turn_back(r):
         rows = rows_of(r)
@@ -1220,10 +1242,9 @@
     def sums_finish(k):
         got(s.sums_got.at[k], sums_r + k)
         total = s.sums[k] + s.sums_got[k]
+        s.sums[k + 1] = total
         if k == 4:
-            o.sums[...] = total
-        else:
-            s.sums[k + 1] = total
+            pltpu.make_async_copy(s.sums.at[5], o.sums, vsem.at[0]).start()
 
     sums_start(0)
 
@@ -1235,8 +1256,6 @@
             acc = acc + dot_nn(s.dk[rows, :], s.w3t[1, :, cols])
             acc = acc + dot_nn(s.dv[rows, :], s.w3t[2, :, cols])
             put_part(dst, add, n, acc)
-    grad_second("i0")
-    grad_first("i1", 1)
     scatter(3, tok_part)
     sums_finish(0)
     sums_start(1)
@@ -1244,6 +1263,7 @@
     def grad_head(m, src):
         s.g3[m * WIDTH:(m + 1) * WIDTH, :] = dot_nn(s.tkt[...], src[...]).astype(BF16)
 
+    grad_third("i0")
     for n in range(4):
         s.go[n] = dot_nn(s.ctxt[...], s.g1[:, 256 * n:256 * n + 256]).astype(BF16)
     grad_head(0, s.dq)
@@ -1252,7 +1272,6 @@
     grad_second("i1")
     grad_first("o")
     grad_first("q")
-    grad_third("i0")
     grad_third("i1")
     grad_second("o")
     grad_first("k")
@@ -1266,15 +1285,15 @@
     at_end(s.gtok_own, gtok_s, home_self)
     grad_second("q")
     grad_first("v")
+    sums_finish(1)
+    sums_start(2)
     grad_third("o")
     grad_second("k")
     grad_third("q")
-    sums_finish(1)
-    sums_start(2)
+    sums_finish(2)
     grad_second("v")
+    sums_start(3)
     grad_third("k")
-    sums_finish(2)
-    sums_start(3)
     grad_third("v")
     sums_finish(3)
     sums_start(4)
@@ -1290,6 +1309,7 @@
     grad_final("k")
     grad_final("v")
 
+    pltpu.make_async_copy(s.sums.at[5], o.sums, vsem.at[0]).wait()
     for size_of, sk, skipped, instead in to_drain:
         if skipped is None:
             left(size_of, sk)
@@ -1334,7 +1354,7 @@
         layer_kernel,
         out_shape=between,
         in_specs=in_specs,
-        out_specs=[stay, stay, vmem] + [stay] * 8,
+        out_specs=[stay] * len(between),
         scratch_shapes=jax.tree.leaves(scratch_table()),
         compiler_params=pltpu.CompilerParams(collective_id=0, has_side_effects=True, vmem_limit_bytes=64 * 1024 * 1000),
         name="layer",

time: 154 us -> 151 us (0.981)
  Pallas kernels: 153 us -> 150 us
    pallas_call x1, Pallas kernels: 150 us -> 146 us  [on_device_fused(): pl.pallas_call(layer_kernel, out_shape=between, in_specs=in_specs, out_sp...]
where the time goes in v4:
time: 151 us; the launch traced here: 150 us
  Pallas kernels  150 us (99%)
    pallas_call x1, Pallas kernels, on_device_fused(): pl.pallas_call(layer_kernel, out_shape=between, in_specs=in_specs, out_sp...  146 us
    pallas_call x1, Pallas kernels, on_device_fused(): pl.pallas_call(result_kernel, out_shape=results, in_specs=[vmem] * len(be...  3.05 us

profile of v4, /device:TPU:1, one launch (start us, length us, event | category | flops | bytes accessed | tf_op | source)
XLA Modules:
  0.0 150.4 jit_solution(12297993538502914464)
XLA Ops:
  0.7 146.5 %layer.1 = (bf16[128,1024]{1,0:T(8,128)(2,1)}, bf16[128,1024]{1,0:T(8,128)(2,1)}, f32[16,1024]{1,0:T(8,128)}, bf16[2,128,256]{2,1,0:T(8,128)(2,1)}, bf16[2,128,2...) custom-call(bf16[128,1024]{1,0:T(8,128)(2,1)} %tok.1, ...), custom_call_target="tpu_custom_call" | custom-call | tf_op jit(solution)/shard_map/layer/pallas_call | solution.py:1353
  147.2 3.0 %results.1 = (bf16[128,1024]{1,0:T(8,128)(2,1)}, f32[128,1024]{1,0:T(8,128)}, f32[128,256]{1,0:T(8,128)}, f32[1,1024]{1,0:T(1,128)}, f32[128,256]{1,0:T(8,128)},...) custom-call(bf16[128,1024]{1,0:T(8,128)(2,1)} %get-tuple-element.45., ...), custom_call_target="tpu_custom_call" | custom-call | tf_op jit(solution)/shard_map/results/pallas_call | solution.py:1367

commit v5 on v4

--- a/solution.py
+++ b/solution.py
@@ -455,7 +455,7 @@
         gb_in=pltpu.VMEM((1, HIDDEN), F32),
         vectors={name: pltpu.VMEM((1, width), F32) for name, width in VECTORS.items()},
         vsem=pltpu.SemaphoreType.DMA((len(VECTORS),)),
-        turn=pltpu.SemaphoreType.REGULAR((4,)),
+        turn=pltpu.SemaphoreType.REGULAR((5,)),
         g3=pltpu.VMEM((3 * WIDTH, HEAD_COLS), BF16),
         go=pltpu.VMEM((4, HEAD_COLS, 256), BF16),
         gi=pltpu.VMEM((WIDTH, HIDDEN), BF16),
@@ -483,6 +483,8 @@
     b, c = dp // 2, dp % 2
     zl, zh = z % 2, z // 2
     t = zl * 2 + c
+    sl = (z + 2 * c) % 4
+    here, away = c == 0, c == 1
     bx = b + 1 - 2 * (b % 2)
     by = (b + 2) % 4
     bd = 3 - b
@@ -497,6 +499,8 @@
     pair = dev(b, c, z_near)
     across = dev(b, c, z_far)
     is_inner = jnp.logical_and(z >= 1, z <= 2)
+    inner_away = jnp.logical_and(is_inner, away)
+    outer_away = jnp.logical_and(jnp.logical_not(is_inner), away)
     x_near = dev(bx, c, z)
     y_near = dev(by, c, z)
 
@@ -586,23 +590,16 @@
     for name, piece in pieces.items():
         piece.s1, piece.r1 = take("s"), take("r")
         piece.s2, piece.r2 = take("s"), take("r", 3)
-        keeps_one = jnp.logical_or(jnp.logical_and(z == 0, c == 0), jnp.logical_and(z == 3, c == 1))
-        at_end(piece.block(b), piece.s1, keeps_one, piece.own(b, 0))
+        at_end(piece.block(b), piece.s1, here, piece.own(b, 0))
         at_end(first_size[name], piece.s2)
 
-    def to_outer(name):
+    def to_local(name):
         piece = pieces[name]
-        is_self = jnp.logical_and(z == 3 * zh, z % 2 == c)
-        send_or_keep(piece.home, piece.own(b, c), dev(b, z % 2, 3 * zh), is_self, piece.s1, piece.r1)
-
-    def to_inner(name):
+        send_or_keep(piece.home, piece.own(b, c), dev(b, 0, z), here, piece.s1, piece.r1)
+
+    def to_across(name):
         piece = pieces[name]
-        send(piece.home, piece.own(b, c), dev(b, z % 2, 2 - zh), piece.s1, piece.r1)
-
-    def to_outer_in_turn(name):
-        @pl.when(is_inner)
-        def _():
-            to_outer(name)
+        send(piece.home, piece.own(b, c), dev(b, 1, z_far), piece.s1, piece.r1)
 
     def over_plane(name):
         piece = pieces[name]
@@ -624,10 +621,6 @@
                 relay(name)
             for name in names:
                 over_plane(name)
-
-    lives_here = jnp.logical_or(jnp.logical_and(z == 0, c == 0), jnp.logical_and(z == 3, c == 1))
-
-    lives_away = jnp.logical_not(lives_here)
 
     def arrived(name):
         piece = pieces[name]
@@ -741,6 +734,8 @@
 
         @pl.when(j == 3)
         def _():
+            if which == 0:
+                over_plane_now((), inner_away, relays=("b0", "b1"))
             got(block_at(full, t3), base + 3)
 
     halves = [pl.ds(k * HALF, HALF) for k in range(2)]
@@ -748,51 +743,18 @@
     def scatter(which, part):
         out, back = s.rs_out, s.rs_got
         ss, rr = scatter_s + which, scatter_r + 5 * which
+        part(t3 * BLOCK, BLOCK, out.at[which, 0])
+        send(out.at[which, 0], back.at[which, 0], partner, ss, rr)
+        part(t2 * BLOCK, BLOCK, out.at[which, 1])
+        got(back.at[which, 0], rr)
         for k in range(2):
-            mine = out.at[which, 0, halves[k], :]
-            part(t3 * BLOCK + k * HALF, HALF, mine, None)
-            send(mine, back.at[which, 0, halves[k], :], partner, ss, rr + k)
-        for k in range(2):
-            mine, theirs = out.at[which, 1, halves[k], :], back.at[which, 0, halves[k], :]
-            got(theirs, rr + k)
-            part(t2 * BLOCK + k * HALF, HALF, mine, theirs)
-            send(mine, back.at[which, 1, halves[k], :], pair, ss, rr + 2 + k)
-        part(t1 * BLOCK, BLOCK, out.at[which, 2], None)
+            rows = halves[k]
+            total = out[which, 1, rows, :].astype(F32) + back[which, 0, rows, :].astype(F32)
+            out[which, 1, rows, :] = total.astype(BF16)
+            send(out.at[which, 1, rows, :], back.at[which, 1, rows, :], pair, ss, rr + 2 + k)
+        part(t1 * BLOCK, BLOCK, out.at[which, 2])
         send(out.at[which, 2], back.at[which, 2], partner, ss, rr + 4)
-        part(t * BLOCK, BLOCK, s.rs_own.at[which], None)
-
-    def scatter_cols(which, blocks, k):
-        out, back = s.rs_out, s.rs_got
-        ss, rr = scatter_s + which, scatter_r + 5 * which
-        slots = [pl.ds(pl.multiple_of(block * 256, 256), 256) for block in blocks]
-        size = s.rs_got.at[which, 0, :, 0:256 * len(blocks)]
-
-        def product(row, block):
-            rows = pl.ds(pl.multiple_of(row * BLOCK, BLOCK), BLOCK)
-            return dot_nn(s.act[rows, :], s.wb[block])
-
-        def cast(row, slot):
-            for block, cols in zip(blocks, slots):
-                out[which, slot, :, cols] = product(row, block).astype(BF16)
-
-        cast(t3, 0)
-        for cols in slots:
-            send(out.at[which, 0, :, cols], back.at[which, 0, :, cols], partner, ss, rr + k)
-        cast(t1, 2)
-        for cols in slots:
-            send(out.at[which, 2, :, cols], back.at[which, 2, :, cols], partner, ss, rr + 4)
-        got(size, rr + k)
-        for block, cols in zip(blocks, slots):
-            total = product(t2, block).astype(BF16).astype(F32) + back[which, 0, :, cols].astype(F32)
-            out[which, 1, :, cols] = total.astype(BF16)
-            send(out.at[which, 1, :, cols], back.at[which, 1, :, cols], pair, ss, rr + 2)
-        for block, cols in zip(blocks, slots):
-            s.rs_own[which, :, cols] = product(t, block).astype(BF16)
-
-    def scatter_cols_wait(which):
-        rr = scatter_r + 5 * which
-        got(s.rs_got.at[which, 2], rr + 4)
-        got(s.rs_got.at[which, 1], rr + 2)
+        part(t * BLOCK, BLOCK, s.rs_own.at[which])
 
     def scatter_wait(which, k):
         rr = scatter_r + 5 * which
@@ -805,20 +767,13 @@
         return total + s.rs_got[which, 1, chunk, :].astype(F32)
 
     def by_halves(which, body, after):
-        if which == 1:
-            scatter_cols_wait(which)
         for k in range(2):
-            if which != 1:
-                scatter_wait(which, k)
+            scatter_wait(which, k)
             loop(2, lambda i: body(2 * k + i))
             after(k)
 
-    def put_part(dst, add, n, value):
-        cols = slice(256 * n, 256 * n + 256)
-        value = value.astype(BF16)
-        if add is not None:
-            value = (value.astype(F32) + add[:, cols].astype(F32)).astype(BF16)
-        dst[:, cols] = value
+    def put_part(dst, n, value):
+        dst[:, 256 * n:256 * n + 256] = value.astype(BF16)
 
     def loop(count, body):
         lax.fori_loop(0, count, lambda i, _: (body(i), 0)[1], 0)
@@ -840,10 +795,9 @@
         i0=grad_in_part(0), i1=grad_in_part(1), b0=grad_back_part(0), b1=grad_back_part(1))
     grad_s = {name: take("s", 2) for name in grad_half}
     grad_r = {name: take("r", 4) for name in grad_half}
-    keeps_part = jnp.logical_or(jnp.logical_and(z == 0, c == 0), jnp.logical_and(z == 3, c == 1))
     for name in grad_half:
         at_end(s.stage[name].at[0:6], grad_s[name])
-        at_end(s.stage[name].at[0:2], grad_s[name] + 1, keeps_part, s.stage[name].at[0])
+        at_end(s.stage[name].at[0:2], grad_s[name] + 1, here, s.stage[name].at[0])
 
     def chunks(name, body):
         size = 64 if name in ("i0", "i1") else 128
@@ -882,52 +836,54 @@
                 total = mine[ch, :].astype(F32) + st[2 * h, ch, :].astype(F32) + st[6 + h, ch, :].astype(F32)
                 st[8 + h, ch, :] = total.astype(BF16)
             chunks(name, add_all)
-            is_self = jnp.logical_and(c == h, z == t)
-            send_or_keep(st.at[8 + h], zr.at[zh], dev(b, h, t), is_self, ss + 1, rr + 3)
+            is_self = here if h == 0 else c < 0
+            send_or_keep(st.at[8 + h], zr.at[zh], dev(b, h, sl), is_self, ss + 1, rr + 3)
 
     def grad_final(name):
         got(landed[name], grad_r[name] + 3)
 
-    to_inner("q")
-    to_inner("k")
+    to_across("q")
+    to_across("k")
     send_tokens()
-    to_inner("v")
-    for name in "qkv":
-        to_outer(name)
-
-    @pl.when(jnp.logical_not(is_inner))
-    def _():
-        for name in ("o", "i0", "i1", "b0", "b1"):
-            to_outer(name)
-
+    to_across("v")
+    for name in pieces:
+        to_local(name)
     send_lens()
     for name, ref in vectors.items():
         pltpu.make_async_copy(getattr(a, name), ref, vsem.at[list(vectors).index(name)]).start()
     s.sums[0] = jnp.zeros((16, WIDTH), F32)
     s.gb_in[...] = jnp.zeros((1, HIDDEN), F32)
-    s.dkt[...] = jnp.zeros((HEAD_COLS, GROUP), F32)
-    s.dvt[...] = jnp.zeros((HEAD_COLS, GROUP), F32)
-    def in_turn(k):
-        @pl.when(is_inner)
-        def _():
-            pl.semaphore_signal(s.turn.at[k], inc=1, device_id=pair, device_id_type=MESH_ID)
-
-        @pl.when(jnp.logical_not(is_inner))
+    leads = jnp.logical_and(is_inner, away)
+
+    def in_turn(k, inner_next, outer_next):
+        @pl.when(leads)
+        def _():
+            for device in (partner, pair, dev(b, 0, z_near)):
+                pl.semaphore_signal(s.turn.at[k], inc=1, device_id=device, device_id_type=MESH_ID)
+
+        @pl.when(jnp.logical_not(leads))
         def _():
             pl.semaphore_wait(s.turn.at[k], 1)
 
-    over_plane("q")
-    over_plane("k")
+        for chosen, names in ((is_inner, inner_next), (jnp.logical_not(is_inner), outer_next)):
+            if names:
+                @pl.when(chosen)
+                def _():
+                    for name in names:
+                        to_across(name)
+
+    over_plane_now(("q", "k", "v", "o"), here)
+    over_plane_now(("q", "k"), away)
     relay("q")
+    over_plane_now(("i0",), here, relays=("k", "v"))
     pass_on(zh, 0)
-    to_inner("o")
+    to_across("o")
 
     @pl.when(is_inner)
     def _():
         pass_on(flip(zh), 1)
 
-    in_turn(0)
-    to_inner("i0")
+    in_turn(0, (), ("i0",))
     take_lens()
 
     def make_bias(r):
@@ -940,29 +896,22 @@
     for name, ref in vectors.items():
         pltpu.make_async_copy(getattr(a, name), ref, vsem.at[list(vectors).index(name)]).wait()
         setattr(a, name, ref)
-    relay("k")
-    over_plane("v")
-    over_plane_now(("o", "i0"), lives_here)
-    over_plane_now(("o",), is_inner)
-    relay("v")
-    over_plane_now(("i1",), lives_here, relays=("o",))
+    over_plane_now(("v", "o"), away, relays=("k",))
+    over_plane_now(("i1",), here, relays=("o",))
+    over_plane_now((), away, relays=("v",))
+    over_plane_now(("b0",), here, relays=("i0",))
+    in_turn(1, ("i0", "i1"), ("i1",))
 
     @pl.when(jnp.logical_not(is_inner))
     def _():
         pass_on(flip(zh), 1)
 
-    in_turn(1)
-    to_outer_in_turn("o")
-    to_outer_in_turn("i0")
-    to_inner("i1")
-    over_plane_now(("o",), jnp.logical_not(jnp.logical_or(is_inner, lives_here)))
-
 
     def turn_tokens(r):
         s.tkt[:, rows_of(r)] = s.tk[rows_of(r), :].T
     loop(SLOTS, turn_tokens)
 
-    head_cols = pl.ds(pl.multiple_of(t * HEAD_COLS, HEAD_COLS), HEAD_COLS)
+    head_cols = pl.ds(pl.multiple_of(sl * HEAD_COLS, HEAD_COLS), HEAD_COLS)
 
     def project(m):
         acc = dot_nn(s.tk[...], s.w3[m * WIDTH:(m + 1) * WIDTH, :])
@@ -982,48 +931,41 @@
     project(0)
     arrived("k")
     project(1)
-    over_plane_now(("i0",), lives_away)
-    over_plane_now(("b0",), lives_here, relays=("i0",))
-    in_turn(2)
-    to_outer_in_turn("i1")
-    to_inner("b0")
+    in_turn(2, ("b0", "b1"), ())
     arrived("v")
     project(2)
 
-    def attend(r):
-        rows = rows_of(r)
+    def attend():
         parts = []
         for h in range(4):
             cols = slice(64 * h, 64 * h + 64)
-            scores = dot_nt(s.q[rows, cols], s.k[:, cols]) + s.bias[rows, :]
+            scores = dot_nt(s.q[:, cols], s.k[:, cols]) + s.bias[...]
             top = jnp.max(scores, axis=-1, keepdims=True)
             weight = jnp.exp(scores - top)
             total = jnp.sum(weight, axis=-1, keepdims=True)
             prob = (weight * (1.0 / total)).astype(BF16)
-            s.ps[h, rows, :] = prob
+            s.ps[h] = prob
             parts.append(dot_nn(prob, s.v[:, cols]))
         context = jnp.concatenate(parts, axis=1).astype(BF16)
-        s.ctx[rows, :] = context
-        s.ctxt[:, rows] = context.T
-    loop(2, attend)
-    over_plane_now((), lives_away, relays=("o",))
-    over_plane_now(("i1",), lives_away)
-    over_plane_now(("b1",), lives_here)
-    in_turn(3)
-    to_outer_in_turn("b0")
-    to_outer_in_turn("b1")
-    to_inner("b1")
-    loop(2, lambda r: attend(r + 2))
-    over_plane_now((), lives_away, relays=("i0",))
-    over_plane_now(("b0",), lives_away)
+        s.ctx[...] = context
+        s.ctxt[...] = context.T
+    over_plane_now((), away, relays=("o",))
+    over_plane_now(("i0", "i1"), inner_away)
+    over_plane_now(("b1",), here, relays=("i1",))
+    attend()
+    over_plane_now(("i0", "i1"), outer_away)
     arrived("o")
 
-    def attn_part(first, count, dst, add):
+    def attn_part(first, count, dst):
         rows = s.ctx[pl.ds(pl.multiple_of(first, HALF), count), :]
         for n in range(4):
-            put_part(dst, add, n, dot_nn(rows, s.wo[n]))
+            put_part(dst, n, dot_nn(rows, s.wo[n]))
     scatter(0, attn_part)
-    relay("i1")
+    @pl.when(jnp.logical_not(is_inner))
+    def _():
+        to_across("b0")
+        to_across("b1")
+
     for m in range(3):
         for n in range(4):
             s.w3t[m, :, 256 * n:256 * n + 256] = s.w3[m * WIDTH + 256 * n:m * WIDTH + 256 * n + 256, :].T
@@ -1049,12 +991,17 @@
         s.inv1[ch, :] = jnp.broadcast_to(inv, (CH, 128))
         s.hid1[ch, :] = hidden
         s.hid[group_chunk(i), :] = hidden.astype(BF16)
-    over_plane_now(("b1",), lives_away)
+    over_plane_now((), here, relays=("b0",))
+    over_plane_now((), inner_away, relays=("i0", "i1"))
+    over_plane_now(("b0", "b1"), outer_away, relays=("i0",))
+    over_plane_now((), outer_away, relays=("i1",))
     by_halves(0, norm_one, lambda k: gather_start(0, s.hid, k))
-    send_cotangent()
-    relay("b0")
+    over_plane_now((), here, relays=("b1",))
+    over_plane_now((), outer_away, relays=("b0", "b1"))
     arrived("i0")
     arrived("i1")
+
+    over_plane_now(("b0", "b1"), inner_away)
 
     def ffn_in(j):
         gather_step(0, s.hid, j)
@@ -1062,29 +1009,33 @@
         rows = rows_of(r)
         for n in range(4):
             cols = slice(256 * n, 256 * n + 256)
-            bias = a.bi[:, pl.ds(pl.multiple_of(t * HIDDEN + n * 256, 256), 256)]
+            bias = a.bi[:, pl.ds(pl.multiple_of(sl * HIDDEN + n * 256, 256), 256)]
             pre = dot_nn(s.hid[rows, :], s.wi[:, cols]) + bias
             cdf = 0.5 * (1.0 + lax.erf(pre * 0.7071067811865476))
             pdf = jnp.exp(-0.5 * pre * pre) * 0.3989422804014327
             s.act[rows, cols] = (pre * cdf).astype(BF16)
             s.slope[rows, cols] = cdf + pre * pdf
     loop(SLOTS, ffn_in)
+    send_cotangent()
 
     def turn_ffn(r):
         rows = rows_of(r)
         s.actt[:, rows] = s.act[rows, :].T
         s.hidt[:, rows] = s.hid[rows, :].T
-    relay("b1")
-    scatter_cols(1, (b, bx, by), 0)
+    arrived("b0")
+    arrived("b1")
+
+    def ffn_part(first, count, dst):
+        rows = pl.ds(pl.multiple_of(first, HALF), count)
+        for n in range(4):
+            put_part(dst, n, dot_nn(s.act[rows, :], s.wb[n]))
+    scatter(1, ffn_part)
     loop(SLOTS, turn_ffn)
 
     def turn_wi(r):
         rows = rows_of(r)
         s.wit[:, rows] = s.wi[rows, :].T
     loop(8, turn_wi)
-    arrived("b0")
-    arrived("b1")
-    scatter_cols(1, (bd,), 1)
 
     def turn_wb(r):
         rows = rows_of(r)
@@ -1158,10 +1109,10 @@
     send_or_keep(s.out_own, o.out, dev(b, zh, t), home_self, out_s, out_r)
     at_end(s.out_own, out_s, home_self)
 
-    def in_part(first, count, dst, add):
+    def in_part(first, count, dst):
         rows = pl.ds(pl.multiple_of(first, HALF), count)
         for n in range(4):
-            put_part(dst, add, n, dot_nn(s.gpre[rows, :], s.wit[:, 256 * n:256 * n + 256]))
+            put_part(dst, n, dot_nn(s.gpre[rows, :], s.wit[:, 256 * n:256 * n + 256]))
     scatter(2, in_part)
     grad_in(0)
     grad_in(1)
@@ -1187,10 +1138,8 @@
     grad_first("i0", 1)
     grad_third("b0")
 
-    def attend_back(j):
-        gather_step(2, s.g1, j)
-        r = slot_step(t, j)
-        rows = rows_of(r)
+    def attend_back(chip, add):
+        rows = pl.ds(pl.multiple_of(chip * 2 * BLOCK, 2 * BLOCK), 2 * BLOCK)
         grad_ctx = dot_nn(s.g1[rows, :], s.wot[...]).astype(BF16)
         s.gctxt[:, rows] = grad_ctx.T
         product = grad_ctx.astype(F32) * s.ctx[rows, :].astype(F32)
@@ -1202,33 +1151,35 @@
             grad_prob = dot_nt(grad_ctx[:, cols], s.v[:, cols])
             grad_score = (prob.astype(F32) * (grad_prob - delta)).astype(BF16)
             parts.append(dot_nn(grad_score, s.ks[:, cols]))
-            s.dkt[cols, :] += dot_nn(s.qt[cols, rows], grad_score)
-            s.dvt[cols, :] += dot_nn(s.gctxt[cols, rows], prob)
+            grad_key = dot_nn(s.qt[cols, rows], grad_score)
+            grad_value = dot_nn(s.gctxt[cols, rows], prob)
+            if add:
+                grad_key, grad_value = s.dkt[cols, :] + grad_key, s.dvt[cols, :] + grad_value
+            s.dkt[cols, :] = grad_key
+            s.dvt[cols, :] = grad_value
         grad_query = jnp.concatenate(parts, axis=1)
         for k in range(4):
-            @pl.when(t == k)
+            @pl.when(sl == k)
             def _():
                 s.sums[0, 6:7, 256 * k:256 * k + 256] += jnp.sum(grad_query, axis=0, keepdims=True)
         s.dq[rows, :] = grad_query.astype(BF16)
-    loop(2, attend_back)
+    gather_step(2, s.g1, 1)
+    attend_back(zl, False)
     grad_third("b1")
-    loop(1, lambda j: attend_back(j + 2))
+    gather_step(2, s.g1, 2)
+    gather_step(2, s.g1, 3)
+    attend_back(flip(zl), True)
     grad_second("i0")
     grad_first("i1")
-    loop(1, lambda j: attend_back(j + 3))
-
-    def turn_back(r):
-        rows = rows_of(r)
-        s.dk[rows, :] = s.dkt[:, rows].T.astype(BF16)
-        grad_value = s.dvt[:, rows].T
-        for k in range(4):
-            @pl.when(t == k)
-            def _():
-                s.sums[0, 7:8, 256 * k:256 * k + 256] += jnp.sum(grad_value, axis=0, keepdims=True)
-        s.dv[rows, :] = grad_value.astype(BF16)
-    loop(SLOTS, turn_back)
+    s.dk[...] = s.dkt[...].T.astype(BF16)
+    grad_value = s.dvt[...].T
     for k in range(4):
-        @pl.when(t == k)
+        @pl.when(sl == k)
+        def _():
+            s.sums[0, 7:8, 256 * k:256 * k + 256] += jnp.sum(grad_value, axis=0, keepdims=True)
+    s.dv[...] = grad_value.astype(BF16)
+    for k in range(4):
+        @pl.when(sl == k)
         def _():
             s.sums[0, 8 + k:9 + k, :] = s.gb_in[...]
 
@@ -1248,14 +1199,14 @@
 
     sums_start(0)
 
-    def tok_part(first, count, dst, add):
+    def tok_part(first, count, dst):
         rows = pl.ds(pl.multiple_of(first, HALF), count)
         for n in range(4):
             cols = slice(256 * n, 256 * n + 256)
             acc = dot_nn(s.dq[rows, :], s.w3t[0, :, cols])
             acc = acc + dot_nn(s.dk[rows, :], s.w3t[1, :, cols])
             acc = acc + dot_nn(s.dv[rows, :], s.w3t[2, :, cols])
-            put_part(dst, add, n, acc)
+            put_part(dst, n, acc)
     scatter(3, tok_part)
     sums_finish(0)
     sums_start(1)
@@ -1272,19 +1223,26 @@
     grad_second("i1")
     grad_first("o")
     grad_first("q")
+    gtok_s, gtok_r = take("s"), take("r")
+    at_end(s.gtok_own, gtok_s, home_self)
+
+    def last_rows(i):
+        ch = own_chunk(i)
+        s.gtok_own[ch, :] = (s.g1f[ch, :] + scatter_rows(3, ch)).astype(BF16)
+
+    def rows_home(chosen):
+        @pl.when(chosen)
+        def _():
+            by_halves(3, last_rows, lambda k: None)
+            send_or_keep(s.gtok_own, o.gtok, dev(b, zh, t), home_self, gtok_s, gtok_r)
+
+    rows_home(is_inner)
     grad_third("i1")
     grad_second("o")
     grad_first("k")
-
-    def last_rows(i):
-        ch = own_chunk(i)
-        s.gtok_own[ch, :] = (s.g1f[ch, :] + scatter_rows(3, ch)).astype(BF16)
-    by_halves(3, last_rows, lambda k: None)
-    gtok_s, gtok_r = take("s"), take("r")
-    send_or_keep(s.gtok_own, o.gtok, dev(b, zh, t), home_self, gtok_s, gtok_r)
-    at_end(s.gtok_own, gtok_s, home_self)
     grad_second("q")
     grad_first("v")
+    rows_home(jnp.logical_not(is_inner))
     sums_finish(1)
     sums_start(2)
     grad_third("o")

time: 151 us -> 148 us (0.980)
  Pallas kernels: 150 us -> 147 us
    pallas_call x1, Pallas kernels: 146 us -> 144 us  [on_device_fused(): pl.pallas_call(layer_kernel, out_shape=between, in_specs=in_specs, out_sp...]
where the time goes in v5:
time: 148 us
  Pallas kernels  147 us (99%)
    pallas_call x1, Pallas kernels, on_device_fused(): pl.pallas_call(layer_kernel, out_shape=between, in_specs=in_specs, out_sp...  144 us
    pallas_call x1, Pallas kernels, on_device_fused(): pl.pallas_call(result_kernel, out_shape=results, in_specs=[vmem] * len(be...  3.05 us

profile of v5, /device:TPU:1, one launch (start us, length us, event | category | flops | bytes accessed | tf_op | source)
XLA Modules:
  0.0 147.8 jit_solution(15014145995675966902)
XLA Ops:
  0.7 143.9 %layer.1 = (bf16[128,1024]{1,0:T(8,128)(2,1)}, bf16[128,1024]{1,0:T(8,128)(2,1)}, f32[16,1024]{1,0:T(8,128)}, bf16[2,128,256]{2,1,0:T(8,128)(2,1)}, bf16[2,128,2...) custom-call(bf16[128,1024]{1,0:T(8,128)(2,1)} %tok.1, ...), custom_call_target="tpu_custom_call" | custom-call | tf_op jit(solution)/shard_map/layer/pallas_call | solution.py:1311
  144.6 3.0 %results.1 = (bf16[128,1024]{1,0:T(8,128)(2,1)}, f32[128,1024]{1,0:T(8,128)}, f32[128,256]{1,0:T(8,128)}, f32[1,1024]{1,0:T(1,128)}, f32[128,256]{1,0:T(8,128)},...) custom-call(bf16[128,1024]{1,0:T(8,128)(2,1)} %get-tuple-element.45., ...), custom_call_target="tpu_custom_call" | custom-call | tf_op jit(solution)/shard_map/results/pallas_call | solution.py:1325

commit v6 on v5

--- a/solution.py
+++ b/solution.py
@@ -727,6 +727,8 @@
 
         @pl.when(j == 2)
         def _():
+            if which == 0:
+                over_plane_now((), inner_away, relays=("b0",))
             for k in range(2):
                 near = half_at(full, t2, k)
                 got(near, base + 1 + k)
@@ -735,7 +737,7 @@
         @pl.when(j == 3)
         def _():
             if which == 0:
-                over_plane_now((), inner_away, relays=("b0", "b1"))
+                over_plane_now((), inner_away, relays=("b1",))
             got(block_at(full, t3), base + 3)
 
     halves = [pl.ds(k * HALF, HALF) for k in range(2)]
@@ -950,10 +952,11 @@
         s.ctx[...] = context
         s.ctxt[...] = context.T
     over_plane_now((), away, relays=("o",))
-    over_plane_now(("i0", "i1"), inner_away)
+    over_plane_now(("i0",), inner_away)
     over_plane_now(("b1",), here, relays=("i1",))
     attend()
-    over_plane_now(("i0", "i1"), outer_away)
+    over_plane_now(("i0",), outer_away)
+    over_plane_now(("i1",), inner_away)
     arrived("o")
 
     def attn_part(first, count, dst):
@@ -992,16 +995,16 @@
         s.hid1[ch, :] = hidden
         s.hid[group_chunk(i), :] = hidden.astype(BF16)
     over_plane_now((), here, relays=("b0",))
-    over_plane_now((), inner_away, relays=("i0", "i1"))
-    over_plane_now(("b0", "b1"), outer_away, relays=("i0",))
-    over_plane_now((), outer_away, relays=("i1",))
+    over_plane_now((), inner_away, relays=("i0",))
+    over_plane_now(("i1", "b0", "b1"), outer_away, relays=("i0",))
     by_halves(0, norm_one, lambda k: gather_start(0, s.hid, k))
     over_plane_now((), here, relays=("b1",))
-    over_plane_now((), outer_away, relays=("b0", "b1"))
+    over_plane_now((), inner_away, relays=("i1",))
+    over_plane_now((), outer_away, relays=("i1", "b0", "b1"))
+    over_plane_now(("b0", "b1"), inner_away)
+    send_cotangent()
     arrived("i0")
     arrived("i1")
-
-    over_plane_now(("b0", "b1"), inner_away)
 
     def ffn_in(j):
         gather_step(0, s.hid, j)
@@ -1016,7 +1019,6 @@
             s.act[rows, cols] = (pre * cdf).astype(BF16)
             s.slope[rows, cols] = cdf + pre * pdf
     loop(SLOTS, ffn_in)
-    send_cotangent()
 
     def turn_ffn(r):
         rows = rows_of(r)
@@ -1281,18 +1283,50 @@
                     left(instead, sk)
 
 
-def result_kernel(out, gtok, sums, zq, zk, zv, zo, zi0, zi1, zb0, zb1, o_out, o_gtok, o_gq, o_gbq, o_gk, o_gv, o_gbv, o_go,
-                  o_gbo, o_gga, o_gsa, o_gi, o_gbi, o_gb, o_gbb, o_ggf, o_gsf):
-    both = lambda ref: ref[0].astype(F32) + ref[1].astype(F32)
-    o_out[...] = out[...]
-    o_gtok[...] = gtok[...].astype(F32)
-    o_gq[...], o_gk[...], o_gv[...], o_go[...] = both(zq), both(zk), both(zv), both(zo)
-    o_gi[:, :512], o_gi[:, 512:] = both(zi0), both(zi1)
-    o_gb[:512, :], o_gb[512:, :] = both(zb0), both(zb1)
-    for row, ref in ((6, o_gbq), (7, o_gbv), (0, o_gbo), (1, o_gga), (2, o_gsa), (3, o_gbb), (4, o_ggf), (5, o_gsf)):
-        ref[...] = sums[row:row + 1, :]
+def result_kernel(*refs):
+    out, gtok, sums, zq, zk, zv, zo, zi0, zi1, zb0, zb1 = refs[:11]
+    (o_out, o_gtok, o_gq, o_gbq, o_gk, o_gv, o_gbv, o_go, o_gbo, o_gga, o_gsa, o_gi, o_gbi, o_gb, o_gbb, o_ggf,
+     o_gsf) = refs[11:28]
+    held, wide, lines, wide_in, in_sem, out_sem = refs[28:39], refs[39:46], refs[46:55], refs[55], refs[56], refs[57]
+    arriving = [pltpu.make_async_copy(src, dst, in_sem.at[n]) for n, (src, dst) in enumerate(zip(refs[:11], held))]
+    for n in (0, 1, 9, 10, 7, 8, 6, 3, 4, 5, 2):
+        arriving[n].start()
+    leaving = []
+
+    def put(src, dst):
+        copy = pltpu.make_async_copy(src, dst, out_sem.at[len(leaving)])
+        copy.start()
+        leaving.append(copy)
+
+    arriving[0].wait()
+    put(held[0], o_out)
+    arriving[1].wait()
+    wide[0][...] = held[1][...].astype(F32)
+    put(wide[0], o_gtok)
+
+    def both(n, dst):
+        arriving[n].wait()
+        dst[...] = held[n][0].astype(F32) + held[n][1].astype(F32)
+
+    both(9, wide[1].at[0:512, :])
+    both(10, wide[1].at[512:1024, :])
+    put(wide[1], o_gb)
+    both(7, wide_in.at[:, 0:512])
+    both(8, wide_in.at[:, 512:1024])
+    put(wide_in, o_gi)
+    for n, buf, dst in ((6, wide[2], o_go), (3, wide[3], o_gq), (4, wide[4], o_gk), (5, wide[5], o_gv)):
+        both(n, buf)
+        put(buf, dst)
+    arriving[2].wait()
+    for row, buf, dst in ((6, 0, o_gbq), (7, 1, o_gbv), (0, 2, o_gbo), (1, 3, o_gga), (2, 4, o_gsa), (3, 5, o_gbb),
+                          (4, 6, o_ggf), (5, 7, o_gsf)):
+        lines[buf][...] = held[2][row:row + 1, :]
+        put(lines[buf], dst)
     for k in range(4):
-        o_gbi[:, WIDTH * k:WIDTH * k + WIDTH] = sums[8 + k:9 + k, :]
+        lines[8][:, WIDTH * k:WIDTH * k + WIDTH] = held[2][8 + k:9 + k, :]
+    put(lines[8], o_gbi)
+    for copy in leaving:
+        copy.wait()
 
 
 def on_device_fused(tokens, lengths, w_query, b_query, w_key, w_value, b_value, w_out, b_out, gain_attn, shift_attn,
@@ -1301,7 +1335,6 @@
     operands = (tokens, lengths, w_query, row(b_query), w_key, w_value, row(b_value), w_out, row(b_out),
                 row(gain_attn), row(shift_attn), w_in, row(b_in), w_back, row(b_back), row(gain_ffn),
                 row(shift_ffn), cotangent)
-    vmem = pl.BlockSpec(memory_space=pltpu.VMEM)
     stay = pl.BlockSpec(memory_space=pl.ANY)
     in_specs = [stay] * len(operands)
     in_specs[1] = pl.BlockSpec(memory_space=pltpu.SMEM)
@@ -1325,8 +1358,14 @@
     outs = pl.pallas_call(
         result_kernel,
         out_shape=results,
-        in_specs=[vmem] * len(between),
-        out_specs=[vmem] * len(results),
+        in_specs=[stay] * len(between),
+        out_specs=[stay] * len(results),
+        scratch_shapes=[pltpu.VMEM(part.shape, part.dtype) for part in between]
+        + [pltpu.VMEM(dims, F32) for dims in (tokens.shape, w_back.shape, w_out.shape, w_query.shape, w_key.shape,
+                                              w_value.shape, (8, 128))]
+        + [pltpu.VMEM((1, WIDTH), F32)] * 8
+        + [pltpu.VMEM((1, b_in.shape[0]), F32), pltpu.VMEM(w_in.shape, F32), pltpu.SemaphoreType.DMA((11,)),
+           pltpu.SemaphoreType.DMA((17,))],
         name="results",
     )(*parts)
     return tuple(v.reshape(-1) if v.shape[0] == 1 else v for v in outs)

time: 148 us -> 146 us (0.986)
  Pallas kernels: 147 us -> 145 us
    pallas_call x1, Pallas kernels: 144 us -> 142 us  [on_device_fused(): pl.pallas_call(layer_kernel, out_shape=between, in_specs=in_specs, out_sp...]
where the time goes in v6:
time: 146 us; the launch traced here: 145 us
  Pallas kernels  145 us (99%)
    pallas_call x1, Pallas kernels, on_device_fused(): pl.pallas_call(layer_kernel, out_shape=between, in_specs=in_specs, out_sp...  142 us

profile of v6, /device:TPU:1, one launch (start us, length us, event | category | flops | bytes accessed | tf_op | source)
XLA Modules:
  0.0 145.5 jit_solution(10170746153051906375)
XLA Ops:
  0.7 142.0 %layer.1 = (bf16[128,1024]{1,0:T(8,128)(2,1)}, bf16[128,1024]{1,0:T(8,128)(2,1)}, f32[16,1024]{1,0:T(8,128)}, bf16[2,128,256]{2,1,0:T(8,128)(2,1)}, bf16[2,128,2...) custom-call(bf16[128,1024]{1,0:T(8,128)(2,1)} %tok.1, ...), custom_call_target="tpu_custom_call" | custom-call | tf_op jit(solution)/shard_map/layer/pallas_call | solution.py:1344
  142.6 2.6 %results.1 = (bf16[128,1024]{1,0:T(8,128)(2,1)}, f32[128,1024]{1,0:T(8,128)}, f32[128,256]{1,0:T(8,128)}, f32[1,1024]{1,0:T(1,128)}, f32[128,256]{1,0:T(8,128)},...) custom-call(bf16[128,1024]{1,0:T(8,128)(2,1)} %get-tuple-element.45., ...), custom_call_target="tpu_custom_call" | custom-call | tf_op jit(solution)/shard_map/results/pallas_call | solution.py:1358

commit v7 on v6

--- a/solution.py
+++ b/solution.py
@@ -728,7 +728,7 @@
         @pl.when(j == 2)
         def _():
             if which == 0:
-                over_plane_now((), inner_away, relays=("b0",))
+                over_plane_now((), away, relays=("b0",))
             for k in range(2):
                 near = half_at(full, t2, k)
                 got(near, base + 1 + k)
@@ -737,7 +737,7 @@
         @pl.when(j == 3)
         def _():
             if which == 0:
-                over_plane_now((), inner_away, relays=("b1",))
+                over_plane_now((), away, relays=("b1",))
             got(block_at(full, t3), base + 3)
 
     halves = [pl.ds(k * HALF, HALF) for k in range(2)]
@@ -758,6 +758,39 @@
         send(out.at[which, 2], back.at[which, 2], partner, ss, rr + 4)
         part(t * BLOCK, BLOCK, s.rs_own.at[which])
 
+    def scatter_cols(which, blocks, k):
+        out, back = s.rs_out, s.rs_got
+        ss, rr = scatter_s + which, scatter_r + 5 * which
+        slots = [pl.ds(pl.multiple_of(block * 256, 256), 256) for block in blocks]
+        size = s.rs_got.at[which, 0, :, 0:256 * len(blocks)]
+
+        def product(row, block):
+            rows = pl.ds(pl.multiple_of(row * BLOCK, BLOCK), BLOCK)
+            return dot_nn(s.act[rows, :], s.wb[block])
+
+        def cast(row, slot):
+            for block, cols in zip(blocks, slots):
+                out[which, slot, :, cols] = product(row, block).astype(BF16)
+
+        cast(t3, 0)
+        for cols in slots:
+            send(out.at[which, 0, :, cols], back.at[which, 0, :, cols], partner, ss, rr + k)
+        cast(t1, 2)
+        for cols in slots:
+            send(out.at[which, 2, :, cols], back.at[which, 2, :, cols], partner, ss, rr + 4)
+        got(size, rr + k)
+        for block, cols in zip(blocks, slots):
+            total = product(t2, block).astype(BF16).astype(F32) + back[which, 0, :, cols].astype(F32)
+            out[which, 1, :, cols] = total.astype(BF16)
+            send(out.at[which, 1, :, cols], back.at[which, 1, :, cols], pair, ss, rr + 2)
+        for block, cols in zip(blocks, slots):
+            s.rs_own[which, :, cols] = product(t, block).astype(BF16)
+
+    def scatter_cols_wait(which):
+        rr = scatter_r + 5 * which
+        got(s.rs_got.at[which, 2], rr + 4)
+        got(s.rs_got.at[which, 1], rr + 2)
+
     def scatter_wait(which, k):
         rr = scatter_r + 5 * which
         if k == 0:
@@ -769,8 +802,11 @@
         return total + s.rs_got[which, 1, chunk, :].astype(F32)
 
     def by_halves(which, body, after):
+        if which == 1:
+            scatter_cols_wait(which)
         for k in range(2):
-            scatter_wait(which, k)
+            if which != 1:
+                scatter_wait(which, k)
             loop(2, lambda i: body(2 * k + i))
             after(k)
 
@@ -955,6 +991,10 @@
     over_plane_now(("i0",), inner_away)
     over_plane_now(("b1",), here, relays=("i1",))
     attend()
+    @pl.when(jnp.logical_not(is_inner))
+    def _():
+        to_across("b0")
+
     over_plane_now(("i0",), outer_away)
     over_plane_now(("i1",), inner_away)
     arrived("o")
@@ -966,7 +1006,6 @@
     scatter(0, attn_part)
     @pl.when(jnp.logical_not(is_inner))
     def _():
-        to_across("b0")
         to_across("b1")
 
     for m in range(3):
@@ -996,11 +1035,11 @@
         s.hid[group_chunk(i), :] = hidden.astype(BF16)
     over_plane_now((), here, relays=("b0",))
     over_plane_now((), inner_away, relays=("i0",))
-    over_plane_now(("i1", "b0", "b1"), outer_away, relays=("i0",))
+    over_plane_now(("i1", "b0"), outer_away, relays=("i0",))
     by_halves(0, norm_one, lambda k: gather_start(0, s.hid, k))
     over_plane_now((), here, relays=("b1",))
     over_plane_now((), inner_away, relays=("i1",))
-    over_plane_now((), outer_away, relays=("i1", "b0", "b1"))
+    over_plane_now(("b1",), outer_away, relays=("i1",))
     over_plane_now(("b0", "b1"), inner_away)
     send_cotangent()
     arrived("i0")
@@ -1024,14 +1063,10 @@
         rows = rows_of(r)
         s.actt[:, rows] = s.act[rows, :].T
         s.hidt[:, rows] = s.hid[rows, :].T
+    scatter_cols(1, (b, bx, by), 0)
     arrived("b0")
     arrived("b1")
-
-    def ffn_part(first, count, dst):
-        rows = pl.ds(pl.multiple_of(first, HALF), count)
-        for n in range(4):
-            put_part(dst, n, dot_nn(s.act[rows, :], s.wb[n]))
-    scatter(1, ffn_part)
+    scatter_cols(1, (bd,), 1)
     loop(SLOTS, turn_ffn)
 
     def turn_wi(r):

time: 146 us -> 144 us (0.986)
  Pallas kernels: 145 us -> 143 us
    pallas_call x1, Pallas kernels: 142 us -> 141 us  [on_device_fused(): pl.pallas_call(layer_kernel, out_shape=between, in_specs=in_specs, out_sp...]
where the time goes in v7:
time: 144 us
  Pallas kernels  143 us (99%)
    pallas_call x1, Pallas kernels, on_device_fused(): pl.pallas_call(layer_kernel, out_shape=between, in_specs=in_specs, out_sp...  141 us

profile of v7, /device:TPU:1, one launch (start us, length us, event | category | flops | bytes accessed | tf_op | source)
XLA Modules:
  0.0 144.0 jit_solution(16823216657752895521)
XLA Ops:
  0.7 140.5 %layer.1 = (bf16[128,1024]{1,0:T(8,128)(2,1)}, bf16[128,1024]{1,0:T(8,128)(2,1)}, f32[16,1024]{1,0:T(8,128)}, bf16[2,128,256]{2,1,0:T(8,128)(2,1)}, bf16[2,128,2...) custom-call(bf16[128,1024]{1,0:T(8,128)(2,1)} %tok.1, ...), custom_call_target="tpu_custom_call" | custom-call | tf_op jit(solution)/shard_map/layer/pallas_call | solution.py:1379
  141.2 2.6 %results.1 = (bf16[128,1024]{1,0:T(8,128)(2,1)}, f32[128,1024]{1,0:T(8,128)}, f32[128,256]{1,0:T(8,128)}, f32[1,1024]{1,0:T(1,128)}, f32[128,256]{1,0:T(8,128)},...) custom-call(bf16[128,1024]{1,0:T(8,128)(2,1)} %get-tuple-element.45., ...), custom_call_target="tpu_custom_call" | custom-call | tf_op jit(solution)/shard_map/results/pallas_call | solution.py:1393

commit v8 on v7

--- a/solution.py
+++ b/solution.py
@@ -1220,19 +1220,33 @@
         def _():
             s.sums[0, 8 + k:9 + k, :] = s.gb_in[...]
 
-    sums_s, sums_r = take("s", 5), take("r", 5)
+    sums_s, sums_r = take("s", 6), take("r", 6)
     sums_to = [partner, across, pair, x_near, y_near]
+    sum_rows = pl.ds(pl.multiple_of(c * 8, 8), 8)
+    other_rows = pl.ds(pl.multiple_of(flip(c) * 8, 8), 8)
+
+    def sums_part(ref, k):
+        return ref.at[k] if k == 0 else ref.at[k, sum_rows, :]
 
     def sums_start(k):
-        send(s.sums.at[k], s.sums_got.at[k], sums_to[k], sums_s + k, sums_r + k)
-        at_end(s.sums.at[k], sums_s + k)
+        mine = sums_part(s.sums, k)
+        send(mine, sums_part(s.sums_got, k), sums_to[k], sums_s + k, sums_r + k)
+        at_end(mine, sums_s + k)
 
     def sums_finish(k):
-        got(s.sums_got.at[k], sums_r + k)
-        total = s.sums[k] + s.sums_got[k]
-        s.sums[k + 1] = total
+        got(sums_part(s.sums_got, k), sums_r + k)
+        if k == 0:
+            s.sums[1] = s.sums[0] + s.sums_got[0]
+        else:
+            s.sums[k + 1, sum_rows, :] = s.sums[k, sum_rows, :] + s.sums_got[k, sum_rows, :]
         if k == 4:
-            pltpu.make_async_copy(s.sums.at[5], o.sums, vsem.at[0]).start()
+            done = s.sums.at[5, sum_rows, :]
+            send(done, done, partner, sums_s + 5, sums_r + 5)
+            at_end(done, sums_s + 5)
+
+    def sums_out():
+        got(s.sums.at[5, other_rows, :], sums_r + 5)
+        pltpu.make_async_copy(s.sums.at[5], o.sums, vsem.at[0]).start()
 
     sums_start(0)
 
@@ -1302,6 +1316,7 @@
     grad_final("q")
     sums_finish(4)
     grad_final("k")
+    sums_out()
     grad_final("v")
 
     pltpu.make_async_copy(s.sums.at[5], o.sums, vsem.at[0]).wait()

time: 144 us -> 144 us (level)
  no operation moved by 1% of the time
where the time goes in v8:
time: 144 us
  Pallas kernels  143 us (99%)
    pallas_call x1, Pallas kernels, on_device_fused(): pl.pallas_call(layer_kernel, out_shape=between, in_specs=in_specs, out_sp...  140 us

profile of v8, /device:TPU:1, one launch (start us, length us, event | category | flops | bytes accessed | tf_op | source)
XLA Modules:
  0.0 143.7 jit_solution(11717518689311989679)
XLA Ops:
  0.7 140.2 %layer.1 = (bf16[128,1024]{1,0:T(8,128)(2,1)}, bf16[128,1024]{1,0:T(8,128)(2,1)}, f32[16,1024]{1,0:T(8,128)}, bf16[2,128,256]{2,1,0:T(8,128)(2,1)}, bf16[2,128,2...) custom-call(bf16[128,1024]{1,0:T(8,128)(2,1)} %tok.1, ...), custom_call_target="tpu_custom_call" | custom-call | tf_op jit(solution)/shard_map/layer/pallas_call | solution.py:1394
  140.8 2.6 %results.1 = (bf16[128,1024]{1,0:T(8,128)(2,1)}, f32[128,1024]{1,0:T(8,128)}, f32[128,256]{1,0:T(8,128)}, f32[1,1024]{1,0:T(1,128)}, f32[128,256]{1,0:T(8,128)},...) custom-call(bf16[128,1024]{1,0:T(8,128)(2,1)} %get-tuple-element.45., ...), custom_call_target="tpu_custom_call" | custom-call | tf_op jit(solution)/shard_map/results/pallas_call | solution.py:1408

commit v9 on v8

--- a/solution.py
+++ b/solution.py
@@ -838,7 +838,7 @@
         at_end(s.stage[name].at[0:2], grad_s[name] + 1, here, s.stage[name].at[0])
 
     def chunks(name, body):
-        size = 64 if name in ("i0", "i1") else 128
+        size = min(HALVES[name][0], 256)
         count = HALVES[name][0] // size
         loop(count, lambda i: body(pl.ds(pl.multiple_of(i * size, size), size)))
 

time: 144 us -> 144 us (level)
  no operation moved by 1% of the time
where the time goes in v9:
time: 144 us
  Pallas kernels  143 us (99%)
    pallas_call x1, Pallas kernels, on_device_fused(): pl.pallas_call(layer_kernel, out_shape=between, in_specs=in_specs, out_sp...  140 us

profile of v9, /device:TPU:1, one launch (start us, length us, event | category | flops | bytes accessed | tf_op | source)
XLA Modules:
  0.0 143.6 jit_solution(13009923908482761497)
XLA Ops:
  0.7 140.1 %layer.1 = (bf16[128,1024]{1,0:T(8,128)(2,1)}, bf16[128,1024]{1,0:T(8,128)(2,1)}, f32[16,1024]{1,0:T(8,128)}, bf16[2,128,256]{2,1,0:T(8,128)(2,1)}, bf16[2,128,2...) custom-call(bf16[128,1024]{1,0:T(8,128)(2,1)} %tok.1, ...), custom_call_target="tpu_custom_call" | custom-call | tf_op jit(solution)/shard_map/layer/pallas_call | solution.py:1394
  140.8 2.6 %results.1 = (bf16[128,1024]{1,0:T(8,128)(2,1)}, f32[128,1024]{1,0:T(8,128)}, f32[128,256]{1,0:T(8,128)}, f32[1,1024]{1,0:T(1,128)}, f32[128,256]{1,0:T(8,128)},...) custom-call(bf16[128,1024]{1,0:T(8,128)(2,1)} %get-tuple-element.45., ...), custom_call_target="tpu_custom_call" | custom-call | tf_op jit(solution)/shard_map/results/pallas_call | solution.py:1408
